TPU v7x, 256 devices: a whole 4x4x8 slice. The times are simulated.
256 devices in a mesh: row: 16 (over z, core), col: 16 (over x, y).
Axes of the slice: x: 4, y: 4, z: 8, core: 2. Of those that a mesh axis runs over, the one named last changes fastest.
Arguments:
- right_side: float32 [1, 16, 4, 1024], P(None, 'row'), may hold values from -6 to 6
- inverse_t: bfloat16 [1, 16, 1024, 1024], P(None, 'row', 'col'), as said below
- u_factor: bfloat16 [1, 16, 1, 16, 128, 1024], P(None, 'row', None, 'col'), may hold values from -0.25 to 0.25
- v_factor: bfloat16 [1, 16, 1, 16, 128, 1024], P(None, 'row', None, 'col'), may hold values from -0.1875 to 0.1875
- ranks: int32 [1, 16, 1, 16], P(None, 'row', None, 'col'), may hold values from 4 to 128, as said below
Outputs:
- whitened: float32 [1, 16, 4, 1024], P(None, 'row')
- loglik: float32 [1, 16, 4], P(None, 'row')
Inputs may be any that keep to these rules, and one draw needn't show every extreme that they name: Tile (i, j) with j < i uses the first ranks of its factor rows. `inverse_t`: upper triangular with a positive diagonal.
All inputs are finite; a program needn't handle non-finite values.
Results may differ from a plain program's by a relative error of at most 0.0085.
Values sent between devices are 32-bit elements; how exact they have to be, the bound alone decides.
No kernel may reach another device: no remote copies, remote signals or barrier semaphores. Data moves between devices by JAX's collectives and lax.ppermute only.
A program may use at most 64 MiB of HBM per device.

v0:
```python
import functools
import math

import jax
import jax.numpy as jnp
from jax import lax
from jax.sharding import Mesh
from jax.sharding import PartitionSpec as P

ROW = ("row_0", "row_1")
COL = ("col_0", "col_1")


def cut_along(array, dim, devices):
    lengths = array.shape
    pieces = array.reshape(*lengths[:dim], devices, lengths[dim] // devices, *lengths[dim + 1 :])
    return jnp.moveaxis(pieces, dim, 0)


def summed_on_arrival(array, axis, dim):
    pieces = cut_along(array, dim, lax.axis_size(axis))
    arrived = lax.all_to_all(pieces, axis, split_axis=0, concat_axis=0, tiled=True)
    return arrived.sum(axis=0)


def from_everyone(array, axis):
    devices = lax.axis_size(axis)
    return lax.all_to_all(
        jnp.broadcast_to(array[None], (devices, *array.shape)), axis, 0, 0, tiled=True
    )


def taken_together(array, axis):
    return from_everyone(array, axis).sum(axis=0)


def over_axes(array, axes):
    far, near = axes
    return taken_together(taken_together(array, near), far)


def one_axis_at_a_time(array, axes):
    return functools.reduce(lax.psum, axes, array)


def rank_part(v_tiles, u_tiles, rounded, limit, offset):
    width = v_tiles.shape[1]
    inner = jnp.einsum("brn,bkn->brk", v_tiles, rounded, preferred_element_type=jnp.float32)
    keep = jnp.arange(width, dtype=jnp.int32)[None, :] + offset < limit[:, None]
    inner = jnp.where(keep[:, :, None], inner, 0.0).astype(jnp.bfloat16)
    return jnp.einsum("brk,brn->bkn", inner, u_tiles, preferred_element_type=jnp.float32)


def project(v_tiles, u_tiles, rounded, limit):
    half = v_tiles.shape[1] // 2
    lower = rank_part(v_tiles[:, :half], u_tiles[:, :half], rounded, limit, 0)
    empty = jnp.zeros(lower.shape, jnp.float32)
    upper = lax.cond(
        jnp.any(limit > half),
        lambda: rank_part(v_tiles[:, half:], u_tiles[:, half:], rounded, limit, half),
        lambda: empty,
    )
    return lower + upper


def local(right_side, inverse_t, u_factor, v_factor, ranks):
    n_row = lax.axis_size(ROW)
    n_col = lax.axis_size(COL)
    cycles = right_side.shape[0]
    nrhs = right_side.shape[2]
    width = right_side.shape[3]
    slab = cycles * n_row
    per_col = slab // n_col
    piece = width // n_col
    rank_max = u_factor.shape[4]
    my_row = lax.axis_index(ROW)
    my_col = lax.axis_index(COL)
    sources = right_side.reshape(cycles, nrhs, width)
    inverse = inverse_t.reshape(cycles, piece, width)
    u_tiles = u_factor.reshape(cycles, per_col, rank_max, width)
    v_tiles = v_factor.reshape(cycles, per_col, rank_max, width)
    limits = ranks.reshape(cycles, per_col)
    block_start = my_col * piece

    def finish(partial_value, cycle, index):
        summed = summed_on_arrival(partial_value, COL, 1)
        own_source = lax.dynamic_index_in_dim(sources, cycle, 0, False)
        local_source = lax.dynamic_slice_in_dim(own_source, block_start, piece, 1)
        reduced = (local_source - summed).astype(jnp.bfloat16)
        term = jnp.dot(
            reduced,
            lax.dynamic_index_in_dim(inverse, cycle, 0, False),
            preferred_element_type=jnp.float32,
        )
        owner = index % n_row == my_row
        term = jnp.where(owner, term, 0.0)
        return over_axes(term, ("row_0", ("row_1", "col_0", "col_1")))

    empty_rows = jnp.zeros((slab, nrhs, width), jnp.float32)

    def right_step(index, carry):
        solved, pending = carry
        cycle = index // n_row
        result = finish(lax.dynamic_index_in_dim(pending, cycle, 0, False), cycle, index)
        solved = lax.dynamic_update_index_in_dim(solved, result, index, 0)
        tile_col = index // n_col
        active = index % n_col == my_col
        later = jnp.arange(cycles, dtype=jnp.int32) * n_row + my_row > index
        column_limit = lax.dynamic_index_in_dim(limits, tile_col, 1, False)
        limit = jnp.where(later & active, column_limit, 0)
        v_column = lax.dynamic_index_in_dim(v_tiles, tile_col, 1, False)
        u_column = lax.dynamic_index_in_dim(u_tiles, tile_col, 1, False)
        rounded = result.astype(jnp.bfloat16)[None]
        pending = pending + project(v_column, u_column, rounded, limit)
        return (solved, pending)

    solved, pending = lax.fori_loop(
        0, slab, right_step, (empty_rows, jnp.zeros((cycles, nrhs, width), jnp.float32))
    )
    square_block = lax.dynamic_slice_in_dim(inverse, block_start, piece, 2)
    diagonal = jnp.diagonal(square_block, axis1=1, axis2=2).astype(jnp.float32)
    log_sums = jnp.sum(jnp.log(diagonal), axis=1)
    logdiag = one_axis_at_a_time(log_sums, COL) / width
    own_rows = lax.dynamic_index_in_dim(solved.reshape(cycles, n_row, nrhs, width), my_row, 1, True)
    quadratic = jnp.mean(own_rows * own_rows, axis=3)
    loglik = -0.5 * quadratic + logdiag[:, None, None] - 0.5 * math.log(2.0 * math.pi)
    return (own_rows, loglik)


def solution(mesh):
    torus = Mesh(mesh.devices.reshape(8, 2, 4, 4), ("row_0", "row_1", "col_0", "col_1"))
    return jax.shard_map(
        local,
        mesh=torus,
        in_specs=(
            P(None, ROW, None, None),
            P(None, ROW, COL, None),
            P(None, ROW, None, COL, None, None),
            P(None, ROW, None, COL, None, None),
            P(None, ROW, None, COL),
        ),
        out_specs=(P(None, ROW, None, None), P(None, ROW, None)),
        check_vma=False,
    )
```

profile of v0, /device:TPU:224, one launch (start us, length us, event | category | flops | bytes accessed | tf_op | source)
XLA Modules:
  0.0 708.8 jit_solution(5286780681341844830)
XLA Ops:
  1.4 684.9 %while.18 = (s32[]{:T(128)}, f32[16,4,1024]{2,1,0:T(4,128)S(1)}, f32[1,4,1024]{2,1,0:T(4,128)S(1)}, s32[]{:T(128)}, f32[1,4,64]{2,1,0:T(4,128)S(1)}, /*index=5*/...) while((s32[]{:T(128)}, f32[16,4,1024]{2,1,0:T(4,128)S(1)}, ...), condition=%wide.region_6.7_spmd.clone, body=%wide.region_0.6_spmd.clone.sunk | while | flops 2807248 | bytes 6509195 | solution.py:117
  2.2 7.0 all-to-all-start
  9.3 7.6 %all-to-all-done = f32[16,1,256]{2,1,0:T(1,128)S(1)} async-done(((f32[16,1,256]{2,1,0:T(1,128)}), f32[16,1,256]{2,1,0:T(1,128)S(1)}, u32[]{:S(2)}, u32[]{:S(2)}) %all-to-all-start) | async-done | bytes 16416 | tf_op jit(solution)/shard_map/while/body/eval_jaxpr/all_to_all | solution.py:22
  18.5 15.3 %all_to_all.42 = f32[32,4,1024]{2,1,0:T(4,128)S(1)} all-to-all(f32[32,4,1024]{2,1,0:T(4,128)S(1)} %broadcast_in_dim.150), channel_id=1, replica_groups=mesh['row_0'=8,'row_1'=2,'col_0'=4,'col_1'=4] {'row_1','col_0','col_1'}, dimensions={0} | all-to-all | bytes 1048576 | tf_op jit(solution)/shard_map/while/body/eval_jaxpr/all_to_all | solution.py:28
  34.5 6.0 all-to-all-start.2
  41.1 5.6 all-to-all-done.2
  51.5 7.5 %all-to-all-done = f32[16,1,256]{2,1,0:T(1,128)S(1)} async-done(((f32[16,1,256]{2,1,0:T(1,128)}), f32[16,1,256]{2,1,0:T(1,128)S(1)}, u32[]{:S(2)}, u32[]{:S(2)}) %all-to-all-start) | async-done | bytes 16416 | tf_op jit(solution)/shard_map/while/body/eval_jaxpr/all_to_all | solution.py:22
  60.6 15.3 %all_to_all.42 = f32[32,4,1024]{2,1,0:T(4,128)S(1)} all-to-all(f32[32,4,1024]{2,1,0:T(4,128)S(1)} %broadcast_in_dim.150), channel_id=1, replica_groups=mesh['row_0'=8,'row_1'=2,'col_0'=4,'col_1'=4] {'row_1','col_0','col_1'}, dimensions={0} | all-to-all | bytes 1048576 | tf_op jit(solution)/shard_map/while/body/eval_jaxpr/all_to_all | solution.py:28
  76.7 6.3 all-to-all-start.2
  83.6 5.5 all-to-all-done.2
  93.8 7.5 %all-to-all-done = f32[16,1,256]{2,1,0:T(1,128)S(1)} async-done(((f32[16,1,256]{2,1,0:T(1,128)}), f32[16,1,256]{2,1,0:T(1,128)S(1)}, u32[]{:S(2)}, u32[]{:S(2)}) %all-to-all-start) | async-done | bytes 16416 | tf_op jit(solution)/shard_map/while/body/eval_jaxpr/all_to_all | solution.py:22
  103.0 15.3 %all_to_all.42 = f32[32,4,1024]{2,1,0:T(4,128)S(1)} all-to-all(f32[32,4,1024]{2,1,0:T(4,128)S(1)} %broadcast_in_dim.150), channel_id=1, replica_groups=mesh['row_0'=8,'row_1'=2,'col_0'=4,'col_1'=4] {'row_1','col_0','col_1'}, dimensions={0} | all-to-all | bytes 1048576 | tf_op jit(solution)/shard_map/while/body/eval_jaxpr/all_to_all | solution.py:28
  119.0 6.5 all-to-all-start.2
  126.2 5.5 all-to-all-done.2
  136.5 7.5 %all-to-all-done = f32[16,1,256]{2,1,0:T(1,128)S(1)} async-done(((f32[16,1,256]{2,1,0:T(1,128)}), f32[16,1,256]{2,1,0:T(1,128)S(1)}, u32[]{:S(2)}, u32[]{:S(2)}) %all-to-all-start) | async-done | bytes 16416 | tf_op jit(solution)/shard_map/while/body/eval_jaxpr/all_to_all | solution.py:22
  145.6 15.3 %all_to_all.42 = f32[32,4,1024]{2,1,0:T(4,128)S(1)} all-to-all(f32[32,4,1024]{2,1,0:T(4,128)S(1)} %broadcast_in_dim.150), channel_id=1, replica_groups=mesh['row_0'=8,'row_1'=2,'col_0'=4,'col_1'=4] {'row_1','col_0','col_1'}, dimensions={0} | all-to-all | bytes 1048576 | tf_op jit(solution)/shard_map/while/body/eval_jaxpr/all_to_all | solution.py:28
  161.7 6.5 all-to-all-start.2
  168.9 5.5 all-to-all-done.2
  179.1 7.5 %all-to-all-done = f32[16,1,256]{2,1,0:T(1,128)S(1)} async-done(((f32[16,1,256]{2,1,0:T(1,128)}), f32[16,1,256]{2,1,0:T(1,128)S(1)}, u32[]{:S(2)}, u32[]{:S(2)}) %all-to-all-start) | async-done | bytes 16416 | tf_op jit(solution)/shard_map/while/body/eval_jaxpr/all_to_all | solution.py:22
  188.2 15.3 %all_to_all.42 = f32[32,4,1024]{2,1,0:T(4,128)S(1)} all-to-all(f32[32,4,1024]{2,1,0:T(4,128)S(1)} %broadcast_in_dim.150), channel_id=1, replica_groups=mesh['row_0'=8,'row_1'=2,'col_0'=4,'col_1'=4] {'row_1','col_0','col_1'}, dimensions={0} | all-to-all | bytes 1048576 | tf_op jit(solution)/shard_map/while/body/eval_jaxpr/all_to_all | solution.py:28
  204.3 6.5 all-to-all-start.2
  211.5 5.5 all-to-all-done.2
  221.7 7.5 %all-to-all-done = f32[16,1,256]{2,1,0:T(1,128)S(1)} async-done(((f32[16,1,256]{2,1,0:T(1,128)}), f32[16,1,256]{2,1,0:T(1,128)S(1)}, u32[]{:S(2)}, u32[]{:S(2)}) %all-to-all-start) | async-done | bytes 16416 | tf_op jit(solution)/shard_map/while/body/eval_jaxpr/all_to_all | solution.py:22
  230.8 15.3 %all_to_all.42 = f32[32,4,1024]{2,1,0:T(4,128)S(1)} all-to-all(f32[32,4,1024]{2,1,0:T(4,128)S(1)} %broadcast_in_dim.150), channel_id=1, replica_groups=mesh['row_0'=8,'row_1'=2,'col_0'=4,'col_1'=4] {'row_1','col_0','col_1'}, dimensions={0} | all-to-all | bytes 1048576 | tf_op jit(solution)/shard_map/while/body/eval_jaxpr/all_to_all | solution.py:28
  246.9 6.5 all-to-all-start.2
  254.1 5.5 all-to-all-done.2
  264.4 7.5 %all-to-all-done = f32[16,1,256]{2,1,0:T(1,128)S(1)} async-done(((f32[16,1,256]{2,1,0:T(1,128)}), f32[16,1,256]{2,1,0:T(1,128)S(1)}, u32[]{:S(2)}, u32[]{:S(2)}) %all-to-all-start) | async-done | bytes 16416 | tf_op jit(solution)/shard_map/while/body/eval_jaxpr/all_to_all | solution.py:22
  273.5 15.3 %all_to_all.42 = f32[32,4,1024]{2,1,0:T(4,128)S(1)} all-to-all(f32[32,4,1024]{2,1,0:T(4,128)S(1)} %broadcast_in_dim.150), channel_id=1, replica_groups=mesh['row_0'=8,'row_1'=2,'col_0'=4,'col_1'=4] {'row_1','col_0','col_1'}, dimensions={0} | all-to-all | bytes 1048576 | tf_op jit(solution)/shard_map/while/body/eval_jaxpr/all_to_all | solution.py:28
  289.5 6.5 all-to-all-start.2
  296.8 5.5 all-to-all-done.2
  307.0 7.5 %all-to-all-done = f32[16,1,256]{2,1,0:T(1,128)S(1)} async-done(((f32[16,1,256]{2,1,0:T(1,128)}), f32[16,1,256]{2,1,0:T(1,128)S(1)}, u32[]{:S(2)}, u32[]{:S(2)}) %all-to-all-start) | async-done | bytes 16416 | tf_op jit(solution)/shard_map/while/body/eval_jaxpr/all_to_all | solution.py:22
  316.1 15.3 %all_to_all.42 = f32[32,4,1024]{2,1,0:T(4,128)S(1)} all-to-all(f32[32,4,1024]{2,1,0:T(4,128)S(1)} %broadcast_in_dim.150), channel_id=1, replica_groups=mesh['row_0'=8,'row_1'=2,'col_0'=4,'col_1'=4] {'row_1','col_0','col_1'}, dimensions={0} | all-to-all | bytes 1048576 | tf_op jit(solution)/shard_map/while/body/eval_jaxpr/all_to_all | solution.py:28
  332.2 6.5 all-to-all-start.2
  339.4 5.5 all-to-all-done.2
  349.6 7.5 %all-to-all-done = f32[16,1,256]{2,1,0:T(1,128)S(1)} async-done(((f32[16,1,256]{2,1,0:T(1,128)}), f32[16,1,256]{2,1,0:T(1,128)S(1)}, u32[]{:S(2)}, u32[]{:S(2)}) %all-to-all-start) | async-done | bytes 16416 | tf_op jit(solution)/shard_map/while/body/eval_jaxpr/all_to_all | solution.py:22
  358.7 15.3 %all_to_all.42 = f32[32,4,1024]{2,1,0:T(4,128)S(1)} all-to-all(f32[32,4,1024]{2,1,0:T(4,128)S(1)} %broadcast_in_dim.150), channel_id=1, replica_groups=mesh['row_0'=8,'row_1'=2,'col_0'=4,'col_1'=4] {'row_1','col_0','col_1'}, dimensions={0} | all-to-all | bytes 1048576 | tf_op jit(solution)/shard_map/while/body/eval_jaxpr/all_to_all | solution.py:28
  374.8 6.5 all-to-all-start.2
  382.0 5.5 all-to-all-done.2
  392.2 7.5 %all-to-all-done = f32[16,1,256]{2,1,0:T(1,128)S(1)} async-done(((f32[16,1,256]{2,1,0:T(1,128)}), f32[16,1,256]{2,1,0:T(1,128)S(1)}, u32[]{:S(2)}, u32[]{:S(2)}) %all-to-all-start) | async-done | bytes 16416 | tf_op jit(solution)/shard_map/while/body/eval_jaxpr/all_to_all | solution.py:22
  401.3 15.3 %all_to_all.42 = f32[32,4,1024]{2,1,0:T(4,128)S(1)} all-to-all(f32[32,4,1024]{2,1,0:T(4,128)S(1)} %broadcast_in_dim.150), channel_id=1, replica_groups=mesh['row_0'=8,'row_1'=2,'col_0'=4,'col_1'=4] {'row_1','col_0','col_1'}, dimensions={0} | all-to-all | bytes 1048576 | tf_op jit(solution)/shard_map/while/body/eval_jaxpr/all_to_all | solution.py:28
  417.4 6.5 all-to-all-start.2
  424.6 5.5 all-to-all-done.2
  434.9 7.5 %all-to-all-done = f32[16,1,256]{2,1,0:T(1,128)S(1)} async-done(((f32[16,1,256]{2,1,0:T(1,128)}), f32[16,1,256]{2,1,0:T(1,128)S(1)}, u32[]{:S(2)}, u32[]{:S(2)}) %all-to-all-start) | async-done | bytes 16416 | tf_op jit(solution)/shard_map/while/body/eval_jaxpr/all_to_all | solution.py:22
  444.0 15.3 %all_to_all.42 = f32[32,4,1024]{2,1,0:T(4,128)S(1)} all-to-all(f32[32,4,1024]{2,1,0:T(4,128)S(1)} %broadcast_in_dim.150), channel_id=1, replica_groups=mesh['row_0'=8,'row_1'=2,'col_0'=4,'col_1'=4] {'row_1','col_0','col_1'}, dimensions={0} | all-to-all | bytes 1048576 | tf_op jit(solution)/shard_map/while/body/eval_jaxpr/all_to_all | solution.py:28
  460.0 6.5 all-to-all-start.2
  467.3 5.5 all-to-all-done.2
  477.5 7.5 %all-to-all-done = f32[16,1,256]{2,1,0:T(1,128)S(1)} async-done(((f32[16,1,256]{2,1,0:T(1,128)}), f32[16,1,256]{2,1,0:T(1,128)S(1)}, u32[]{:S(2)}, u32[]{:S(2)}) %all-to-all-start) | async-done | bytes 16416 | tf_op jit(solution)/shard_map/while/body/eval_jaxpr/all_to_all | solution.py:22
  486.6 15.3 %all_to_all.42 = f32[32,4,1024]{2,1,0:T(4,128)S(1)} all-to-all(f32[32,4,1024]{2,1,0:T(4,128)S(1)} %broadcast_in_dim.150), channel_id=1, replica_groups=mesh['row_0'=8,'row_1'=2,'col_0'=4,'col_1'=4] {'row_1','col_0','col_1'}, dimensions={0} | all-to-all | bytes 1048576 | tf_op jit(solution)/shard_map/while/body/eval_jaxpr/all_to_all | solution.py:28
  502.7 6.5 all-to-all-start.2
  509.9 5.5 all-to-all-done.2
  520.1 7.5 %all-to-all-done = f32[16,1,256]{2,1,0:T(1,128)S(1)} async-done(((f32[16,1,256]{2,1,0:T(1,128)}), f32[16,1,256]{2,1,0:T(1,128)S(1)}, u32[]{:S(2)}, u32[]{:S(2)}) %all-to-all-start) | async-done | bytes 16416 | tf_op jit(solution)/shard_map/while/body/eval_jaxpr/all_to_all | solution.py:22
  529.2 15.3 %all_to_all.42 = f32[32,4,1024]{2,1,0:T(4,128)S(1)} all-to-all(f32[32,4,1024]{2,1,0:T(4,128)S(1)} %broadcast_in_dim.150), channel_id=1, replica_groups=mesh['row_0'=8,'row_1'=2,'col_0'=4,'col_1'=4] {'row_1','col_0','col_1'}, dimensions={0} | all-to-all | bytes 1048576 | tf_op jit(solution)/shard_map/while/body/eval_jaxpr/all_to_all | solution.py:28
  545.3 6.5 all-to-all-start.2
  562.7 7.5 %all-to-all-done = f32[16,1,256]{2,1,0:T(1,128)S(1)} async-done(((f32[16,1,256]{2,1,0:T(1,128)}), f32[16,1,256]{2,1,0:T(1,128)S(1)}, u32[]{:S(2)}, u32[]{:S(2)}) %all-to-all-start) | async-done | bytes 16416 | tf_op jit(solution)/shard_map/while/body/eval_jaxpr/all_to_all | solution.py:22
  571.9 15.3 %all_to_all.42 = f32[32,4,1024]{2,1,0:T(4,128)S(1)} all-to-all(f32[32,4,1024]{2,1,0:T(4,128)S(1)} %broadcast_in_dim.150), channel_id=1, replica_groups=mesh['row_0'=8,'row_1'=2,'col_0'=4,'col_1'=4] {'row_1','col_0','col_1'}, dimensions={0} | all-to-all | bytes 1048576 | tf_op jit(solution)/shard_map/while/body/eval_jaxpr/all_to_all | solution.py:28
  587.9 6.5 all-to-all-start.2
  605.4 7.5 %all-to-all-done = f32[16,1,256]{2,1,0:T(1,128)S(1)} async-done(((f32[16,1,256]{2,1,0:T(1,128)}), f32[16,1,256]{2,1,0:T(1,128)S(1)}, u32[]{:S(2)}, u32[]{:S(2)}) %all-to-all-start) | async-done | bytes 16416 | tf_op jit(solution)/shard_map/while/body/eval_jaxpr/all_to_all | solution.py:22
  614.5 15.3 %all_to_all.42 = f32[32,4,1024]{2,1,0:T(4,128)S(1)} all-to-all(f32[32,4,1024]{2,1,0:T(4,128)S(1)} %broadcast_in_dim.150), channel_id=1, replica_groups=mesh['row_0'=8,'row_1'=2,'col_0'=4,'col_1'=4] {'row_1','col_0','col_1'}, dimensions={0} | all-to-all | bytes 1048576 | tf_op jit(solution)/shard_map/while/body/eval_jaxpr/all_to_all | solution.py:28
  630.6 6.5 all-to-all-start.2
  648.0 7.5 %all-to-all-done = f32[16,1,256]{2,1,0:T(1,128)S(1)} async-done(((f32[16,1,256]{2,1,0:T(1,128)}), f32[16,1,256]{2,1,0:T(1,128)S(1)}, u32[]{:S(2)}, u32[]{:S(2)}) %all-to-all-start) | async-done | bytes 16416 | tf_op jit(solution)/shard_map/while/body/eval_jaxpr/all_to_all | solution.py:22
  657.1 15.3 %all_to_all.42 = f32[32,4,1024]{2,1,0:T(4,128)S(1)} all-to-all(f32[32,4,1024]{2,1,0:T(4,128)S(1)} %broadcast_in_dim.150), channel_id=1, replica_groups=mesh['row_0'=8,'row_1'=2,'col_0'=4,'col_1'=4] {'row_1','col_0','col_1'}, dimensions={0} | all-to-all | bytes 1048576 | tf_op jit(solution)/shard_map/while/body/eval_jaxpr/all_to_all | solution.py:28
  673.2 6.5 all-to-all-start.2
  689.3 8.9 %psum.14 = f32[1]{0:T(128)} all-reduce(f32[1]{0:T(128)} %bitcast.13), channel_id=1, replica_groups=mesh['row_0'=8,'row_1'=2,'col_0'=4,'col_1'=4] {'col_0'}, use_global_device_ids=true, to_apply=%region_9.10 | all-reduce | flops 1 | bytes 8 | tf_op jit(solution)/shard_map/psum | solution.py:43
  698.2 9.5 %psum.15 = f32[1]{0:T(128)} all-reduce(f32[1]{0:T(128)} %psum.14), channel_id=1, replica_groups=mesh['row_0'=8,'row_1'=2,'col_0'=4,'col_1'=4] {'col_1'}, use_global_device_ids=true, to_apply=%region_10.11 | all-reduce | flops 1 | bytes 8 | tf_op jit(solution)/shard_map/psum | solution.py:43
  (414 shorter events, 134.6 us)
Async XLA Ops:
  1.5 16.7 %copy-start.3 = (bf16[1,64,1024]{2,1,0:T(8,128)(2,1)S(1)}, bf16[1,64,1024]{2,1,0:T(8,128)(2,1)}, u32[]{:S(2)}) copy-start(bf16[1,64,1024]{2,1,0:T(8,128)(2,1)} %get-tuple-element.450) | copy-start | bytes 393220 | tf_op jit(solution)/shard_map/while
  2.2 14.6 %all-to-all-start = ((f32[16,1,256]{2,1,0:T(1,128)}), f32[16,1,256]{2,1,0:T(1,128)S(1)}, u32[]{:S(2)}, u32[]{:S(2)}) async-start(f32[16,1,256]{2,1,0:T(1,128)} %reshape.227), calls=%async_computation | async-start | bytes 32768 | tf_op jit(solution)/shard_map/while/body/eval_jaxpr/all_to_all | solution.py:22
  33.8 12.9 %copy-start.2 = (bf16[1,1,128,1024]{3,2,1,0:T(8,128)(2,1)S(1)}, bf16[1,1,128,1024]{3,2,1,0:T(8,128)(2,1)}, u32[]{:S(2)}) copy-start(bf16[1,1,128,1024]{3,2,1,0:T(8,128)(2,1)} %get-tuple-element.454) | copy-start | bytes 786436 | tf_op jit(solution)/shard_map/while
  34.5 12.2 %all-to-all-start.2 = ((f32[8,4,1024]{2,1,0:T(4,128)}), f32[8,4,1024]{2,1,0:T(4,128)S(1)}, u32[]{:S(2)}, u32[]{:S(2)}) async-start(f32[8,4,1024]{2,1,0:T(4,128)} %broadcast_in_dim.151), calls=%async_computation.2 | async-start | bytes 262144 | tf_op jit(solution)/shard_map/while/body/eval_jaxpr/all_to_all | solution.py:28
  47.2 13.1 %copy-start.3 = (bf16[1,64,1024]{2,1,0:T(8,128)(2,1)S(1)}, bf16[1,64,1024]{2,1,0:T(8,128)(2,1)}, u32[]{:S(2)}) copy-start(bf16[1,64,1024]{2,1,0:T(8,128)(2,1)} %get-tuple-element.450) | copy-start | bytes 393220 | tf_op jit(solution)/shard_map/while
  48.0 11.0 %all-to-all-start = ((f32[16,1,256]{2,1,0:T(1,128)}), f32[16,1,256]{2,1,0:T(1,128)S(1)}, u32[]{:S(2)}, u32[]{:S(2)}) async-start(f32[16,1,256]{2,1,0:T(1,128)} %reshape.227), calls=%async_computation | async-start | bytes 32768 | tf_op jit(solution)/shard_map/while/body/eval_jaxpr/all_to_all | solution.py:22
  76.0 13.1 %copy-start.2 = (bf16[1,1,128,1024]{3,2,1,0:T(8,128)(2,1)S(1)}, bf16[1,1,128,1024]{3,2,1,0:T(8,128)(2,1)}, u32[]{:S(2)}) copy-start(bf16[1,1,128,1024]{3,2,1,0:T(8,128)(2,1)} %get-tuple-element.454) | copy-start | bytes 786436 | tf_op jit(solution)/shard_map/while
  76.7 12.4 %all-to-all-start.2 = ((f32[8,4,1024]{2,1,0:T(4,128)}), f32[8,4,1024]{2,1,0:T(4,128)S(1)}, u32[]{:S(2)}, u32[]{:S(2)}) async-start(f32[8,4,1024]{2,1,0:T(4,128)} %broadcast_in_dim.151), calls=%async_computation.2 | async-start | bytes 262144 | tf_op jit(solution)/shard_map/while/body/eval_jaxpr/all_to_all | solution.py:28
  89.6 13.1 %copy-start.3 = (bf16[1,64,1024]{2,1,0:T(8,128)(2,1)S(1)}, bf16[1,64,1024]{2,1,0:T(8,128)(2,1)}, u32[]{:S(2)}) copy-start(bf16[1,64,1024]{2,1,0:T(8,128)(2,1)} %get-tuple-element.450) | copy-start | bytes 393220 | tf_op jit(solution)/shard_map/while
  90.3 11.0 %all-to-all-start = ((f32[16,1,256]{2,1,0:T(1,128)}), f32[16,1,256]{2,1,0:T(1,128)S(1)}, u32[]{:S(2)}, u32[]{:S(2)}) async-start(f32[16,1,256]{2,1,0:T(1,128)} %reshape.227), calls=%async_computation | async-start | bytes 32768 | tf_op jit(solution)/shard_map/while/body/eval_jaxpr/all_to_all | solution.py:22
  118.4 13.4 %copy-start.2 = (bf16[1,1,128,1024]{3,2,1,0:T(8,128)(2,1)S(1)}, bf16[1,1,128,1024]{3,2,1,0:T(8,128)(2,1)}, u32[]{:S(2)}) copy-start(bf16[1,1,128,1024]{3,2,1,0:T(8,128)(2,1)} %get-tuple-element.454) | copy-start | bytes 786436 | tf_op jit(solution)/shard_map/while
  119.0 12.7 %all-to-all-start.2 = ((f32[8,4,1024]{2,1,0:T(4,128)}), f32[8,4,1024]{2,1,0:T(4,128)S(1)}, u32[]{:S(2)}, u32[]{:S(2)}) async-start(f32[8,4,1024]{2,1,0:T(4,128)} %broadcast_in_dim.151), calls=%async_computation.2 | async-start | bytes 262144 | tf_op jit(solution)/shard_map/while/body/eval_jaxpr/all_to_all | solution.py:28
  132.2 13.1 %copy-start.3 = (bf16[1,64,1024]{2,1,0:T(8,128)(2,1)S(1)}, bf16[1,64,1024]{2,1,0:T(8,128)(2,1)}, u32[]{:S(2)}) copy-start(bf16[1,64,1024]{2,1,0:T(8,128)(2,1)} %get-tuple-element.450) | copy-start | bytes 393220 | tf_op jit(solution)/shard_map/while
  133.0 11.0 %all-to-all-start = ((f32[16,1,256]{2,1,0:T(1,128)}), f32[16,1,256]{2,1,0:T(1,128)S(1)}, u32[]{:S(2)}, u32[]{:S(2)}) async-start(f32[16,1,256]{2,1,0:T(1,128)} %reshape.227), calls=%async_computation | async-start | bytes 32768 | tf_op jit(solution)/shard_map/while/body/eval_jaxpr/all_to_all | solution.py:22
  161.0 13.4 %copy-start.2 = (bf16[1,1,128,1024]{3,2,1,0:T(8,128)(2,1)S(1)}, bf16[1,1,128,1024]{3,2,1,0:T(8,128)(2,1)}, u32[]{:S(2)}) copy-start(bf16[1,1,128,1024]{3,2,1,0:T(8,128)(2,1)} %get-tuple-element.454) | copy-start | bytes 786436 | tf_op jit(solution)/shard_map/while
  161.7 12.7 %all-to-all-start.2 = ((f32[8,4,1024]{2,1,0:T(4,128)}), f32[8,4,1024]{2,1,0:T(4,128)S(1)}, u32[]{:S(2)}, u32[]{:S(2)}) async-start(f32[8,4,1024]{2,1,0:T(4,128)} %broadcast_in_dim.151), calls=%async_computation.2 | async-start | bytes 262144 | tf_op jit(solution)/shard_map/while/body/eval_jaxpr/all_to_all | solution.py:28
  174.9 13.1 %copy-start.3 = (bf16[1,64,1024]{2,1,0:T(8,128)(2,1)S(1)}, bf16[1,64,1024]{2,1,0:T(8,128)(2,1)}, u32[]{:S(2)}) copy-start(bf16[1,64,1024]{2,1,0:T(8,128)(2,1)} %get-tuple-element.450) | copy-start | bytes 393220 | tf_op jit(solution)/shard_map/while
  175.6 11.0 %all-to-all-start = ((f32[16,1,256]{2,1,0:T(1,128)}), f32[16,1,256]{2,1,0:T(1,128)S(1)}, u32[]{:S(2)}, u32[]{:S(2)}) async-start(f32[16,1,256]{2,1,0:T(1,128)} %reshape.227), calls=%async_computation | async-start | bytes 32768 | tf_op jit(solution)/shard_map/while/body/eval_jaxpr/all_to_all | solution.py:22
  203.6 13.4 %copy-start.2 = (bf16[1,1,128,1024]{3,2,1,0:T(8,128)(2,1)S(1)}, bf16[1,1,128,1024]{3,2,1,0:T(8,128)(2,1)}, u32[]{:S(2)}) copy-start(bf16[1,1,128,1024]{3,2,1,0:T(8,128)(2,1)} %get-tuple-element.454) | copy-start | bytes 786436 | tf_op jit(solution)/shard_map/while
  204.3 12.7 %all-to-all-start.2 = ((f32[8,4,1024]{2,1,0:T(4,128)}), f32[8,4,1024]{2,1,0:T(4,128)S(1)}, u32[]{:S(2)}, u32[]{:S(2)}) async-start(f32[8,4,1024]{2,1,0:T(4,128)} %broadcast_in_dim.151), calls=%async_computation.2 | async-start | bytes 262144 | tf_op jit(solution)/shard_map/while/body/eval_jaxpr/all_to_all | solution.py:28
  217.5 13.1 %copy-start.3 = (bf16[1,64,1024]{2,1,0:T(8,128)(2,1)S(1)}, bf16[1,64,1024]{2,1,0:T(8,128)(2,1)}, u32[]{:S(2)}) copy-start(bf16[1,64,1024]{2,1,0:T(8,128)(2,1)} %get-tuple-element.450) | copy-start | bytes 393220 | tf_op jit(solution)/shard_map/while
  218.2 11.0 %all-to-all-start = ((f32[16,1,256]{2,1,0:T(1,128)}), f32[16,1,256]{2,1,0:T(1,128)S(1)}, u32[]{:S(2)}, u32[]{:S(2)}) async-start(f32[16,1,256]{2,1,0:T(1,128)} %reshape.227), calls=%async_computation | async-start | bytes 32768 | tf_op jit(solution)/shard_map/while/body/eval_jaxpr/all_to_all | solution.py:22
  246.2 13.4 %copy-start.2 = (bf16[1,1,128,1024]{3,2,1,0:T(8,128)(2,1)S(1)}, bf16[1,1,128,1024]{3,2,1,0:T(8,128)(2,1)}, u32[]{:S(2)}) copy-start(bf16[1,1,128,1024]{3,2,1,0:T(8,128)(2,1)} %get-tuple-element.454) | copy-start | bytes 786436 | tf_op jit(solution)/shard_map/while
  246.9 12.7 %all-to-all-start.2 = ((f32[8,4,1024]{2,1,0:T(4,128)}), f32[8,4,1024]{2,1,0:T(4,128)S(1)}, u32[]{:S(2)}, u32[]{:S(2)}) async-start(f32[8,4,1024]{2,1,0:T(4,128)} %broadcast_in_dim.151), calls=%async_computation.2 | async-start | bytes 262144 | tf_op jit(solution)/shard_map/while/body/eval_jaxpr/all_to_all | solution.py:28
  260.1 13.1 %copy-start.3 = (bf16[1,64,1024]{2,1,0:T(8,128)(2,1)S(1)}, bf16[1,64,1024]{2,1,0:T(8,128)(2,1)}, u32[]{:S(2)}) copy-start(bf16[1,64,1024]{2,1,0:T(8,128)(2,1)} %get-tuple-element.450) | copy-start | bytes 393220 | tf_op jit(solution)/shard_map/while
  260.8 11.0 %all-to-all-start = ((f32[16,1,256]{2,1,0:T(1,128)}), f32[16,1,256]{2,1,0:T(1,128)S(1)}, u32[]{:S(2)}, u32[]{:S(2)}) async-start(f32[16,1,256]{2,1,0:T(1,128)} %reshape.227), calls=%async_computation | async-start | bytes 32768 | tf_op jit(solution)/shard_map/while/body/eval_jaxpr/all_to_all | solution.py:22
  288.9 13.4 %copy-start.2 = (bf16[1,1,128,1024]{3,2,1,0:T(8,128)(2,1)S(1)}, bf16[1,1,128,1024]{3,2,1,0:T(8,128)(2,1)}, u32[]{:S(2)}) copy-start(bf16[1,1,128,1024]{3,2,1,0:T(8,128)(2,1)} %get-tuple-element.454) | copy-start | bytes 786436 | tf_op jit(solution)/shard_map/while
  289.5 12.7 %all-to-all-start.2 = ((f32[8,4,1024]{2,1,0:T(4,128)}), f32[8,4,1024]{2,1,0:T(4,128)S(1)}, u32[]{:S(2)}, u32[]{:S(2)}) async-start(f32[8,4,1024]{2,1,0:T(4,128)} %broadcast_in_dim.151), calls=%async_computation.2 | async-start | bytes 262144 | tf_op jit(solution)/shard_map/while/body/eval_jaxpr/all_to_all | solution.py:28
  302.8 13.1 %copy-start.3 = (bf16[1,64,1024]{2,1,0:T(8,128)(2,1)S(1)}, bf16[1,64,1024]{2,1,0:T(8,128)(2,1)}, u32[]{:S(2)}) copy-start(bf16[1,64,1024]{2,1,0:T(8,128)(2,1)} %get-tuple-element.450) | copy-start | bytes 393220 | tf_op jit(solution)/shard_map/while
  303.5 11.0 %all-to-all-start = ((f32[16,1,256]{2,1,0:T(1,128)}), f32[16,1,256]{2,1,0:T(1,128)S(1)}, u32[]{:S(2)}, u32[]{:S(2)}) async-start(f32[16,1,256]{2,1,0:T(1,128)} %reshape.227), calls=%async_computation | async-start | bytes 32768 | tf_op jit(solution)/shard_map/while/body/eval_jaxpr/all_to_all | solution.py:22
  331.5 13.4 %copy-start.2 = (bf16[1,1,128,1024]{3,2,1,0:T(8,128)(2,1)S(1)}, bf16[1,1,128,1024]{3,2,1,0:T(8,128)(2,1)}, u32[]{:S(2)}) copy-start(bf16[1,1,128,1024]{3,2,1,0:T(8,128)(2,1)} %get-tuple-element.454) | copy-start | bytes 786436 | tf_op jit(solution)/shard_map/while
  332.2 12.7 %all-to-all-start.2 = ((f32[8,4,1024]{2,1,0:T(4,128)}), f32[8,4,1024]{2,1,0:T(4,128)S(1)}, u32[]{:S(2)}, u32[]{:S(2)}) async-start(f32[8,4,1024]{2,1,0:T(4,128)} %broadcast_in_dim.151), calls=%async_computation.2 | async-start | bytes 262144 | tf_op jit(solution)/shard_map/while/body/eval_jaxpr/all_to_all | solution.py:28
  345.4 13.1 %copy-start.3 = (bf16[1,64,1024]{2,1,0:T(8,128)(2,1)S(1)}, bf16[1,64,1024]{2,1,0:T(8,128)(2,1)}, u32[]{:S(2)}) copy-start(bf16[1,64,1024]{2,1,0:T(8,128)(2,1)} %get-tuple-element.450) | copy-start | bytes 393220 | tf_op jit(solution)/shard_map/while
  346.1 11.0 %all-to-all-start = ((f32[16,1,256]{2,1,0:T(1,128)}), f32[16,1,256]{2,1,0:T(1,128)S(1)}, u32[]{:S(2)}, u32[]{:S(2)}) async-start(f32[16,1,256]{2,1,0:T(1,128)} %reshape.227), calls=%async_computation | async-start | bytes 32768 | tf_op jit(solution)/shard_map/while/body/eval_jaxpr/all_to_all | solution.py:22
  374.1 13.4 %copy-start.2 = (bf16[1,1,128,1024]{3,2,1,0:T(8,128)(2,1)S(1)}, bf16[1,1,128,1024]{3,2,1,0:T(8,128)(2,1)}, u32[]{:S(2)}) copy-start(bf16[1,1,128,1024]{3,2,1,0:T(8,128)(2,1)} %get-tuple-element.454) | copy-start | bytes 786436 | tf_op jit(solution)/shard_map/while
  374.8 12.7 %all-to-all-start.2 = ((f32[8,4,1024]{2,1,0:T(4,128)}), f32[8,4,1024]{2,1,0:T(4,128)S(1)}, u32[]{:S(2)}, u32[]{:S(2)}) async-start(f32[8,4,1024]{2,1,0:T(4,128)} %broadcast_in_dim.151), calls=%async_computation.2 | async-start | bytes 262144 | tf_op jit(solution)/shard_map/while/body/eval_jaxpr/all_to_all | solution.py:28
  388.0 13.1 %copy-start.3 = (bf16[1,64,1024]{2,1,0:T(8,128)(2,1)S(1)}, bf16[1,64,1024]{2,1,0:T(8,128)(2,1)}, u32[]{:S(2)}) copy-start(bf16[1,64,1024]{2,1,0:T(8,128)(2,1)} %get-tuple-element.450) | copy-start | bytes 393220 | tf_op jit(solution)/shard_map/while
  388.7 11.0 %all-to-all-start = ((f32[16,1,256]{2,1,0:T(1,128)}), f32[16,1,256]{2,1,0:T(1,128)S(1)}, u32[]{:S(2)}, u32[]{:S(2)}) async-start(f32[16,1,256]{2,1,0:T(1,128)} %reshape.227), calls=%async_computation | async-start | bytes 32768 | tf_op jit(solution)/shard_map/while/body/eval_jaxpr/all_to_all | solution.py:22
  416.8 13.4 %copy-start.2 = (bf16[1,1,128,1024]{3,2,1,0:T(8,128)(2,1)S(1)}, bf16[1,1,128,1024]{3,2,1,0:T(8,128)(2,1)}, u32[]{:S(2)}) copy-start(bf16[1,1,128,1024]{3,2,1,0:T(8,128)(2,1)} %get-tuple-element.454) | copy-start | bytes 786436 | tf_op jit(solution)/shard_map/while
  417.4 12.7 %all-to-all-start.2 = ((f32[8,4,1024]{2,1,0:T(4,128)}), f32[8,4,1024]{2,1,0:T(4,128)S(1)}, u32[]{:S(2)}, u32[]{:S(2)}) async-start(f32[8,4,1024]{2,1,0:T(4,128)} %broadcast_in_dim.151), calls=%async_computation.2 | async-start | bytes 262144 | tf_op jit(solution)/shard_map/while/body/eval_jaxpr/all_to_all | solution.py:28
  430.6 13.1 %copy-start.3 = (bf16[1,64,1024]{2,1,0:T(8,128)(2,1)S(1)}, bf16[1,64,1024]{2,1,0:T(8,128)(2,1)}, u32[]{:S(2)}) copy-start(bf16[1,64,1024]{2,1,0:T(8,128)(2,1)} %get-tuple-element.450) | copy-start | bytes 393220 | tf_op jit(solution)/shard_map/while
  431.4 11.0 %all-to-all-start = ((f32[16,1,256]{2,1,0:T(1,128)}), f32[16,1,256]{2,1,0:T(1,128)S(1)}, u32[]{:S(2)}, u32[]{:S(2)}) async-start(f32[16,1,256]{2,1,0:T(1,128)} %reshape.227), calls=%async_computation | async-start | bytes 32768 | tf_op jit(solution)/shard_map/while/body/eval_jaxpr/all_to_all | solution.py:22
  459.4 13.4 %copy-start.2 = (bf16[1,1,128,1024]{3,2,1,0:T(8,128)(2,1)S(1)}, bf16[1,1,128,1024]{3,2,1,0:T(8,128)(2,1)}, u32[]{:S(2)}) copy-start(bf16[1,1,128,1024]{3,2,1,0:T(8,128)(2,1)} %get-tuple-element.454) | copy-start | bytes 786436 | tf_op jit(solution)/shard_map/while
  460.0 12.7 %all-to-all-start.2 = ((f32[8,4,1024]{2,1,0:T(4,128)}), f32[8,4,1024]{2,1,0:T(4,128)S(1)}, u32[]{:S(2)}, u32[]{:S(2)}) async-start(f32[8,4,1024]{2,1,0:T(4,128)} %broadcast_in_dim.151), calls=%async_computation.2 | async-start | bytes 262144 | tf_op jit(solution)/shard_map/while/body/eval_jaxpr/all_to_all | solution.py:28
  473.3 13.1 %copy-start.3 = (bf16[1,64,1024]{2,1,0:T(8,128)(2,1)S(1)}, bf16[1,64,1024]{2,1,0:T(8,128)(2,1)}, u32[]{:S(2)}) copy-start(bf16[1,64,1024]{2,1,0:T(8,128)(2,1)} %get-tuple-element.450) | copy-start | bytes 393220 | tf_op jit(solution)/shard_map/while
  474.0 11.0 %all-to-all-start = ((f32[16,1,256]{2,1,0:T(1,128)}), f32[16,1,256]{2,1,0:T(1,128)S(1)}, u32[]{:S(2)}, u32[]{:S(2)}) async-start(f32[16,1,256]{2,1,0:T(1,128)} %reshape.227), calls=%async_computation | async-start | bytes 32768 | tf_op jit(solution)/shard_map/while/body/eval_jaxpr/all_to_all | solution.py:22
  502.0 13.4 %copy-start.2 = (bf16[1,1,128,1024]{3,2,1,0:T(8,128)(2,1)S(1)}, bf16[1,1,128,1024]{3,2,1,0:T(8,128)(2,1)}, u32[]{:S(2)}) copy-start(bf16[1,1,128,1024]{3,2,1,0:T(8,128)(2,1)} %get-tuple-element.454) | copy-start | bytes 786436 | tf_op jit(solution)/shard_map/while
  502.7 12.7 %all-to-all-start.2 = ((f32[8,4,1024]{2,1,0:T(4,128)}), f32[8,4,1024]{2,1,0:T(4,128)S(1)}, u32[]{:S(2)}, u32[]{:S(2)}) async-start(f32[8,4,1024]{2,1,0:T(4,128)} %broadcast_in_dim.151), calls=%async_computation.2 | async-start | bytes 262144 | tf_op jit(solution)/shard_map/while/body/eval_jaxpr/all_to_all | solution.py:28
  515.9 13.1 %copy-start.3 = (bf16[1,64,1024]{2,1,0:T(8,128)(2,1)S(1)}, bf16[1,64,1024]{2,1,0:T(8,128)(2,1)}, u32[]{:S(2)}) copy-start(bf16[1,64,1024]{2,1,0:T(8,128)(2,1)} %get-tuple-element.450) | copy-start | bytes 393220 | tf_op jit(solution)/shard_map/while
  516.6 11.0 %all-to-all-start = ((f32[16,1,256]{2,1,0:T(1,128)}), f32[16,1,256]{2,1,0:T(1,128)S(1)}, u32[]{:S(2)}, u32[]{:S(2)}) async-start(f32[16,1,256]{2,1,0:T(1,128)} %reshape.227), calls=%async_computation | async-start | bytes 32768 | tf_op jit(solution)/shard_map/while/body/eval_jaxpr/all_to_all | solution.py:22
  544.6 13.4 %copy-start.2 = (bf16[1,1,128,1024]{3,2,1,0:T(8,128)(2,1)S(1)}, bf16[1,1,128,1024]{3,2,1,0:T(8,128)(2,1)}, u32[]{:S(2)}) copy-start(bf16[1,1,128,1024]{3,2,1,0:T(8,128)(2,1)} %get-tuple-element.454) | copy-start | bytes 786436 | tf_op jit(solution)/shard_map/while
  545.3 12.7 %all-to-all-start.2 = ((f32[8,4,1024]{2,1,0:T(4,128)}), f32[8,4,1024]{2,1,0:T(4,128)S(1)}, u32[]{:S(2)}, u32[]{:S(2)}) async-start(f32[8,4,1024]{2,1,0:T(4,128)} %broadcast_in_dim.151), calls=%async_computation.2 | async-start | bytes 262144 | tf_op jit(solution)/shard_map/while/body/eval_jaxpr/all_to_all | solution.py:28
  558.5 13.1 %copy-start.3 = (bf16[1,64,1024]{2,1,0:T(8,128)(2,1)S(1)}, bf16[1,64,1024]{2,1,0:T(8,128)(2,1)}, u32[]{:S(2)}) copy-start(bf16[1,64,1024]{2,1,0:T(8,128)(2,1)} %get-tuple-element.450) | copy-start | bytes 393220 | tf_op jit(solution)/shard_map/while
  559.2 11.0 %all-to-all-start = ((f32[16,1,256]{2,1,0:T(1,128)}), f32[16,1,256]{2,1,0:T(1,128)S(1)}, u32[]{:S(2)}, u32[]{:S(2)}) async-start(f32[16,1,256]{2,1,0:T(1,128)} %reshape.227), calls=%async_computation | async-start | bytes 32768 | tf_op jit(solution)/shard_map/while/body/eval_jaxpr/all_to_all | solution.py:22
  587.3 13.4 %copy-start.2 = (bf16[1,1,128,1024]{3,2,1,0:T(8,128)(2,1)S(1)}, bf16[1,1,128,1024]{3,2,1,0:T(8,128)(2,1)}, u32[]{:S(2)}) copy-start(bf16[1,1,128,1024]{3,2,1,0:T(8,128)(2,1)} %get-tuple-element.454) | copy-start | bytes 786436 | tf_op jit(solution)/shard_map/while
  587.9 12.7 %all-to-all-start.2 = ((f32[8,4,1024]{2,1,0:T(4,128)}), f32[8,4,1024]{2,1,0:T(4,128)S(1)}, u32[]{:S(2)}, u32[]{:S(2)}) async-start(f32[8,4,1024]{2,1,0:T(4,128)} %broadcast_in_dim.151), calls=%async_computation.2 | async-start | bytes 262144 | tf_op jit(solution)/shard_map/while/body/eval_jaxpr/all_to_all | solution.py:28
  601.1 13.1 %copy-start.3 = (bf16[1,64,1024]{2,1,0:T(8,128)(2,1)S(1)}, bf16[1,64,1024]{2,1,0:T(8,128)(2,1)}, u32[]{:S(2)}) copy-start(bf16[1,64,1024]{2,1,0:T(8,128)(2,1)} %get-tuple-element.450) | copy-start | bytes 393220 | tf_op jit(solution)/shard_map/while
  601.9 11.0 %all-to-all-start = ((f32[16,1,256]{2,1,0:T(1,128)}), f32[16,1,256]{2,1,0:T(1,128)S(1)}, u32[]{:S(2)}, u32[]{:S(2)}) async-start(f32[16,1,256]{2,1,0:T(1,128)} %reshape.227), calls=%async_computation | async-start | bytes 32768 | tf_op jit(solution)/shard_map/while/body/eval_jaxpr/all_to_all | solution.py:22
  629.9 13.4 %copy-start.2 = (bf16[1,1,128,1024]{3,2,1,0:T(8,128)(2,1)S(1)}, bf16[1,1,128,1024]{3,2,1,0:T(8,128)(2,1)}, u32[]{:S(2)}) copy-start(bf16[1,1,128,1024]{3,2,1,0:T(8,128)(2,1)} %get-tuple-element.454) | copy-start | bytes 786436 | tf_op jit(solution)/shard_map/while
  630.6 12.7 %all-to-all-start.2 = ((f32[8,4,1024]{2,1,0:T(4,128)}), f32[8,4,1024]{2,1,0:T(4,128)S(1)}, u32[]{:S(2)}, u32[]{:S(2)}) async-start(f32[8,4,1024]{2,1,0:T(4,128)} %broadcast_in_dim.151), calls=%async_computation.2 | async-start | bytes 262144 | tf_op jit(solution)/shard_map/while/body/eval_jaxpr/all_to_all | solution.py:28
  643.8 13.1 %copy-start.3 = (bf16[1,64,1024]{2,1,0:T(8,128)(2,1)S(1)}, bf16[1,64,1024]{2,1,0:T(8,128)(2,1)}, u32[]{:S(2)}) copy-start(bf16[1,64,1024]{2,1,0:T(8,128)(2,1)} %get-tuple-element.450) | copy-start | bytes 393220 | tf_op jit(solution)/shard_map/while
  644.5 11.0 %all-to-all-start = ((f32[16,1,256]{2,1,0:T(1,128)}), f32[16,1,256]{2,1,0:T(1,128)S(1)}, u32[]{:S(2)}, u32[]{:S(2)}) async-start(f32[16,1,256]{2,1,0:T(1,128)} %reshape.227), calls=%async_computation | async-start | bytes 32768 | tf_op jit(solution)/shard_map/while/body/eval_jaxpr/all_to_all | solution.py:22
  672.5 13.4 %copy-start.2 = (bf16[1,1,128,1024]{3,2,1,0:T(8,128)(2,1)S(1)}, bf16[1,1,128,1024]{3,2,1,0:T(8,128)(2,1)}, u32[]{:S(2)}) copy-start(bf16[1,1,128,1024]{3,2,1,0:T(8,128)(2,1)} %get-tuple-element.454) | copy-start | bytes 786436 | tf_op jit(solution)/shard_map/while
  673.2 12.7 %all-to-all-start.2 = ((f32[8,4,1024]{2,1,0:T(4,128)}), f32[8,4,1024]{2,1,0:T(4,128)S(1)}, u32[]{:S(2)}, u32[]{:S(2)}) async-start(f32[8,4,1024]{2,1,0:T(4,128)} %broadcast_in_dim.151), calls=%async_computation.2 | async-start | bytes 262144 | tf_op jit(solution)/shard_map/while/body/eval_jaxpr/all_to_all | solution.py:28
  (17 other events, 204.0 us)
where the time goes:
time: 719 us; the launch traced here: 709 us
  blocking collectives  263 us (37%)
  waiting for transfers between devices  208 us (29%)
  starting transfers between devices  163 us (23%)
  local copies, waits for them, and re-layouts  37.4 us (5%)
  other arithmetic  15.5 us (2%)
  loops' own time  12.7 us (2%)
    all_to_all x16, blocking collectives, from_everyone(): lax.all_to_all(jnp.broadcast_to(array[None], (devices, *array.shape)), ax...  245 us
    all_to_all x16, waiting for transfers between devices, summed_on_arrival(): lax.all_to_all(pieces, axis, split_axis=0, concat_axis=0, tiled=True)  121 us
    all_to_all x16, starting transfers between devices, from_everyone(): lax.all_to_all(jnp.broadcast_to(array[None], (devices, *array.shape)), ax...  104 us
    all_to_all x16, waiting for transfers between devices, from_everyone(): lax.all_to_all(jnp.broadcast_to(array[None], (devices, *array.shape)), ax...  87.7 us
    all_to_all x16, starting transfers between devices, summed_on_arrival(): lax.all_to_all(pieces, axis, split_axis=0, concat_axis=0, tiled=True)  59.5 us
    psum x2, blocking collectives, one_axis_at_a_time(): return functools.reduce(lax.psum, axes, array)  18.4 us
  transfers between devices with their start and end apart: 32, of which 32 were waited for; matrix products, arithmetic and copies ran while one was open for 0% of the time, Pallas kernels for 0%

commit v1 on v0

v1 whole, which is shorter than its diff:
```python
import math

import jax
import jax.numpy as jnp
from jax import lax
from jax.sharding import PartitionSpec as P

ROW = "row"
COL = "col"
BOTH = (ROW, COL)
SIDE = 4
CHAIN_PERIOD = 8
SPREAD_PERIOD = 7
ARRIVAL = {2: 0, 3: 1, 4: 1, 5: 2, 6: 2, 7: 2, 8: 3, 9: 3, 10: 3, 11: 3, 12: 4, 13: 4, 14: 4, 15: 4}
SENDER = {2: 1, 3: 1, 4: 2, 5: 1, 6: 2, 7: 4, 8: 1, 9: 2, 10: 4, 11: 6, 12: 1, 13: 2, 14: 4, 15: 6}


def solver(i):
    return (i, max(i - 1, 0))


def union(rounds, period):
    patterns = []
    for first in range(min(period, len(rounds))):
        pairs = sorted({pair for moves in rounds[first::period] for pair in moves})
        assert len({s for s, _ in pairs}) == len(pairs) == len({d for _, d in pairs})
        patterns.append(pairs)
    return [patterns[r % period] for r in range(len(rounds))]


def plan(n):
    chain, spread, gather = [], [], []
    for r in range(n - 1):
        chain.append([(solver(r), solver(r + 1))])
        spread_moves, gather_moves = [], []
        for i in range(n):
            for j in range(i - 1):
                d = i - j
                if j + ARRIVAL[d] == r:
                    source = solver(j) if SENDER[d] == 1 else (j + SENDER[d], j)
                    spread_moves.append((source, (i, j)))
                if i - 1 - (d - 2) // 2 == r:
                    (spread_moves if d % 2 else gather_moves).append(((i, j), solver(i)))
        spread.append(spread_moves)
        gather.append(gather_moves)
    return union(chain, CHAIN_PERIOD), union(spread, SPREAD_PERIOD), union(gather, SPREAD_PERIOD)


def local(right_side, inverse_t, u_factor, v_factor, ranks):
    n = lax.axis_size(ROW)
    n_col = lax.axis_size(COL)
    nrhs, width = right_side.shape[2:]
    piece = width // n_col
    quarter = width // SIDE
    rank_max = u_factor.shape[4]
    row = lax.axis_index(ROW)
    col = lax.axis_index(COL)
    source = right_side.reshape(nrhs, width)
    u_tile = u_factor.reshape(rank_max, width)
    v_tile = v_factor.reshape(rank_max, width)
    limit = ranks.reshape(1, 1)

    def move(array, pairs):
        numbered = [(s[0] * n_col + s[1], d[0] * n_col + d[1]) for s, d in pairs]
        return lax.ppermute(array, BOTH, numbered)

    def home(r):
        return divmod(solver(r)[1], SIDE)

    rows = inverse_t.reshape(piece, width).astype(jnp.float32)
    slabs = []
    for k in range(SIDE):
        pairs = []
        for r in range(n):
            for x in range(SIDE):
                if home(r)[1] != k:
                    pairs.append(((r, x * SIDE + k), (r, x * SIDE + home(r)[1])))
        slabs.append(move(rows, pairs) + jnp.where(col % SIDE == k, rows, 0.0))
    block = jnp.concatenate(slabs, axis=0)
    quarters = []
    for k in range(SIDE):
        pairs = []
        for r in range(n):
            x, y = home(r)
            if x != k:
                pairs.append(((r, k * SIDE + y), (r, x * SIDE + y)))
        part = block[:, k * quarter :]
        got = (move(part, pairs) + jnp.where(col // SIDE == k, part, 0.0)).astype(jnp.bfloat16)
        quarters.append(jnp.pad(got, ((0, 0), (k * quarter, 0))))
    inverse = lax.optimization_barrier(jnp.concatenate(quarters, axis=0))

    gap = row - col
    solves = (gap == 1) | ((row == 0) & (col == 0))
    keep = jnp.arange(rank_max, dtype=jnp.int32)[:, None] < limit

    def contribution(known):
        inner = jnp.einsum("rn,kn->rk", v_tile, known.astype(jnp.bfloat16), preferred_element_type=jnp.float32)
        inner = jnp.where(keep, inner, 0.0).astype(jnp.bfloat16)
        return jnp.einsum("rk,rn->kn", inner, u_tile, preferred_element_type=jnp.float32)

    def solve(known, pending):
        own = contribution(known)
        reduced = (source - pending - own).astype(jnp.bfloat16)
        return own, jnp.dot(reduced, inverse, preferred_element_type=jnp.float32)

    arrival = jnp.zeros((), jnp.int32)
    for d, when in ARRIVAL.items():
        arrival = jnp.where(gap == d, when, arrival)
    chain, spread, gather = plan(n)
    known = jnp.zeros((nrhs, width), jnp.float32)
    pending = jnp.zeros((nrhs, width), jnp.float32)
    own, result = solve(known, pending)
    for r in range(n - 1):
        behind = row - 1 - r
        first = move(result, chain[r])
        third = move(own, gather[r])
        second = move(jnp.where(solves, result, jnp.where(gap % 2 == 1, own, known)), spread[r])
        takes = (gap == 1) & (col == r)
        hears = (gap >= 2) & (col + arrival == r)
        adds = (gap == 1) & (behind >= 0)
        adds_odd = adds & (3 + 2 * behind <= row)
        adds_even = adds & (2 + 2 * behind <= row)
        known = known + jnp.where(takes, first, 0.0) + jnp.where(hears, second, 0.0)
        pending = pending + jnp.where(adds_odd, second, 0.0) + jnp.where(adds_even, third, 0.0)
        own, result = solve(known, pending)

    square = lax.dynamic_slice_in_dim(rows, col * piece, piece, 1)
    log_sum = jnp.sum(jnp.log(jnp.diagonal(square)))
    payload = jnp.concatenate([result, jnp.broadcast_to(log_sum, (nrhs, 128))], axis=1)
    payload = jnp.broadcast_to(payload[None], (n_col, *payload.shape))
    arrived = lax.all_to_all(payload, COL, 0, 0, tiled=True)
    solved = lax.dynamic_index_in_dim(arrived, jnp.maximum(row - 1, 0), 0, False)[:, :width]
    logdiag = jnp.sum(arrived[:, 0, width]) / width
    quadratic = jnp.mean(solved * solved, axis=1)
    loglik = -0.5 * quadratic + logdiag - 0.5 * math.log(2.0 * math.pi)
    return solved.reshape(1, 1, nrhs, width), loglik.reshape(1, 1, nrhs)


def solution(mesh):
    return jax.shard_map(
        local,
        mesh=mesh,
        in_specs=(
            P(None, ROW, None, None),
            P(None, ROW, COL, None),
            P(None, ROW, None, COL, None, None),
            P(None, ROW, None, COL, None, None),
            P(None, ROW, None, COL),
        ),
        out_specs=(P(None, ROW, None, None), P(None, ROW, None)),
        check_vma=False,
    )
```

time: 719 us -> 215 us (0.30); the launches traced: 709 us -> 214 us
  blocking collectives: 263 us -> 0 us
  waiting for transfers between devices: 208 us -> 31.2 us
  local copies, waits for them, and re-layouts: 37.4 us -> 5.02 us
  loops' own time: 12.7 us -> 0 us
  starting transfers between devices: 163 us -> 151 us
    all_to_all x16 -> x0, blocking collectives: 245 us -> none  [from_everyone(): lax.all_to_all(jnp.broadcast_to(array[None], (devices, *array.shape)), ax...]
    all_to_all x32 -> x1, waiting for transfers between devices: 208 us -> 8.66 us  [local(): arrived = lax.all_to_all(payload, COL, 0, 0, tiled=True)]
    all_to_all x32 -> x1, starting transfers between devices: 163 us -> 4.87 us  [local(): arrived = lax.all_to_all(payload, COL, 0, 0, tiled=True)]
    ppermute x0 -> x53, starting transfers between devices: none -> 146 us  [move(): return lax.ppermute(array, BOTH, numbered)]
    ppermute x0 -> x53, waiting for transfers between devices: none -> 22.5 us  [move(): return lax.ppermute(array, BOTH, numbered)]
    psum x2 -> x0, blocking collectives: 18.4 us -> none  [one_axis_at_a_time(): return functools.reduce(lax.psum, axes, array)]
    another operation x17 -> x0, loops' own time: 12.7 us -> none  [the longest x1 12.3 us: local(): lax.fori_loop(0, slab, right_step, (empty_rows, jnp.zeros((cycles, nrhs,...]
    while x128 -> x0, local copies, waits for them, and re-layouts: 12.7 us -> none
  transfers between devices with their start and end apart: 32 -> 54, of which waited for: 32 -> 6; matrix products, arithmetic and copies ran while one was open for 0% -> 4% of each run, Pallas kernels for 0% -> 0%
where the time goes in v1:
time: 215 us; the launch traced here: 214 us
  starting transfers between devices  151 us (70%)
  waiting for transfers between devices  31.2 us (15%)
  matrix products  12.2 us (6%)
  other arithmetic  10.8 us (5%)
  local copies, waits for them, and re-layouts  5.02 us (2%)
  between operations  3.32 us (2%)
    ppermute x53, starting transfers between devices, move(): return lax.ppermute(array, BOTH, numbered)  146 us
    ppermute x53, waiting for transfers between devices, move(): return lax.ppermute(array, BOTH, numbered)  22.5 us
    all_to_all x1, waiting for transfers between devices, local(): arrived = lax.all_to_all(payload, COL, 0, 0, tiled=True)  8.66 us
    dot_general x16, matrix products, solve(): return (own, jnp.dot(reduced, inverse, preferred_element_type=jnp.float32))  6.24 us
    dot_general x16, matrix products, contribution(): jnp.einsum('rk,rn->kn', inner, u_tile, preferred_element_type=jnp.float32)  5.92 us
    all_to_all x1, starting transfers between devices, local(): arrived = lax.all_to_all(payload, COL, 0, 0, tiled=True)  4.87 us
    convert_element_type x4, other arithmetic, local(): (move(part, pairs) + jnp.where(col // SIDE == k, part, 0.0)).astype(jnp.b...  4.82 us
  transfers between devices with their start and end apart: 54, of which 6 were waited for; matrix products, arithmetic and copies ran while one was open for 4% of the time, Pallas kernels for 0%

profile of v1, /device:TPU:224, one launch (start us, length us, event | category | flops | bytes accessed | tf_op | source)
XLA Modules:
  0.0 213.6 jit_solution(7747128901419990619)
XLA Ops:
  0.6 1.7 fusion.241
  2.3 3.5 %collective-permute-start = (f32[64,1024]{1,0:T(8,128)S(1)}, f32[64,1024]{1,0:T(8,128)S(1)}, u32[]{:S(2)}, u32[]{:S(2)}) collective-permute-start(f32[64,1024]{1,0:T(8,128)S(1)} %get-tuple-element.3), channel_id=1, source_target_pairs={{32,33},{36,37},{40,41},{44,45},{48,50},{52,54},{56,58},{60,62},{6... | collective-permute-start | bytes 786440 | tf_op jit(solution)/shard_map/ppermute | solution.py:65
  5.8 0.7 collective-permute-start.1
  6.5 0.7 collective-permute-start.2
  7.2 0.7 collective-permute-start.3
  8.6 3.5 %collective-permute-done = f32[64,1024]{1,0:T(8,128)S(1)} collective-permute-done((f32[64,1024]{1,0:T(8,128)S(1)}, f32[64,1024]{1,0:T(8,128)S(1)}, u32[]{:S(2)}, u32[]{:S(2)}) %collective-permute-start) | collective-permute-done | bytes 262176 | tf_op jit(solution)/shard_map/ppermute | solution.py:65
  12.0 1.1 select_add_fusion.3
  13.2 1.8 collective-permute-start.4
  15.1 0.8 slice.23
  15.9 0.7 slice.24
  16.6 1.6 collective-permute-start.5
  18.2 1.5 collective-permute-start.6
  19.6 1.4 collective-permute-start.7
  21.4 1.0 add_convert_fusion.3
  22.4 1.1 add_convert_fusion.2
  23.6 1.2 add_convert_fusion.1
  24.8 1.4 add_convert_fusion
  28.0 0.7 collective-permute-start.8
  28.7 25.2 %collective-permute-start.9 = (f32[4,1024]{1,0:T(4,128)S(1)}, f32[4,1024]{1,0:T(4,128)S(1)}, u32[]{:S(2)}, u32[]{:S(2)}) collective-permute-start(f32[4,1024]{1,0:T(4,128)S(1)} %fusion.39), channel_id=1, source_target_pairs={{134,135},{149,152},{164,169},{179,186},{194,203},{209,220},{224,2... | collective-permute-start | bytes 49160 | tf_op jit(solution)/shard_map/ppermute | solution.py:65
  54.3 0.9 collective-permute-done.9
  56.3 0.7 collective-permute-start.13
  57.0 0.7 collective-permute-start.12
  59.2 0.7 collective-permute-start.16
  59.9 0.7 collective-permute-start.15
  61.4 0.7 collective-permute-start.17
  62.1 0.7 collective-permute-start.19
  62.7 0.7 collective-permute-start.18
  64.3 1.3 collective-permute-start.20
  65.5 0.7 collective-permute-start.22
  66.2 0.7 collective-permute-start.21
  66.9 10.7 %collective-permute-done.20 = f32[4,1024]{1,0:T(4,128)S(1)} collective-permute-done((f32[4,1024]{1,0:T(4,128)S(1)}, f32[4,1024]{1,0:T(4,128)S(1)}, u32[]{:S(2)}, u32[]{:S(2)}) %collective-permute-start.20) | collective-permute-done | bytes 16416 | tf_op jit(solution)/shard_map/ppermute | solution.py:65
  79.0 0.7 collective-permute-start.25
  79.7 0.7 collective-permute-start.24
  81.2 0.7 collective-permute-start.26
  81.9 0.7 collective-permute-start.28
  82.6 0.7 collective-permute-start.27
  84.1 0.7 collective-permute-start.29
  84.8 0.7 collective-permute-start.31
  85.4 39.2 %collective-permute-start.30 = (f32[4,1024]{1,0:T(4,128)S(1)}, f32[4,1024]{1,0:T(4,128)S(1)}, u32[]{:S(2)}, u32[]{:S(2)}) collective-permute-start(f32[4,1024]{1,0:T(4,128)S(1)} %fusion.32), channel_id=1, source_target_pairs={{134,135},{149,152},{164,169},{179,186},{194,203},{209,220},{224,2... | collective-permute-start | bytes 49160 | tf_op jit(solution)/shard_map/ppermute | solution.py:65
  124.7 1.4 collective-permute-done.30
  127.5 0.7 collective-permute-start.34
  128.2 0.7 collective-permute-start.33
  129.7 0.7 collective-permute-start.35
  130.4 0.7 collective-permute-start.37
  131.0 0.7 collective-permute-start.36
  132.6 0.7 collective-permute-start.38
  133.2 0.7 collective-permute-start.40
  133.9 0.7 collective-permute-start.39
  135.4 1.3 collective-permute-start.41
  136.7 0.7 collective-permute-start.43
  137.4 0.7 collective-permute-start.42
  138.1 6.0 %collective-permute-done.41 = f32[4,1024]{1,0:T(4,128)S(1)} collective-permute-done((f32[4,1024]{1,0:T(4,128)S(1)}, f32[4,1024]{1,0:T(4,128)S(1)}, u32[]{:S(2)}, u32[]{:S(2)}) %collective-permute-start.41) | collective-permute-done | bytes 16416 | tf_op jit(solution)/shard_map/ppermute | solution.py:65
  144.5 0.7 collective-permute-start.45
  146.2 0.7 collective-permute-start.46
  146.9 0.8 dynamic-slice_bitcast_fusion
  148.1 0.7 collective-permute-start.48
  149.8 0.7 collective-permute-start.49
  150.5 0.8 gather_fusion
  151.8 41.2 %collective-permute-start.51 = (f32[4,1024]{1,0:T(4,128)S(1)}, f32[4,1024]{1,0:T(4,128)S(1)}, u32[]{:S(2)}, u32[]{:S(2)}) collective-permute-start(f32[4,1024]{1,0:T(4,128)S(1)} %fusion.25), channel_id=1, source_target_pairs={{134,135},{149,152},{164,169},{179,186},{194,203},{209,220},{224,2... | collective-permute-start | bytes 49160 | tf_op jit(solution)/shard_map/ppermute | solution.py:65
  194.0 0.7 collective-permute-start.52
  196.8 0.8 broadcast_in_dim.179
  197.5 4.9 %all-to-all-start = ((f32[16,4,1152]{2,1,0:T(4,128)}), f32[16,4,1152]{2,1,0:T(4,128)S(1)}, u32[]{:S(2)}, u32[]{:S(2)}) async-start(f32[16,4,1152]{2,1,0:T(4,128)} %broadcast_in_dim.179), calls=%async_computation | async-start | bytes 589824 | tf_op jit(solution)/shard_map/all_to_all | solution.py:131
  202.4 8.7 %all-to-all-done = f32[16,4,1152]{2,1,0:T(4,128)S(1)} async-done(((f32[16,4,1152]{2,1,0:T(4,128)}), f32[16,4,1152]{2,1,0:T(4,128)S(1)}, u32[]{:S(2)}, u32[]{:S(2)}) %all-to-all-start) | async-done | bytes 294944 | tf_op jit(solution)/shard_map/all_to_all | solution.py:131
  211.1 0.7 multiply_reduce_fusion
  (118 shorter events, 21.1 us)
Async XLA Ops:
  0.6 20.4 %copy-start = (bf16[1,1,1,1,128,1024]{5,4,3,2,1,0:T(8,128)(2,1)S(1)}, bf16[1,1,1,1,128,1024]{5,4,3,2,1,0:T(8,128)(2,1)}, u32[]{:S(2)}) copy-start(bf16[1,1,1,1,128,1024]{5,4,3,2,1,0:T(8,128)(2,1)} %param.7) | copy-start | bytes 786436
  2.3 9.7 %collective-permute-start = (f32[64,1024]{1,0:T(8,128)S(1)}, f32[64,1024]{1,0:T(8,128)S(1)}, u32[]{:S(2)}, u32[]{:S(2)}) collective-permute-start(f32[64,1024]{1,0:T(8,128)S(1)} %get-tuple-element.3), channel_id=1, source_target_pairs={{32,33},{36,37},{40,41},{44,45},{48,50},{52,54},{56,58},{60,62},{6... | collective-permute-start | bytes 786440 | tf_op jit(solution)/shard_map/ppermute | solution.py:65
  5.8 6.2 %collective-permute-start.1 = (f32[64,1024]{1,0:T(8,128)S(1)}, f32[64,1024]{1,0:T(8,128)S(1)}, u32[]{:S(2)}, u32[]{:S(2)}) collective-permute-start(f32[64,1024]{1,0:T(8,128)S(1)} %get-tuple-element.3), channel_id=1, source_target_pairs={{1,0},{5,4},{9,8},{13,12},{17,16},{21,20},{25,24},{29,28},{49,50},... | collective-permute-start | bytes 786440 | tf_op jit(solution)/shard_map/ppermute | solution.py:65
  6.5 5.5 %collective-permute-start.2 = (f32[64,1024]{1,0:T(8,128)S(1)}, f32[64,1024]{1,0:T(8,128)S(1)}, u32[]{:S(2)}, u32[]{:S(2)}) collective-permute-start(f32[64,1024]{1,0:T(8,128)S(1)} %get-tuple-element.3), channel_id=1, source_target_pairs={{2,0},{6,4},{10,8},{14,12},{18,16},{22,20},{26,24},{30,28},{34,33}... | collective-permute-start | bytes 786440 | tf_op jit(solution)/shard_map/ppermute | solution.py:65
  7.2 4.8 %collective-permute-start.3 = (f32[64,1024]{1,0:T(8,128)S(1)}, f32[64,1024]{1,0:T(8,128)S(1)}, u32[]{:S(2)}, u32[]{:S(2)}) collective-permute-start(f32[64,1024]{1,0:T(8,128)S(1)} %get-tuple-element.3), channel_id=1, source_target_pairs={{3,0},{7,4},{11,8},{15,12},{19,16},{23,20},{27,24},{31,28},{35,33}... | collective-permute-start | bytes 786440 | tf_op jit(solution)/shard_map/ppermute | solution.py:65
  13.2 7.8 %copy-start.1 = (bf16[1,1,1,1,128,1024]{5,4,3,2,1,0:T(8,128)(2,1)S(1)}, bf16[1,1,1,1,128,1024]{5,4,3,2,1,0:T(8,128)(2,1)}, u32[]{:S(2)}) copy-start(bf16[1,1,1,1,128,1024]{5,4,3,2,1,0:T(8,128)(2,1)} %param.8) | copy-start | bytes 786436
  13.2 11.6 %collective-permute-start.4 = (f32[256,1024]{1,0:T(8,128)S(1)}, f32[256,1024]{1,0:T(8,128)}, u32[]{:S(2)}, u32[]{:S(2)}) collective-permute-start(f32[256,1024]{1,0:T(8,128)S(1)} %pad_maximum_fusion), channel_id=1, source_target_pairs={{80,84},{97,101},{114,118},{131,135},{144,152},{161,169},{178,186}... | collective-permute-start | bytes 3145736 | tf_op jit(solution)/shard_map/ppermute | solution.py:65
  16.6 6.9 %collective-permute-start.5 = (f32[256,768]{1,0:T(8,128)S(1)}, f32[256,768]{1,0:T(8,128)}, u32[]{:S(2)}, u32[]{:S(2)}) collective-permute-start(f32[256,768]{1,0:T(8,128)S(1)} %slice.22), channel_id=1, source_target_pairs={{4,0},{20,16},{37,33},{54,50},{71,67},{148,152},{165,169},{182,186... | collective-permute-start | bytes 2359304 | tf_op jit(solution)/shard_map/ppermute | solution.py:65
  18.2 4.2 %collective-permute-start.6 = (f32[256,512]{1,0:T(8,128)}, f32[256,512]{1,0:T(8,128)}, u32[]{:S(2)}, u32[]{:S(2)}) collective-permute-start(f32[256,512]{1,0:T(8,128)} %slice.23), channel_id=1, source_target_pairs={{8,0},{24,16},{41,33},{58,50},{75,67},{88,84},{105,101},{122,118},... | collective-permute-start | bytes 1572872 | tf_op jit(solution)/shard_map/ppermute | solution.py:65
  19.6 1.7 collective-permute-start.7
  26.2 0.7 copy-start.2
  27.4 26.6 %collective-permute-start.10 = (f32[4,1024]{1,0:T(4,128)S(1)}, f32[4,1024]{1,0:T(4,128)S(1)}, u32[]{:S(2)}, u32[]{:S(2)}) collective-permute-start(f32[4,1024]{1,0:T(4,128)S(1)} %get-tuple-element.37), channel_id=1, source_target_pairs={{0,16},{135,152}} | collective-permute-start | bytes 49160 | tf_op jit(solution)/shard_map/ppermute | solution.py:65
  28.0 25.9 %collective-permute-start.8 = (f32[4,1024]{1,0:T(4,128)S(1)}, f32[4,1024]{1,0:T(4,128)S(1)}, u32[]{:S(2)}, u32[]{:S(2)}) collective-permute-start(f32[4,1024]{1,0:T(4,128)S(1)} %get-tuple-element.36), channel_id=1, source_target_pairs={{0,32},{50,243},{67,196},{84,165},{100,212},{101,150},{117,181},{1... | collective-permute-start | bytes 49160 | tf_op jit(solution)/shard_map/ppermute | solution.py:65
  28.7 26.6 %collective-permute-start.9 = (f32[4,1024]{1,0:T(4,128)S(1)}, f32[4,1024]{1,0:T(4,128)S(1)}, u32[]{:S(2)}, u32[]{:S(2)}) collective-permute-start(f32[4,1024]{1,0:T(4,128)S(1)} %fusion.39), channel_id=1, source_target_pairs={{134,135},{149,152},{164,169},{179,186},{194,203},{209,220},{224,2... | collective-permute-start | bytes 49160 | tf_op jit(solution)/shard_map/ppermute | solution.py:65
  55.7 2.0 collective-permute-start.11
  56.3 1.4 collective-permute-start.13
  57.0 0.7 collective-permute-start.12
  58.5 2.0 collective-permute-start.14
  59.2 1.4 collective-permute-start.16
  59.9 0.7 collective-permute-start.15
  61.4 2.0 collective-permute-start.17
  62.1 1.4 collective-permute-start.19
  62.7 0.7 collective-permute-start.18
  64.3 13.3 %collective-permute-start.20 = (f32[4,1024]{1,0:T(4,128)S(1)}, f32[4,1024]{1,0:T(4,128)S(1)}, u32[]{:S(2)}, u32[]{:S(2)}) collective-permute-start(f32[4,1024]{1,0:T(4,128)S(1)} %get-tuple-element.44), channel_id=1, source_target_pairs={{0,192},{16,145},{32,208},{33,114},{49,161},{50,99},{64,224},{66,1... | collective-permute-start | bytes 49160 | tf_op jit(solution)/shard_map/ppermute | solution.py:65
  65.5 12.0 %collective-permute-start.22 = (f32[4,1024]{1,0:T(4,128)S(1)}, f32[4,1024]{1,0:T(4,128)S(1)}, u32[]{:S(2)}, u32[]{:S(2)}) collective-permute-start(f32[4,1024]{1,0:T(4,128)S(1)} %get-tuple-element.45), channel_id=1, source_target_pairs={{67,84},{203,220}} | collective-permute-start | bytes 49160 | tf_op jit(solution)/shard_map/ppermute | solution.py:65
  66.2 11.4 %collective-permute-start.21 = (f32[4,1024]{1,0:T(4,128)S(1)}, f32[4,1024]{1,0:T(4,128)S(1)}, u32[]{:S(2)}, u32[]{:S(2)}) collective-permute-start(f32[4,1024]{1,0:T(4,128)S(1)} %fusion.35), channel_id=1, source_target_pairs={{83,84},{98,101},{113,118},{128,135},{202,203},{217,220},{232,237}... | collective-permute-start | bytes 49160 | tf_op jit(solution)/shard_map/ppermute | solution.py:65
  78.4 2.0 collective-permute-start.23
  79.0 1.4 collective-permute-start.25
  79.7 0.7 collective-permute-start.24
  81.2 2.0 collective-permute-start.26
  81.9 1.4 collective-permute-start.28
  82.6 0.7 collective-permute-start.27
  84.1 40.6 %collective-permute-start.29 = (f32[4,1024]{1,0:T(4,128)S(1)}, f32[4,1024]{1,0:T(4,128)S(1)}, u32[]{:S(2)}, u32[]{:S(2)}) collective-permute-start(f32[4,1024]{1,0:T(4,128)S(1)} %get-tuple-element.50), channel_id=1, source_target_pairs={{0,32},{50,243},{67,196},{84,165},{100,212},{101,150},{117,181},{1... | collective-permute-start | bytes 49160 | tf_op jit(solution)/shard_map/ppermute | solution.py:65
  84.8 39.9 %collective-permute-start.31 = (f32[4,1024]{1,0:T(4,128)S(1)}, f32[4,1024]{1,0:T(4,128)S(1)}, u32[]{:S(2)}, u32[]{:S(2)}) collective-permute-start(f32[4,1024]{1,0:T(4,128)S(1)} %get-tuple-element.51), channel_id=1, source_target_pairs={{118,135}} | collective-permute-start | bytes 49160 | tf_op jit(solution)/shard_map/ppermute | solution.py:65
  85.4 40.6 %collective-permute-start.30 = (f32[4,1024]{1,0:T(4,128)S(1)}, f32[4,1024]{1,0:T(4,128)S(1)}, u32[]{:S(2)}, u32[]{:S(2)}) collective-permute-start(f32[4,1024]{1,0:T(4,128)S(1)} %fusion.32), channel_id=1, source_target_pairs={{134,135},{149,152},{164,169},{179,186},{194,203},{209,220},{224,2... | collective-permute-start | bytes 49160 | tf_op jit(solution)/shard_map/ppermute | solution.py:65
  126.8 2.0 collective-permute-start.32
  127.5 1.4 collective-permute-start.34
  128.2 0.7 collective-permute-start.33
  129.7 2.0 collective-permute-start.35
  130.4 1.4 collective-permute-start.37
  131.0 0.7 collective-permute-start.36
  132.6 2.0 collective-permute-start.38
  133.2 1.4 collective-permute-start.40
  133.9 0.7 collective-permute-start.39
  135.4 8.6 %collective-permute-start.41 = (f32[4,1024]{1,0:T(4,128)S(1)}, f32[4,1024]{1,0:T(4,128)S(1)}, u32[]{:S(2)}, u32[]{:S(2)}) collective-permute-start(f32[4,1024]{1,0:T(4,128)S(1)} %get-tuple-element.58), channel_id=1, source_target_pairs={{0,192},{16,145},{32,208},{33,114},{49,161},{50,99},{64,224},{66,1... | collective-permute-start | bytes 49160 | tf_op jit(solution)/shard_map/ppermute | solution.py:65
  136.7 7.3 %collective-permute-start.43 = (f32[4,1024]{1,0:T(4,128)S(1)}, f32[4,1024]{1,0:T(4,128)S(1)}, u32[]{:S(2)}, u32[]{:S(2)}) collective-permute-start(f32[4,1024]{1,0:T(4,128)S(1)} %get-tuple-element.59), channel_id=1, source_target_pairs={{50,67},{186,203}} | collective-permute-start | bytes 49160 | tf_op jit(solution)/shard_map/ppermute | solution.py:65
  137.4 6.7 %collective-permute-start.42 = (f32[4,1024]{1,0:T(4,128)S(1)}, f32[4,1024]{1,0:T(4,128)S(1)}, u32[]{:S(2)}, u32[]{:S(2)}) collective-permute-start(f32[4,1024]{1,0:T(4,128)S(1)} %fusion.28), channel_id=1, source_target_pairs={{83,84},{98,101},{113,118},{128,135},{202,203},{217,220},{232,237}... | collective-permute-start | bytes 49160 | tf_op jit(solution)/shard_map/ppermute | solution.py:65
  144.5 3.2 %collective-permute-start.45 = (f32[4,1024]{1,0:T(4,128)S(1)}, f32[4,1024]{1,0:T(4,128)S(1)}, u32[]{:S(2)}, u32[]{:S(2)}) collective-permute-start(f32[4,1024]{1,0:T(4,128)S(1)} %fusion.27), channel_id=1, source_target_pairs={{100,101},{115,118},{130,135},{145,152},{160,169},{219,220},{234,2... | collective-permute-start | bytes 49160 | tf_op jit(solution)/shard_map/ppermute | solution.py:65
  145.5 2.2 %collective-permute-start.44 = (f32[4,1024]{1,0:T(4,128)S(1)}, f32[4,1024]{1,0:T(4,128)S(1)}, u32[]{:S(2)}, u32[]{:S(2)}) collective-permute-start(f32[4,1024]{1,0:T(4,128)S(1)} %get-tuple-element.60), channel_id=1, source_target_pairs={{16,209},{33,162},{49,225},{50,131},{66,178},{67,116},{81,241},{83... | collective-permute-start | bytes 49160 | tf_op jit(solution)/shard_map/ppermute | solution.py:65
  146.2 1.5 collective-permute-start.46
  148.1 3.3 %collective-permute-start.48 = (f32[4,1024]{1,0:T(4,128)S(1)}, f32[4,1024]{1,0:T(4,128)S(1)}, u32[]{:S(2)}, u32[]{:S(2)}) collective-permute-start(f32[4,1024]{1,0:T(4,128)S(1)} %fusion.26), channel_id=1, source_target_pairs={{117,118},{132,135},{147,152},{162,169},{177,186},{192,203},{236,2... | collective-permute-start | bytes 49160 | tf_op jit(solution)/shard_map/ppermute | solution.py:65
  149.2 2.2 %collective-permute-start.47 = (f32[4,1024]{1,0:T(4,128)S(1)}, f32[4,1024]{1,0:T(4,128)S(1)}, u32[]{:S(2)}, u32[]{:S(2)}) collective-permute-start(f32[4,1024]{1,0:T(4,128)S(1)} %get-tuple-element.62), channel_id=1, source_target_pairs={{33,226},{50,179},{66,242},{67,148},{83,195},{84,133},{100,164},{1... | collective-permute-start | bytes 49160 | tf_op jit(solution)/shard_map/ppermute | solution.py:65
  149.8 1.5 collective-permute-start.49
  151.8 43.5 %collective-permute-start.51 = (f32[4,1024]{1,0:T(4,128)S(1)}, f32[4,1024]{1,0:T(4,128)S(1)}, u32[]{:S(2)}, u32[]{:S(2)}) collective-permute-start(f32[4,1024]{1,0:T(4,128)S(1)} %fusion.25), channel_id=1, source_target_pairs={{134,135},{149,152},{164,169},{179,186},{194,203},{209,220},{224,2... | collective-permute-start | bytes 49160 | tf_op jit(solution)/shard_map/ppermute | solution.py:65
  193.4 1.9 collective-permute-start.50
  194.0 1.3 collective-permute-start.52
  197.5 13.5 %all-to-all-start = ((f32[16,4,1152]{2,1,0:T(4,128)}), f32[16,4,1152]{2,1,0:T(4,128)S(1)}, u32[]{:S(2)}, u32[]{:S(2)}) async-start(f32[16,4,1152]{2,1,0:T(4,128)} %broadcast_in_dim.179), calls=%async_computation | async-start | bytes 589824 | tf_op jit(solution)/shard_map/all_to_all | solution.py:131

commit v2 on v1

v2 whole, which is shorter than its diff:
```python
import math

import jax
import jax.numpy as jnp
from jax import lax
from jax.experimental import pallas as pl
from jax.experimental.pallas import tpu as pltpu
from jax.sharding import PartitionSpec as P


ROW = "row"
COL = "col"
BOTH = (ROW, COL)
SIDE = 4
BAND = 2
PERIOD = 7
SPREAD_PERIOD = 5
ARRIVAL = {3: 0, 4: 1, 5: 1, 6: 2, 7: 2, 8: 2, 9: 2, 10: 3, 11: 3, 12: 3, 13: 3, 14: 3, 15: 3}
SENDER = {3: 1, 4: 1, 5: 3, 6: 1, 7: 3, 8: 4, 9: 5, 10: 1, 11: 3, 12: 4, 13: 5, 14: 6, 15: 7}


def solver(i):
    return (i, i - 1 if i else 1)


def union(rounds, period):
    patterns = []
    for first in range(min(period, len(rounds))):
        pairs = sorted({pair for moves in rounds[first::period] for pair in moves})
        assert len({s for s, _ in pairs}) == len(pairs) == len({d for _, d in pairs})
        patterns.append(pairs)
    return [patterns[r % period] for r in range(len(rounds))]


def plan(n):
    chain, spread, odd, even = [], [], [], []
    for r in range(n - 1):
        chain.append([(solver(r), solver(r + 1))])
        spread.append([])
        odd.append([])
        even.append([])
        for i in range(n):
            for j in range(i - BAND):
                d = i - j
                if j + ARRIVAL[d] == r:
                    spread[r].append((solver(j) if SENDER[d] == 1 else (j + SENDER[d], j), (i, j)))
                if i - 2 - (d - 3) // 2 == r:
                    (odd if d % 2 else even)[r].append(((i, j), solver(i)))
    return union(chain, PERIOD), union(spread, SPREAD_PERIOD), union(odd, PERIOD), union(even, PERIOD)


def assemble(place, block, parts):
    quarter, width = block.shape

    def body(place_ref, block_ref, *refs):
        out = refs[-1]
        for k in range(SIDE):
            start = k * quarter
            got = refs[k][...] + jnp.where(place_ref[0] == k, block_ref[:, start:], 0.0)
            if start:
                out[start : start + quarter, :start] = jnp.zeros((quarter, start), jnp.bfloat16)
            out[start : start + quarter, start:] = got.astype(jnp.bfloat16)

    vmem = pl.BlockSpec(memory_space=pltpu.VMEM)
    return pl.pallas_call(
        body,
        in_specs=[pl.BlockSpec(memory_space=pltpu.SMEM)] + [vmem] * (1 + SIDE),
        out_specs=vmem,
        out_shape=jax.ShapeDtypeStruct((width, width), jnp.bfloat16),
        compiler_params=pltpu.CompilerParams(vmem_limit_bytes=16 * 2**20),
        name="assemble",
    )(place, block, *parts)


def step(r, where, came, heard, odds, evens, state, source, v_band, u_band, inverse):
    held = max(1, min(BAND, r + 1))
    nrhs, width = source.shape
    block = 256

    def body(round_ref, where_ref, came_ref, heard_ref, odds_ref, evens_ref, state_ref, source_ref, *refs):
        v_refs, u_refs = refs[:held], refs[held : 2 * held]
        inverse_ref, bundle_ref, spread_ref, own_ref, after_ref = refs[2 * held :]
        now = round_ref[0]
        row, col, arrival = where_ref[0], where_ref[1], where_ref[2]
        gap = row - col
        solves = (gap == 1) | ((row == 0) & (col == 1))
        takes = (gap == 1) & (col == now)
        hears = (gap > BAND) & (col + arrival == now)
        behind = row - 1 - now
        adds = (gap == 1) & (behind >= 0) & (now >= 1)
        adds_odd = adds & (3 + 2 * behind <= row)
        adds_even = adds & (4 + 2 * behind <= row)
        ys = []
        for d in range(BAND):
            y = state_ref[d] + jnp.where(takes, came_ref[d], 0.0)
            if d == 0:
                y = y + jnp.where(hears, heard_ref[...], 0.0)
            ys.append(y)
            after_ref[d] = y
        pending = state_ref[BAND] + jnp.where(adds_odd, odds_ref[...], 0.0) + jnp.where(adds_even, evens_ref[...], 0.0)
        after_ref[BAND] = pending
        total = source_ref[...] - pending
        inners = [
            lax.dot_general(ys[d].astype(jnp.bfloat16), v_refs[d][...], (((1,), (1,)), ((), ())), preferred_element_type=jnp.float32)
            for d in range(held)
        ]
        for d in range(held):
            part = jnp.dot(inners[d].astype(jnp.bfloat16), u_refs[d][...], preferred_element_type=jnp.float32)
            if d == 0:
                own_ref[...] = part
            total = total - part
        reduced = total.astype(jnp.bfloat16)
        columns = []
        for n in range(0, width, block):
            columns.append(
                jnp.dot(reduced[:, : n + block], inverse_ref[: n + block, n : n + block], preferred_element_type=jnp.float32)
            )
        result = jnp.concatenate(columns, axis=1)
        bundle_ref[0] = result
        for d in range(BAND - 1):
            bundle_ref[d + 1] = ys[d]
        spread_ref[...] = jnp.where(solves, result, ys[0])

    vmem = pl.BlockSpec(memory_space=pltpu.VMEM)
    smem = pl.BlockSpec(memory_space=pltpu.SMEM)
    small = jax.ShapeDtypeStruct((nrhs, width), jnp.float32)
    return pl.pallas_call(
        body,
        in_specs=[smem, smem] + [vmem] * (6 + 2 * held + 1),
        out_specs=[vmem] * 4,
        out_shape=[
            jax.ShapeDtypeStruct((BAND, nrhs, width), jnp.float32),
            small,
            small,
            jax.ShapeDtypeStruct((BAND + 1, nrhs, width), jnp.float32),
        ],
        compiler_params=pltpu.CompilerParams(vmem_limit_bytes=8 * 2**20),
        name="step",
    )(jnp.full((1,), r, jnp.int32), where, came, heard, odds, evens, state, source, *v_band[:held], *u_band[:held], inverse)


def local(right_side, inverse_t, u_factor, v_factor, ranks):
    n = lax.axis_size(ROW)
    n_col = lax.axis_size(COL)
    nrhs, width = right_side.shape[2:]
    piece = width // n_col
    rank_max = u_factor.shape[4]
    row = lax.axis_index(ROW)
    col = lax.axis_index(COL)
    gap = row - col
    source = right_side.reshape(nrhs, width)
    u_tile = u_factor.reshape(rank_max, width)
    v_tile = v_factor.reshape(rank_max, width)
    keep = jnp.arange(rank_max, dtype=jnp.int32)[:, None] < ranks.reshape(1, 1)
    u_tile = jnp.where(keep, u_tile, jnp.zeros_like(u_tile))

    def move(array, pairs):
        numbered = [(s[0] * n_col + s[1], d[0] * n_col + d[1]) for s, d in pairs]
        return lax.ppermute(array, BOTH, numbered)

    rows = inverse_t.reshape(piece, width).astype(jnp.float32)
    quarter = width // SIDE
    slabs = []
    for k in range(SIDE):
        pairs = [
            ((r, x * SIDE + k), (r, x * SIDE + solver(r)[1] % SIDE))
            for r in range(n)
            for x in range(SIDE)
            if solver(r)[1] % SIDE != k
        ]
        slabs.append(move(rows, pairs) + jnp.where(col % SIDE == k, rows, 0.0))
    square = lax.dynamic_slice_in_dim(rows, col * piece, piece, 1)
    log_sum = jnp.sum(jnp.log(jnp.diagonal(square)))
    both = jnp.concatenate([v_tile, u_tile], axis=0).astype(jnp.float32)
    block, both, log_sum = lax.optimization_barrier((jnp.concatenate(slabs, axis=0), both, log_sum))
    parts = []
    for k in range(SIDE):
        pairs = [
            ((r, k * SIDE + solver(r)[1] % SIDE), solver(r)) for r in range(n) if solver(r)[1] // SIDE != k
        ]
        parts.append(move(block[:, k * quarter :], pairs))
    place = jnp.stack([col // SIDE]).astype(jnp.int32)

    second = move(both, [((i, i - 2), solver(i)) for i in range(2, n)])
    inverse = assemble(place, block, parts)
    second = (second + jnp.where(gap == 1, 0.0, both)).astype(jnp.bfloat16)
    v_band = [v_tile, second[:rank_max]]
    u_band = [u_tile, second[rank_max:]]

    arrival = jnp.full((), 99, jnp.int32)
    for d, when in ARRIVAL.items():
        arrival = jnp.where(gap == d, when, arrival)
    chain, spread, odd, even = plan(n)
    where = jnp.stack([row, col, arrival]).astype(jnp.int32)
    nothing = jnp.zeros((nrhs, width), jnp.float32)
    state = jnp.zeros((BAND + 1, nrhs, width), jnp.float32)
    no_bundle = jnp.zeros((BAND, nrhs, width), jnp.float32)
    bundle, spread_out, own, state = step(
        -1, where, no_bundle, nothing, nothing, nothing, state, source, v_band, u_band, inverse
    )
    odds = evens = nothing
    for r in range(n - 1):
        came = move(bundle, chain[r])
        heard = more_odds = more_evens = nothing
        if spread[r]:
            heard = move(spread_out, spread[r])
        if 1 <= r < n - 2:
            more_odds = move(own, odd[r])
        if 2 <= r < n - 2:
            more_evens = move(own, even[r])
        bundle, spread_out, own, state = step(
            r, where, came, heard, odds, evens, state, source, v_band, u_band, inverse
        )
        odds, evens = more_odds, more_evens
    result = bundle[0]

    payload = jnp.concatenate([result, jnp.broadcast_to(log_sum, (nrhs, 128))], axis=1)
    payload = jnp.broadcast_to(payload[None], (n_col, *payload.shape))
    arrived = lax.all_to_all(payload, COL, 0, 0, tiled=True)
    solved = lax.dynamic_index_in_dim(arrived, jnp.where(row == 0, 1, row - 1), 0, False)[:, :width]
    logdiag = jnp.sum(arrived[:, 0, width]) / width
    quadratic = jnp.mean(solved * solved, axis=1)
    loglik = -0.5 * quadratic + logdiag - 0.5 * math.log(2.0 * math.pi)
    return solved.reshape(1, 1, nrhs, width), loglik.reshape(1, 1, nrhs)


def solution(mesh):
    return jax.shard_map(
        local,
        mesh=mesh,
        in_specs=(
            P(None, ROW, None, None),
            P(None, ROW, COL, None),
            P(None, ROW, None, COL, None, None),
            P(None, ROW, None, COL, None, None),
            P(None, ROW, None, COL),
        ),
        out_specs=(P(None, ROW, None, None), P(None, ROW, None)),
        check_vma=False,
    )
```

time: 215 us -> 206 us (0.958)
  the two profiles are of different devices: /device:TPU:224 before, /device:TPU:1 now
where the time goes in v2:
time: 206 us; the launch traced here: 204 us
  starting transfers between devices  131 us (64%)
  waiting for transfers between devices  35.3 us (17%)
  Pallas kernels  22.1 us (11%)
  other arithmetic  8.31 us (4%)
  local copies, waits for them, and re-layouts  4.98 us (2%)
  between operations  2.96 us (1%)
    ppermute x64, starting transfers between devices, move(): return lax.ppermute(array, BOTH, numbered)  127 us
    ppermute x64, waiting for transfers between devices, move(): return lax.ppermute(array, BOTH, numbered)  27.9 us
    pallas_call x16, Pallas kernels, step(): pl.pallas_call(body, in_specs=[smem, smem] + [vmem] * (6 + 2 * held + 1),...  20.7 us
    all_to_all x1, waiting for transfers between devices, local(): arrived = lax.all_to_all(payload, COL, 0, 0, tiled=True)  7.45 us
  transfers between devices with their start and end apart: 65, of which 18 were waited for; matrix products, arithmetic and copies ran while one was open for 4% of the time, Pallas kernels for 1%

profile of v2, /device:TPU:1, one launch (start us, length us, event | category | flops | bytes accessed | tf_op | source)
XLA Modules:
  0.0 204.3 jit_solution(2536536921412932539)
XLA Ops:
  0.6 1.0 fusion.1
  2.3 1.3 collective-permute-start.1
  3.6 1.3 collective-permute-start.2
  4.9 1.3 collective-permute-start.3
  6.9 1.0 bitcast_select_fusion.refs_1_.refs_2_
  8.1 0.8 gather_fusion
  9.6 2.1 %maximum_convert_fusion = f32[256,1024]{1,0:T(8,128)} fusion(bf16[128,1024]{1,0:T(8,128)(2,1)S(1)} %bitcast_select_fusion.refs_1_.refs_2_, bf16[128,1024]{1,0:T(8,128)(2,1)} %bitcast.32), kind=kLoop, calls=%fused_computation.3 | loop fusion | flops 1048576 | bytes 1572864 | tf_op jit(solution)/shard_map/convert_element_type | solution.py:174
  12.4 2.7 %collective-permute-done.3 = f32[64,1024]{1,0:T(8,128)S(1)} collective-permute-done((f32[64,1024]{1,0:T(8,128)S(1)}, f32[64,1024]{1,0:T(8,128)S(1)}, u32[]{:S(2)}, u32[]{:S(2)}) %collective-permute-start.3) | collective-permute-done | bytes 262176 | tf_op jit(solution)/shard_map/ppermute | solution.py:159
  16.0 1.6 collective-permute-start.12
  17.6 1.0 slice.24
  18.6 1.3 collective-permute-start.5
  19.9 0.9 slice.25
  20.7 1.3 collective-permute-start.6
  22.8 1.3 collective-permute-start.7
  24.2 11.0 %collective-permute-done.7.refs_3_ = f32[256,256]{1,0:T(8,128)S(1)} collective-permute-done((f32[256,256]{1,0:T(8,128)}, f32[256,256]{1,0:T(8,128)S(1)}, u32[]{:S(2)}, u32[]{:S(2)}) %collective-permute-start.7) | collective-permute-done | bytes 262176 | tf_op jit(solution)/shard_map/ppermute | solution.py:159
  35.2 1.4 assemble.1.refs_2_.refs_4_
  36.7 1.6 step.16
  38.3 1.3 collective-permute-start.8
  40.2 1.4 add_convert_fusion
  41.7 2.9 %collective-permute-done.8.came_ref = f32[2,4,1024]{2,1,0:T(4,128)S(1)} collective-permute-done((f32[2,4,1024]{2,1,0:T(4,128)S(1)}, f32[2,4,1024]{2,1,0:T(4,128)S(1)}, u32[]{:S(2)}, u32[]{:S(2)}) %collective-permute-start.8) | collective-permute-done | bytes 32800 | tf_op jit(solution)/shard_map/ppermute | solution.py:159
  44.6 1.2 step.17
  45.8 4.7 %collective-permute-start.10 = (f32[2,4,1024]{2,1,0:T(4,128)S(1)}, f32[2,4,1024]{2,1,0:T(4,128)S(1)}, u32[]{:S(2)}, u32[]{:S(2)}) collective-permute-start(f32[2,4,1024]{2,1,0:T(4,128)S(1)} %get-tuple-element.68), channel_id=1, source_target_pairs={{16,33},{135,152}} | collective-permute-start | bytes 98312 | tf_op jit(solution)/shard_map/ppermute | solution.py:159
  50.5 1.3 collective-permute-start.11
  52.6 1.2 step.18
  55.2 1.3 collective-permute-start.14
  56.5 0.8 collective-permute-done.14.heard_ref
  57.3 1.2 step.19
  60.6 1.3 collective-permute-start.17
  61.9 0.8 collective-permute-done.17.heard_ref
  62.7 1.2 step.20
  65.9 1.3 collective-permute-start.21
  67.3 0.8 collective-permute-done.21.heard_ref
  68.1 1.2 step.21
  72.0 1.2 step.22
  75.3 8.3 %collective-permute-start.29 = (f32[4,1024]{1,0:T(4,128)S(1)}, f32[4,1024]{1,0:T(4,128)S(1)}, u32[]{:S(2)}, u32[]{:S(2)}) collective-permute-start(f32[4,1024]{1,0:T(4,128)S(1)} %get-tuple-element.89), channel_id=1, source_target_pairs={{1,64},{16,65},{48,80},{50,211},{67,164},{84,149},{99,227},{101,15... | collective-permute-start | bytes 49160 | tf_op jit(solution)/shard_map/ppermute | solution.py:159
  83.7 0.8 collective-permute-done.29.heard_ref
  84.5 1.2 step.23
  85.7 1.3 collective-permute-start.32
  88.4 1.3 collective-permute-start.33
  89.7 0.8 collective-permute-done.33.heard_ref
  90.9 1.2 step.24
  92.2 2.4 %collective-permute-start.36 = (f32[2,4,1024]{2,1,0:T(4,128)S(1)}, f32[2,4,1024]{2,1,0:T(4,128)S(1)}, u32[]{:S(2)}, u32[]{:S(2)}) collective-permute-start(f32[2,4,1024]{2,1,0:T(4,128)S(1)} %get-tuple-element.96), channel_id=1, source_target_pairs={{16,33},{135,152}} | collective-permute-start | bytes 98312 | tf_op jit(solution)/shard_map/ppermute | solution.py:159
  95.9 16.1 %collective-permute-start.37 = (f32[4,1024]{1,0:T(4,128)S(1)}, f32[4,1024]{1,0:T(4,128)S(1)}, u32[]{:S(2)}, u32[]{:S(2)}) collective-permute-start(f32[4,1024]{1,0:T(4,128)S(1)} %get-tuple-element.97), channel_id=1, source_target_pairs={{1,160},{16,113},{33,98},{48,176},{50,99},{64,192},{65,129},{80,20... | collective-permute-start | bytes 49160 | tf_op jit(solution)/shard_map/ppermute | solution.py:159
  112.0 0.8 collective-permute-done.37.heard_ref
  112.8 1.2 step.25
  116.1 18.3 %collective-permute-start.41 = (f32[4,1024]{1,0:T(4,128)S(1)}, f32[4,1024]{1,0:T(4,128)S(1)}, u32[]{:S(2)}, u32[]{:S(2)}) collective-permute-start(f32[4,1024]{1,0:T(4,128)S(1)} %get-tuple-element.101), channel_id=1, source_target_pairs={{16,177},{33,130},{50,115},{65,193},{67,116},{81,209},{82,146},{97... | collective-permute-start | bytes 49160 | tf_op jit(solution)/shard_map/ppermute | solution.py:159
  134.4 0.8 collective-permute-done.41.heard_ref
  135.2 1.2 step.26
  139.2 1.2 step.27
  142.4 1.3 collective-permute-start.49
  143.7 0.8 collective-permute-done.49.heard_ref
  144.6 1.2 step.28
  147.8 7.9 %collective-permute-start.53 = (f32[4,1024]{1,0:T(4,128)S(1)}, f32[4,1024]{1,0:T(4,128)S(1)}, u32[]{:S(2)}, u32[]{:S(2)}) collective-permute-start(f32[4,1024]{1,0:T(4,128)S(1)} %get-tuple-element.113), channel_id=1, source_target_pairs={{1,96},{16,81},{33,82},{48,112},{64,128},{65,97},{67,228},{80,144}... | collective-permute-start | bytes 49160 | tf_op jit(solution)/shard_map/ppermute | solution.py:159
  155.7 0.8 collective-permute-done.53.heard_ref
  156.5 1.2 step.29
  159.8 2.2 %collective-permute-start.57 = (f32[4,1024]{1,0:T(4,128)S(1)}, f32[4,1024]{1,0:T(4,128)S(1)}, u32[]{:S(2)}, u32[]{:S(2)}) collective-permute-start(f32[4,1024]{1,0:T(4,128)S(1)} %get-tuple-element.117), channel_id=1, source_target_pairs={{1,160},{16,113},{33,98},{48,176},{50,99},{64,192},{65,129},{80,20... | collective-permute-start | bytes 49160 | tf_op jit(solution)/shard_map/ppermute | solution.py:159
  162.0 0.8 collective-permute-done.57.heard_ref
  162.9 1.5 step.30
  164.4 1.3 collective-permute-start.60
  167.0 19.6 %collective-permute-start.61 = (f32[4,1024]{1,0:T(4,128)S(1)}, f32[4,1024]{1,0:T(4,128)S(1)}, u32[]{:S(2)}, u32[]{:S(2)}) collective-permute-start(f32[4,1024]{1,0:T(4,128)S(1)} %get-tuple-element.121), channel_id=1, source_target_pairs={{16,177},{33,130},{50,115},{65,193},{67,116},{81,209},{82,146},{97... | collective-permute-start | bytes 49160 | tf_op jit(solution)/shard_map/ppermute | solution.py:159
  186.6 0.8 collective-permute-done.61.heard_ref
  187.5 1.8 step.31
  190.8 3.5 %all-to-all-start = ((f32[16,4,1152]{2,1,0:T(4,128)}), f32[16,4,1152]{2,1,0:T(4,128)S(1)}, u32[]{:S(2)}, u32[]{:S(2)}) async-start(f32[16,4,1152]{2,1,0:T(4,128)} %broadcast_in_dim.50), calls=%async_computation | async-start | bytes 589824 | tf_op jit(solution)/shard_map/all_to_all | solution.py:219
  194.3 7.5 %all-to-all-done = f32[16,4,1152]{2,1,0:T(4,128)S(1)} async-done(((f32[16,4,1152]{2,1,0:T(4,128)}), f32[16,4,1152]{2,1,0:T(4,128)S(1)}, u32[]{:S(2)}, u32[]{:S(2)}) %all-to-all-start) | async-done | bytes 294944 | tf_op jit(solution)/shard_map/all_to_all | solution.py:219
  (115 shorter events, 33.9 us)
Async XLA Ops:
  1.7 9.9 %collective-permute-start = (f32[64,1024]{1,0:T(8,128)S(1)}, f32[64,1024]{1,0:T(8,128)S(1)}, u32[]{:S(2)}, u32[]{:S(2)}) collective-permute-start(f32[64,1024]{1,0:T(8,128)S(1)} %get-tuple-element.129), channel_id=1, source_target_pairs={{0,1},{4,5},{8,9},{12,13},{32,33},{36,37},{40,41},{44,45},{48,50},... | collective-permute-start | bytes 786440 | tf_op jit(solution)/shard_map/ppermute | solution.py:159
  2.3 9.3 %collective-permute-start.1 = (f32[64,1024]{1,0:T(8,128)S(1)}, f32[64,1024]{1,0:T(8,128)S(1)}, u32[]{:S(2)}, u32[]{:S(2)}) collective-permute-start(f32[64,1024]{1,0:T(8,128)S(1)} %get-tuple-element.129), channel_id=1, source_target_pairs={{17,16},{21,20},{25,24},{29,28},{49,50},{53,54},{57,58},{61,62},{6... | collective-permute-start | bytes 786440 | tf_op jit(solution)/shard_map/ppermute | solution.py:159
  3.6 8.7 %collective-permute-start.2 = (f32[64,1024]{1,0:T(8,128)S(1)}, f32[64,1024]{1,0:T(8,128)S(1)}, u32[]{:S(2)}, u32[]{:S(2)}) collective-permute-start(f32[64,1024]{1,0:T(8,128)S(1)} %get-tuple-element.129), channel_id=1, source_target_pairs={{2,1},{6,5},{10,9},{14,13},{18,16},{22,20},{26,24},{30,28},{34,33}... | collective-permute-start | bytes 786440 | tf_op jit(solution)/shard_map/ppermute | solution.py:159
  4.9 10.1 %collective-permute-start.3 = (f32[64,1024]{1,0:T(8,128)S(1)}, f32[64,1024]{1,0:T(8,128)S(1)}, u32[]{:S(2)}, u32[]{:S(2)}) collective-permute-start(f32[64,1024]{1,0:T(8,128)S(1)} %get-tuple-element.129), channel_id=1, source_target_pairs={{3,1},{7,5},{11,9},{15,13},{19,16},{23,20},{27,24},{31,28},{35,33}... | collective-permute-start | bytes 786440 | tf_op jit(solution)/shard_map/ppermute | solution.py:159
  15.3 19.9 %collective-permute-start.4 = (f32[256,1024]{1,0:T(8,128)S(1)}, f32[256,1024]{1,0:T(8,128)S(1)}, u32[]{:S(2)}, u32[]{:S(2)}) collective-permute-start(f32[256,1024]{1,0:T(8,128)S(1)} %pad_maximum_fusion.block_ref), channel_id=1, source_target_pairs={{80,84},{97,101},{114,118},{131,135},{144,152},{161,169},{178,186}... | collective-permute-start | bytes 3145736 | tf_op jit(solution)/shard_map/ppermute | solution.py:159
  16.0 24.2 %collective-permute-start.12 = (f32[256,1024]{1,0:T(8,128)}, f32[256,1024]{1,0:T(8,128)}, u32[]{:S(2)}, u32[]{:S(2)}) collective-permute-start(f32[256,1024]{1,0:T(8,128)} %maximum_convert_fusion), channel_id=1, source_target_pairs={{32,33},{49,50},{66,67},{83,84},{100,101},{117,118},{134,135},{151... | collective-permute-start | bytes 3145736 | tf_op jit(solution)/shard_map/ppermute | solution.py:159
  18.6 16.6 %collective-permute-start.5 = (f32[256,768]{1,0:T(8,128)}, f32[256,768]{1,0:T(8,128)S(1)}, u32[]{:S(2)}, u32[]{:S(2)}) collective-permute-start(f32[256,768]{1,0:T(8,128)} %slice.24), channel_id=1, source_target_pairs={{5,1},{20,16},{37,33},{54,50},{71,67},{148,152},{165,169},{182,186... | collective-permute-start | bytes 2359304 | tf_op jit(solution)/shard_map/ppermute | solution.py:159
  20.7 14.4 %collective-permute-start.6 = (f32[256,512]{1,0:T(8,128)}, f32[256,512]{1,0:T(8,128)}, u32[]{:S(2)}, u32[]{:S(2)}) collective-permute-start(f32[256,512]{1,0:T(8,128)} %slice.25), channel_id=1, source_target_pairs={{9,1},{24,16},{41,33},{58,50},{75,67},{88,84},{105,101},{122,118},... | collective-permute-start | bytes 1572872 | tf_op jit(solution)/shard_map/ppermute | solution.py:159
  22.8 12.4 %collective-permute-start.7 = (f32[256,256]{1,0:T(8,128)}, f32[256,256]{1,0:T(8,128)S(1)}, u32[]{:S(2)}, u32[]{:S(2)}) collective-permute-start(f32[256,256]{1,0:T(8,128)} %slice.26), channel_id=1, source_target_pairs={{13,1},{28,16},{45,33},{62,50},{79,67},{92,84},{109,101},{126,118}... | collective-permute-start | bytes 786440 | tf_op jit(solution)/shard_map/ppermute | solution.py:159
  38.3 6.3 %collective-permute-start.8 = (f32[2,4,1024]{2,1,0:T(4,128)S(1)}, f32[2,4,1024]{2,1,0:T(4,128)S(1)}, u32[]{:S(2)}, u32[]{:S(2)}) collective-permute-start(f32[2,4,1024]{2,1,0:T(4,128)S(1)} %get-tuple-element.65), channel_id=1, source_target_pairs={{1,16},{118,135},{237,254}} | collective-permute-start | bytes 98312 | tf_op jit(solution)/shard_map/ppermute | solution.py:159
  39.6 2.1 %collective-permute-start.9 = (f32[4,1024]{1,0:T(4,128)S(1)}, f32[4,1024]{1,0:T(4,128)S(1)}, u32[]{:S(2)}, u32[]{:S(2)}) collective-permute-start(f32[4,1024]{1,0:T(4,128)S(1)} %get-tuple-element.66), channel_id=1, source_target_pairs={{1,48},{33,194},{50,147},{67,132},{82,210},{84,133},{98,226},{99,1... | collective-permute-start | bytes 49160 | tf_op jit(solution)/shard_map/ppermute | solution.py:159
  45.8 6.8 %collective-permute-start.10 = (f32[2,4,1024]{2,1,0:T(4,128)S(1)}, f32[2,4,1024]{2,1,0:T(4,128)S(1)}, u32[]{:S(2)}, u32[]{:S(2)}) collective-permute-start(f32[2,4,1024]{2,1,0:T(4,128)S(1)} %get-tuple-element.68), channel_id=1, source_target_pairs={{16,33},{135,152}} | collective-permute-start | bytes 98312 | tf_op jit(solution)/shard_map/ppermute | solution.py:159
  50.5 2.1 %collective-permute-start.11 = (f32[4,1024]{1,0:T(4,128)S(1)}, f32[4,1024]{1,0:T(4,128)S(1)}, u32[]{:S(2)}, u32[]{:S(2)}) collective-permute-start(f32[4,1024]{1,0:T(4,128)S(1)} %get-tuple-element.69), channel_id=1, source_target_pairs={{1,64},{16,65},{48,80},{50,211},{67,164},{84,149},{99,227},{101,15... | collective-permute-start | bytes 49160 | tf_op jit(solution)/shard_map/ppermute | solution.py:159
  53.8 3.5 %collective-permute-start.13 = (f32[2,4,1024]{2,1,0:T(4,128)S(1)}, f32[2,4,1024]{2,1,0:T(4,128)S(1)}, u32[]{:S(2)}, u32[]{:S(2)}) collective-permute-start(f32[2,4,1024]{2,1,0:T(4,128)S(1)} %get-tuple-element.72), channel_id=1, source_target_pairs={{33,50},{152,169}} | collective-permute-start | bytes 98312 | tf_op jit(solution)/shard_map/ppermute | solution.py:159
  54.5 2.0 collective-permute-start.15
  55.2 2.1 %collective-permute-start.14 = (f32[4,1024]{1,0:T(4,128)S(1)}, f32[4,1024]{1,0:T(4,128)S(1)}, u32[]{:S(2)}, u32[]{:S(2)}) collective-permute-start(f32[4,1024]{1,0:T(4,128)S(1)} %get-tuple-element.73), channel_id=1, source_target_pairs={{1,96},{16,81},{33,82},{48,112},{64,128},{65,97},{67,228},{80,144}... | collective-permute-start | bytes 49160 | tf_op jit(solution)/shard_map/ppermute | solution.py:159
  58.5 4.2 %collective-permute-start.16 = (f32[2,4,1024]{2,1,0:T(4,128)S(1)}, f32[2,4,1024]{2,1,0:T(4,128)S(1)}, u32[]{:S(2)}, u32[]{:S(2)}) collective-permute-start(f32[2,4,1024]{2,1,0:T(4,128)S(1)} %get-tuple-element.76), channel_id=1, source_target_pairs={{50,67},{169,186}} | collective-permute-start | bytes 98312 | tf_op jit(solution)/shard_map/ppermute | solution.py:159
  59.2 2.6 %collective-permute-start.18 = (f32[4,1024]{1,0:T(4,128)S(1)}, f32[4,1024]{1,0:T(4,128)S(1)}, u32[]{:S(2)}, u32[]{:S(2)}) collective-permute-start(f32[4,1024]{1,0:T(4,128)S(1)} %get-tuple-element.78), channel_id=1, source_target_pairs={{65,67},{80,84},{184,186},{199,203},{214,220},{229,237},{244,254}} | collective-permute-start | bytes 49160 | tf_op jit(solution)/shard_map/ppermute | solution.py:159
  59.9 2.0 collective-permute-start.19
  60.6 2.1 %collective-permute-start.17 = (f32[4,1024]{1,0:T(4,128)S(1)}, f32[4,1024]{1,0:T(4,128)S(1)}, u32[]{:S(2)}, u32[]{:S(2)}) collective-permute-start(f32[4,1024]{1,0:T(4,128)S(1)} %get-tuple-element.77), channel_id=1, source_target_pairs={{1,160},{16,113},{33,98},{48,176},{50,99},{64,192},{65,129},{80,20... | collective-permute-start | bytes 49160 | tf_op jit(solution)/shard_map/ppermute | solution.py:159
  63.9 4.2 %collective-permute-start.20 = (f32[2,4,1024]{2,1,0:T(4,128)S(1)}, f32[2,4,1024]{2,1,0:T(4,128)S(1)}, u32[]{:S(2)}, u32[]{:S(2)}) collective-permute-start(f32[2,4,1024]{2,1,0:T(4,128)S(1)} %get-tuple-element.80), channel_id=1, source_target_pairs={{67,84},{186,203}} | collective-permute-start | bytes 98312 | tf_op jit(solution)/shard_map/ppermute | solution.py:159
  64.6 2.6 %collective-permute-start.22 = (f32[4,1024]{1,0:T(4,128)S(1)}, f32[4,1024]{1,0:T(4,128)S(1)}, u32[]{:S(2)}, u32[]{:S(2)}) collective-permute-start(f32[4,1024]{1,0:T(4,128)S(1)} %get-tuple-element.82), channel_id=1, source_target_pairs={{82,84},{97,101},{112,118},{201,203},{216,220},{231,237},{246,254}} | collective-permute-start | bytes 49160 | tf_op jit(solution)/shard_map/ppermute | solution.py:159
  65.3 2.0 collective-permute-start.23
  65.9 2.1 %collective-permute-start.21 = (f32[4,1024]{1,0:T(4,128)S(1)}, f32[4,1024]{1,0:T(4,128)S(1)}, u32[]{:S(2)}, u32[]{:S(2)}) collective-permute-start(f32[4,1024]{1,0:T(4,128)S(1)} %get-tuple-element.81), channel_id=1, source_target_pairs={{16,177},{33,130},{50,115},{65,193},{67,116},{81,209},{82,146},{97... | collective-permute-start | bytes 49160 | tf_op jit(solution)/shard_map/ppermute | solution.py:159
  69.3 2.7 %collective-permute-start.24 = (f32[2,4,1024]{2,1,0:T(4,128)S(1)}, f32[2,4,1024]{2,1,0:T(4,128)S(1)}, u32[]{:S(2)}, u32[]{:S(2)}) collective-permute-start(f32[2,4,1024]{2,1,0:T(4,128)S(1)} %get-tuple-element.84), channel_id=1, source_target_pairs={{84,101},{203,220}} | collective-permute-start | bytes 98312 | tf_op jit(solution)/shard_map/ppermute | solution.py:159
  70.0 2.0 collective-permute-start.26
  70.7 1.4 collective-permute-start.27
  71.3 0.7 collective-permute-start.25
  73.3 11.2 %collective-permute-start.28 = (f32[2,4,1024]{2,1,0:T(4,128)S(1)}, f32[2,4,1024]{2,1,0:T(4,128)S(1)}, u32[]{:S(2)}, u32[]{:S(2)}) collective-permute-start(f32[2,4,1024]{2,1,0:T(4,128)S(1)} %get-tuple-element.88), channel_id=1, source_target_pairs={{101,118},{220,237}} | collective-permute-start | bytes 98312 | tf_op jit(solution)/shard_map/ppermute | solution.py:159
  73.9 9.7 %collective-permute-start.30 = (f32[4,1024]{1,0:T(4,128)S(1)}, f32[4,1024]{1,0:T(4,128)S(1)}, u32[]{:S(2)}, u32[]{:S(2)}) collective-permute-start(f32[4,1024]{1,0:T(4,128)S(1)} %get-tuple-element.90), channel_id=1, source_target_pairs={{116,118},{131,135},{146,152},{161,169},{176,186},{235,237},{250,2... | collective-permute-start | bytes 49160 | tf_op jit(solution)/shard_map/ppermute | solution.py:159
  74.6 9.0 %collective-permute-start.31 = (f32[4,1024]{1,0:T(4,128)S(1)}, f32[4,1024]{1,0:T(4,128)S(1)}, u32[]{:S(2)}, u32[]{:S(2)}) collective-permute-start(f32[4,1024]{1,0:T(4,128)S(1)} %get-tuple-element.90), channel_id=1, source_target_pairs={{115,118},{130,135},{145,152},{160,169},{234,237},{249,254}} | collective-permute-start | bytes 49160 | tf_op jit(solution)/shard_map/ppermute | solution.py:159
  75.3 9.2 %collective-permute-start.29 = (f32[4,1024]{1,0:T(4,128)S(1)}, f32[4,1024]{1,0:T(4,128)S(1)}, u32[]{:S(2)}, u32[]{:S(2)}) collective-permute-start(f32[4,1024]{1,0:T(4,128)S(1)} %get-tuple-element.89), channel_id=1, source_target_pairs={{1,64},{16,65},{48,80},{50,211},{67,164},{84,149},{99,227},{101,15... | collective-permute-start | bytes 49160 | tf_op jit(solution)/shard_map/ppermute | solution.py:159
  85.7 5.2 %collective-permute-start.32 = (f32[2,4,1024]{2,1,0:T(4,128)S(1)}, f32[2,4,1024]{2,1,0:T(4,128)S(1)}, u32[]{:S(2)}, u32[]{:S(2)}) collective-permute-start(f32[2,4,1024]{2,1,0:T(4,128)S(1)} %get-tuple-element.92), channel_id=1, source_target_pairs={{1,16},{118,135},{237,254}} | collective-permute-start | bytes 98312 | tf_op jit(solution)/shard_map/ppermute | solution.py:159
  87.0 2.6 %collective-permute-start.34 = (f32[4,1024]{1,0:T(4,128)S(1)}, f32[4,1024]{1,0:T(4,128)S(1)}, u32[]{:S(2)}, u32[]{:S(2)}) collective-permute-start(f32[4,1024]{1,0:T(4,128)S(1)} %get-tuple-element.94), channel_id=1, source_target_pairs={{133,135},{148,152},{163,169},{178,186},{193,203},{208,220},{252,2... | collective-permute-start | bytes 49160 | tf_op jit(solution)/shard_map/ppermute | solution.py:159
  87.7 2.0 collective-permute-start.35
  88.4 2.1 %collective-permute-start.33 = (f32[4,1024]{1,0:T(4,128)S(1)}, f32[4,1024]{1,0:T(4,128)S(1)}, u32[]{:S(2)}, u32[]{:S(2)}) collective-permute-start(f32[4,1024]{1,0:T(4,128)S(1)} %get-tuple-element.93), channel_id=1, source_target_pairs={{1,96},{16,81},{33,82},{48,112},{64,128},{65,97},{67,228},{80,144}... | collective-permute-start | bytes 49160 | tf_op jit(solution)/shard_map/ppermute | solution.py:159
  92.2 20.7 %collective-permute-start.36 = (f32[2,4,1024]{2,1,0:T(4,128)S(1)}, f32[2,4,1024]{2,1,0:T(4,128)S(1)}, u32[]{:S(2)}, u32[]{:S(2)}) collective-permute-start(f32[2,4,1024]{2,1,0:T(4,128)S(1)} %get-tuple-element.96), channel_id=1, source_target_pairs={{16,33},{135,152}} | collective-permute-start | bytes 98312 | tf_op jit(solution)/shard_map/ppermute | solution.py:159
  94.6 17.4 %collective-permute-start.38 = (f32[4,1024]{1,0:T(4,128)S(1)}, f32[4,1024]{1,0:T(4,128)S(1)}, u32[]{:S(2)}, u32[]{:S(2)}) collective-permute-start(f32[4,1024]{1,0:T(4,128)S(1)} %get-tuple-element.98), channel_id=1, source_target_pairs={{150,152},{165,169},{180,186},{195,203},{210,220},{225,237},{240,2... | collective-permute-start | bytes 49160 | tf_op jit(solution)/shard_map/ppermute | solution.py:159
  95.2 16.8 %collective-permute-start.39 = (f32[4,1024]{1,0:T(4,128)S(1)}, f32[4,1024]{1,0:T(4,128)S(1)}, u32[]{:S(2)}, u32[]{:S(2)}) collective-permute-start(f32[4,1024]{1,0:T(4,128)S(1)} %get-tuple-element.98), channel_id=1, source_target_pairs={{149,152},{164,169},{179,186},{194,203},{209,220},{224,237}} | collective-permute-start | bytes 49160 | tf_op jit(solution)/shard_map/ppermute | solution.py:159
  95.9 16.9 %collective-permute-start.37 = (f32[4,1024]{1,0:T(4,128)S(1)}, f32[4,1024]{1,0:T(4,128)S(1)}, u32[]{:S(2)}, u32[]{:S(2)}) collective-permute-start(f32[4,1024]{1,0:T(4,128)S(1)} %get-tuple-element.97), channel_id=1, source_target_pairs={{1,160},{16,113},{33,98},{48,176},{50,99},{64,192},{65,129},{80,20... | collective-permute-start | bytes 49160 | tf_op jit(solution)/shard_map/ppermute | solution.py:159
  114.1 21.2 %collective-permute-start.40 = (f32[2,4,1024]{2,1,0:T(4,128)S(1)}, f32[2,4,1024]{2,1,0:T(4,128)S(1)}, u32[]{:S(2)}, u32[]{:S(2)}) collective-permute-start(f32[2,4,1024]{2,1,0:T(4,128)S(1)} %get-tuple-element.100), channel_id=1, source_target_pairs={{33,50},{152,169}} | collective-permute-start | bytes 98312 | tf_op jit(solution)/shard_map/ppermute | solution.py:159
  114.7 19.6 %collective-permute-start.42 = (f32[4,1024]{1,0:T(4,128)S(1)}, f32[4,1024]{1,0:T(4,128)S(1)}, u32[]{:S(2)}, u32[]{:S(2)}) collective-permute-start(f32[4,1024]{1,0:T(4,128)S(1)} %get-tuple-element.102), channel_id=1, source_target_pairs={{48,50},{167,169},{182,186},{197,203},{212,220},{227,237},{242,254}} | collective-permute-start | bytes 49160 | tf_op jit(solution)/shard_map/ppermute | solution.py:159
  115.4 19.0 %collective-permute-start.43 = (f32[4,1024]{1,0:T(4,128)S(1)}, f32[4,1024]{1,0:T(4,128)S(1)}, u32[]{:S(2)}, u32[]{:S(2)}) collective-permute-start(f32[4,1024]{1,0:T(4,128)S(1)} %get-tuple-element.102), channel_id=1, source_target_pairs={{166,169},{181,186},{196,203},{211,220},{226,237},{241,254}} | collective-permute-start | bytes 49160 | tf_op jit(solution)/shard_map/ppermute | solution.py:159
  116.1 19.2 %collective-permute-start.41 = (f32[4,1024]{1,0:T(4,128)S(1)}, f32[4,1024]{1,0:T(4,128)S(1)}, u32[]{:S(2)}, u32[]{:S(2)}) collective-permute-start(f32[4,1024]{1,0:T(4,128)S(1)} %get-tuple-element.101), channel_id=1, source_target_pairs={{16,177},{33,130},{50,115},{65,193},{67,116},{81,209},{82,146},{97... | collective-permute-start | bytes 49160 | tf_op jit(solution)/shard_map/ppermute | solution.py:159
  136.5 2.7 %collective-permute-start.44 = (f32[2,4,1024]{2,1,0:T(4,128)S(1)}, f32[2,4,1024]{2,1,0:T(4,128)S(1)}, u32[]{:S(2)}, u32[]{:S(2)}) collective-permute-start(f32[2,4,1024]{2,1,0:T(4,128)S(1)} %get-tuple-element.104), channel_id=1, source_target_pairs={{50,67},{169,186}} | collective-permute-start | bytes 98312 | tf_op jit(solution)/shard_map/ppermute | solution.py:159
  137.1 2.0 collective-permute-start.46
  137.8 1.4 collective-permute-start.47
  140.4 4.2 %collective-permute-start.48 = (f32[2,4,1024]{2,1,0:T(4,128)S(1)}, f32[2,4,1024]{2,1,0:T(4,128)S(1)}, u32[]{:S(2)}, u32[]{:S(2)}) collective-permute-start(f32[2,4,1024]{2,1,0:T(4,128)S(1)} %get-tuple-element.108), channel_id=1, source_target_pairs={{67,84},{186,203}} | collective-permute-start | bytes 98312 | tf_op jit(solution)/shard_map/ppermute | solution.py:159
  141.1 2.6 %collective-permute-start.50 = (f32[4,1024]{1,0:T(4,128)S(1)}, f32[4,1024]{1,0:T(4,128)S(1)}, u32[]{:S(2)}, u32[]{:S(2)}) collective-permute-start(f32[4,1024]{1,0:T(4,128)S(1)} %get-tuple-element.110), channel_id=1, source_target_pairs={{82,84},{97,101},{112,118},{201,203},{216,220},{231,237},{246,254}} | collective-permute-start | bytes 49160 | tf_op jit(solution)/shard_map/ppermute | solution.py:159
  141.7 2.0 collective-permute-start.51
  142.4 2.1 %collective-permute-start.49 = (f32[4,1024]{1,0:T(4,128)S(1)}, f32[4,1024]{1,0:T(4,128)S(1)}, u32[]{:S(2)}, u32[]{:S(2)}) collective-permute-start(f32[4,1024]{1,0:T(4,128)S(1)} %get-tuple-element.109), channel_id=1, source_target_pairs={{1,64},{16,65},{48,80},{50,211},{67,164},{84,149},{99,227},{101,15... | collective-permute-start | bytes 49160 | tf_op jit(solution)/shard_map/ppermute | solution.py:159
  145.8 10.8 %collective-permute-start.52 = (f32[2,4,1024]{2,1,0:T(4,128)S(1)}, f32[2,4,1024]{2,1,0:T(4,128)S(1)}, u32[]{:S(2)}, u32[]{:S(2)}) collective-permute-start(f32[2,4,1024]{2,1,0:T(4,128)S(1)} %get-tuple-element.112), channel_id=1, source_target_pairs={{84,101},{203,220}} | collective-permute-start | bytes 98312 | tf_op jit(solution)/shard_map/ppermute | solution.py:159
  146.5 9.2 %collective-permute-start.54 = (f32[4,1024]{1,0:T(4,128)S(1)}, f32[4,1024]{1,0:T(4,128)S(1)}, u32[]{:S(2)}, u32[]{:S(2)}) collective-permute-start(f32[4,1024]{1,0:T(4,128)S(1)} %get-tuple-element.114), channel_id=1, source_target_pairs={{99,101},{114,118},{129,135},{144,152},{218,220},{233,237},{248,254}} | collective-permute-start | bytes 49160 | tf_op jit(solution)/shard_map/ppermute | solution.py:159
  147.1 8.6 %collective-permute-start.55 = (f32[4,1024]{1,0:T(4,128)S(1)}, f32[4,1024]{1,0:T(4,128)S(1)}, u32[]{:S(2)}, u32[]{:S(2)}) collective-permute-start(f32[4,1024]{1,0:T(4,128)S(1)} %get-tuple-element.114), channel_id=1, source_target_pairs={{98,101},{113,118},{128,135},{217,220},{232,237},{247,254}} | collective-permute-start | bytes 49160 | tf_op jit(solution)/shard_map/ppermute | solution.py:159
  147.8 8.7 %collective-permute-start.53 = (f32[4,1024]{1,0:T(4,128)S(1)}, f32[4,1024]{1,0:T(4,128)S(1)}, u32[]{:S(2)}, u32[]{:S(2)}) collective-permute-start(f32[4,1024]{1,0:T(4,128)S(1)} %get-tuple-element.113), channel_id=1, source_target_pairs={{1,96},{16,81},{33,82},{48,112},{64,128},{65,97},{67,228},{80,144}... | collective-permute-start | bytes 49160 | tf_op jit(solution)/shard_map/ppermute | solution.py:159
  157.8 5.1 %collective-permute-start.56 = (f32[2,4,1024]{2,1,0:T(4,128)S(1)}, f32[2,4,1024]{2,1,0:T(4,128)S(1)}, u32[]{:S(2)}, u32[]{:S(2)}) collective-permute-start(f32[2,4,1024]{2,1,0:T(4,128)S(1)} %get-tuple-element.116), channel_id=1, source_target_pairs={{101,118},{220,237}} | collective-permute-start | bytes 98312 | tf_op jit(solution)/shard_map/ppermute | solution.py:159
  158.4 3.6 %collective-permute-start.58 = (f32[4,1024]{1,0:T(4,128)S(1)}, f32[4,1024]{1,0:T(4,128)S(1)}, u32[]{:S(2)}, u32[]{:S(2)}) collective-permute-start(f32[4,1024]{1,0:T(4,128)S(1)} %get-tuple-element.118), channel_id=1, source_target_pairs={{116,118},{131,135},{146,152},{161,169},{176,186},{235,237},{250,2... | collective-permute-start | bytes 49160 | tf_op jit(solution)/shard_map/ppermute | solution.py:159
  159.1 2.9 %collective-permute-start.59 = (f32[4,1024]{1,0:T(4,128)S(1)}, f32[4,1024]{1,0:T(4,128)S(1)}, u32[]{:S(2)}, u32[]{:S(2)}) collective-permute-start(f32[4,1024]{1,0:T(4,128)S(1)} %get-tuple-element.118), channel_id=1, source_target_pairs={{115,118},{130,135},{145,152},{160,169},{234,237},{249,254}} | collective-permute-start | bytes 49160 | tf_op jit(solution)/shard_map/ppermute | solution.py:159
  159.8 3.1 %collective-permute-start.57 = (f32[4,1024]{1,0:T(4,128)S(1)}, f32[4,1024]{1,0:T(4,128)S(1)}, u32[]{:S(2)}, u32[]{:S(2)}) collective-permute-start(f32[4,1024]{1,0:T(4,128)S(1)} %get-tuple-element.117), channel_id=1, source_target_pairs={{1,160},{16,113},{33,98},{48,176},{50,99},{64,192},{65,129},{80,20... | collective-permute-start | bytes 49160 | tf_op jit(solution)/shard_map/ppermute | solution.py:159
  164.4 23.1 %collective-permute-start.60 = (f32[2,4,1024]{2,1,0:T(4,128)S(1)}, f32[2,4,1024]{2,1,0:T(4,128)S(1)}, u32[]{:S(2)}, u32[]{:S(2)}) collective-permute-start(f32[2,4,1024]{2,1,0:T(4,128)S(1)} %get-tuple-element.120), channel_id=1, source_target_pairs={{1,16},{118,135},{237,254}} | collective-permute-start | bytes 98312 | tf_op jit(solution)/shard_map/ppermute | solution.py:159
  165.7 20.9 %collective-permute-start.62 = (f32[4,1024]{1,0:T(4,128)S(1)}, f32[4,1024]{1,0:T(4,128)S(1)}, u32[]{:S(2)}, u32[]{:S(2)}) collective-permute-start(f32[4,1024]{1,0:T(4,128)S(1)} %get-tuple-element.122), channel_id=1, source_target_pairs={{133,135},{148,152},{163,169},{178,186},{193,203},{208,220},{252,2... | collective-permute-start | bytes 49160 | tf_op jit(solution)/shard_map/ppermute | solution.py:159
  166.4 20.3 %collective-permute-start.63 = (f32[4,1024]{1,0:T(4,128)S(1)}, f32[4,1024]{1,0:T(4,128)S(1)}, u32[]{:S(2)}, u32[]{:S(2)}) collective-permute-start(f32[4,1024]{1,0:T(4,128)S(1)} %get-tuple-element.122), channel_id=1, source_target_pairs={{132,135},{147,152},{162,169},{177,186},{192,203},{251,254}} | collective-permute-start | bytes 49160 | tf_op jit(solution)/shard_map/ppermute | solution.py:159
  167.0 20.4 %collective-permute-start.61 = (f32[4,1024]{1,0:T(4,128)S(1)}, f32[4,1024]{1,0:T(4,128)S(1)}, u32[]{:S(2)}, u32[]{:S(2)}) collective-permute-start(f32[4,1024]{1,0:T(4,128)S(1)} %get-tuple-element.121), channel_id=1, source_target_pairs={{16,177},{33,130},{50,115},{65,193},{67,116},{81,209},{82,146},{97... | collective-permute-start | bytes 49160 | tf_op jit(solution)/shard_map/ppermute | solution.py:159
  190.8 11.0 %all-to-all-start = ((f32[16,4,1152]{2,1,0:T(4,128)}), f32[16,4,1152]{2,1,0:T(4,128)S(1)}, u32[]{:S(2)}, u32[]{:S(2)}) async-start(f32[16,4,1152]{2,1,0:T(4,128)} %broadcast_in_dim.50), calls=%async_computation | async-start | bytes 589824 | tf_op jit(solution)/shard_map/all_to_all | solution.py:219
  (4 other events, 18.1 us)

commit v3 on v2

v3 whole, which is shorter than its diff:
```python
import math

import jax
import jax.numpy as jnp
from jax import lax
from jax.experimental import pallas as pl
from jax.experimental.pallas import tpu as pltpu
from jax.sharding import Mesh
from jax.sharding import PartitionSpec as P


ROW = "row"
COL = ("col_x", "col_y")
BOTH = (ROW, *COL)
SIDE = 4
BAND = 2
CHAIN_PERIOD = 5
SPREAD_PERIOD = 7
FAR_PERIOD = 7
ARRIVAL = {3: 0, 4: 1, 5: 1, 6: 2, 7: 2, 8: 2, 9: 3, 10: 3, 11: 3, 12: 3, 13: 3, 14: 3, 15: 4}
SENDER = {3: 1, 4: 1, 5: 3, 6: 3, 7: 4, 8: 5, 9: 3, 10: 4, 11: 5, 12: 6, 13: 7, 14: 8, 15: 3}


def solver(i):
    return (i, i - 1 if i else 1)


def union(rounds, period):
    patterns = []
    for first in range(min(period, len(rounds))):
        pairs = sorted({pair for moves in rounds[first::period] for pair in moves})
        assert len({s for s, _ in pairs}) == len(pairs) == len({d for _, d in pairs})
        patterns.append(pairs)
    return [patterns[r % period] for r in range(len(rounds))]


def plan(n):
    chain, spread, odd, even = [], [], [], []
    for r in range(n - 1):
        chain.append([(solver(r), solver(r + 1))])
        spread.append([])
        odd.append([])
        even.append([])
        for i in range(n):
            for j in range(i - BAND):
                d = i - j
                if j + ARRIVAL[d] == r:
                    spread[r].append((solver(j) if SENDER[d] == 1 else (j + SENDER[d], j), (i, j)))
                if i - 2 - (d - 3) // 2 == r:
                    (odd if d % 2 else even)[r].append(((i, j), solver(i)))
    return (
        union(chain, CHAIN_PERIOD),
        union(spread, SPREAD_PERIOD),
        union(odd, FAR_PERIOD),
        union(even, FAR_PERIOD),
    )


def assemble(place, block, parts):
    quarter, width = block.shape

    def body(place_ref, block_ref, *refs):
        out = refs[-1]
        for k in range(SIDE):
            start = k * quarter
            got = refs[k][...] + jnp.where(place_ref[0] == k, block_ref[:, start:], 0.0)
            if start:
                out[start : start + quarter, :start] = jnp.zeros((quarter, start), jnp.bfloat16)
            out[start : start + quarter, start:] = got.astype(jnp.bfloat16)

    vmem = pl.BlockSpec(memory_space=pltpu.VMEM)
    return pl.pallas_call(
        body,
        in_specs=[pl.BlockSpec(memory_space=pltpu.SMEM)] + [vmem] * (1 + SIDE),
        out_specs=vmem,
        out_shape=jax.ShapeDtypeStruct((width, width), jnp.bfloat16),
        compiler_params=pltpu.CompilerParams(vmem_limit_bytes=16 * 2**20),
        name="assemble",
    )(place, block, *parts)


def step(now, came, heard, odds, evens, value, own, pending, source, v_band, u_band, inverse):
    held = 1 if now < 1 else BAND
    nrhs, width = source.shape
    block = 256

    def body(came_ref, heard_ref, odds_ref, evens_ref, value_ref, own_ref, pending_ref, source_ref, *refs):
        v_refs, u_refs = refs[:held], refs[held : 2 * held]
        inverse_ref, bundle_out, value_out, own_out, pending_out = refs[2 * held :]
        row = lax.axis_index(ROW)
        col = lax.axis_index(COL[0]) * SIDE + lax.axis_index(COL[1])
        gap = row - col
        if now < 0:
            turn = (row == 0) & (col == 1)
        else:
            turn = (row == now + 1) & (gap == 1)
        hears = row < 0
        for when in sorted(set(ARRIVAL.values())):
            gaps = [d for d in ARRIVAL if ARRIVAL[d] == when]
            hears = hears | ((gap >= min(gaps)) & (gap <= max(gaps)) & (col == now - when))
        behind = row - 1 - now
        adds = (gap == 1) & (behind >= 0)
        left = pending_ref[...]
        if now >= 2:
            left = left + jnp.where(adds & (3 + 2 * behind <= row), odds_ref[...], 0.0)
        if now >= 3:
            left = left + jnp.where(adds & (4 + 2 * behind <= row), evens_ref[...], 0.0)
        pending_out[...] = left

        def share(known, d):
            inner = lax.dot_general(
                known.astype(jnp.bfloat16), v_refs[d][...], (((1,), (1,)), ((), ())), preferred_element_type=jnp.float32
            )
            return jnp.dot(inner.astype(jnp.bfloat16), u_refs[d][...], preferred_element_type=jnp.float32)

        @pl.when(jnp.logical_not(turn | hears))
        def _():
            value_out[...] = value_ref[...]
            own_out[...] = own_ref[...]

        @pl.when(hears)
        def _():
            value_out[...] = heard_ref[...]
            own_out[...] = share(heard_ref[...], 0)

        @pl.when(turn)
        def _():
            total = source_ref[...] - left
            if now >= 0:
                for d in range(held):
                    total = total - share(came_ref[d], d)
                bundle_out[1] = came_ref[0]
            else:
                bundle_out[1] = jnp.zeros((nrhs, width), jnp.float32)
            reduced = total.astype(jnp.bfloat16)
            columns = []
            for n in range(0, width, block):
                columns.append(
                    jnp.dot(
                        reduced[:, : n + block],
                        inverse_ref[: n + block, n : n + block],
                        preferred_element_type=jnp.float32,
                    )
                )
            result = jnp.concatenate(columns, axis=1)
            bundle_out[0] = result
            value_out[...] = result
            own_out[...] = own_ref[...]

    vmem = pl.BlockSpec(memory_space=pltpu.VMEM)
    small = jax.ShapeDtypeStruct((nrhs, width), jnp.float32)
    return pl.pallas_call(
        body,
        in_specs=[vmem] * (8 + 2 * held + 1),
        out_specs=[vmem] * 4,
        out_shape=[jax.ShapeDtypeStruct((BAND, nrhs, width), jnp.float32), small, small, small],
        compiler_params=pltpu.CompilerParams(vmem_limit_bytes=8 * 2**20),
        name="step",
    )(came, heard, odds, evens, value, own, pending, source, *v_band[:held], *u_band[:held], inverse)


def local(right_side, inverse_t, u_factor, v_factor, ranks):
    n = lax.axis_size(ROW)
    n_col = lax.axis_size(COL)
    nrhs, width = right_side.shape[2:]
    piece = width // n_col
    rank_max = u_factor.shape[4]
    row = lax.axis_index(ROW)
    col = lax.axis_index(COL)
    gap = row - col
    source = right_side.reshape(nrhs, width)
    u_tile = u_factor.reshape(rank_max, width)
    v_tile = v_factor.reshape(rank_max, width)
    keep = jnp.arange(rank_max, dtype=jnp.int32)[:, None] < ranks.reshape(1, 1)
    u_tile = jnp.where(keep, u_tile, jnp.zeros_like(u_tile))

    def move(array, pairs):
        numbered = [(s[0] * n_col + s[1], d[0] * n_col + d[1]) for s, d in pairs]
        return lax.ppermute(array, BOTH, numbered)

    rows = inverse_t.reshape(piece, width).astype(jnp.float32)
    quarter = width // SIDE
    slabs = []
    for k in range(SIDE):
        pairs = [
            ((r, x * SIDE + k), (r, x * SIDE + solver(r)[1] % SIDE))
            for r in range(n)
            for x in range(SIDE)
            if solver(r)[1] % SIDE != k
        ]
        slabs.append(move(rows, pairs) + jnp.where(col % SIDE == k, rows, 0.0))
    block = jnp.concatenate(slabs, axis=0)
    square = lax.dynamic_slice_in_dim(rows, col * piece, piece, 1)
    log_sum = jnp.sum(jnp.log(jnp.diagonal(square)))
    both = jnp.concatenate([v_tile, u_tile], axis=0).astype(jnp.float32)
    block, both, log_sum = lax.optimization_barrier((block, both, log_sum))
    parts = []
    for k in range(SIDE):
        pairs = [
            ((r, k * SIDE + solver(r)[1] % SIDE), solver(r)) for r in range(n) if solver(r)[1] // SIDE != k
        ]
        parts.append(move(block[:, k * quarter :], pairs))
    place = jnp.stack([col // SIDE]).astype(jnp.int32)

    second = move(both, [((i, i - 2), solver(i)) for i in range(2, n)])
    inverse = assemble(place, block, parts)
    second = (second + jnp.where(gap == 1, 0.0, both)).astype(jnp.bfloat16)
    v_band = [v_tile, second[:rank_max]]
    u_band = [u_tile, second[rank_max:]]

    chain, spread, odd, even = plan(n)
    nothing = jnp.zeros((nrhs, width), jnp.float32)
    no_bundle = jnp.zeros((BAND, nrhs, width), jnp.float32)
    bundle, value, own, pending = step(
        -1, no_bundle, nothing, nothing, nothing, nothing, nothing, nothing, source, v_band, u_band, inverse
    )
    odds = evens = nothing
    for r in range(n - 1):
        came = move(bundle, chain[r])
        heard = more_odds = more_evens = nothing
        if spread[r]:
            heard = move(value, spread[r])
        if 1 <= r < n - 2:
            more_odds = move(own, odd[r])
        if 2 <= r < n - 2:
            more_evens = move(own, even[r])
        bundle, value, own, pending = step(
            r, came, heard, odds, evens, value, own, pending, source, v_band, u_band, inverse
        )
        odds, evens = more_odds, more_evens
    result = value

    payload = jnp.concatenate([result, jnp.broadcast_to(log_sum, (nrhs, 128))], axis=1)
    payload = jnp.broadcast_to(payload[None], (n_col, *payload.shape))
    arrived = lax.all_to_all(payload, COL, 0, 0, tiled=True)
    solved = lax.dynamic_index_in_dim(arrived, jnp.where(row == 0, 1, row - 1), 0, False)[:, :width]
    logdiag = jnp.sum(arrived[:, 0, width]) / width
    quadratic = jnp.mean(solved * solved, axis=1)
    loglik = -0.5 * quadratic + logdiag - 0.5 * math.log(2.0 * math.pi)
    return solved.reshape(1, 1, nrhs, width), loglik.reshape(1, 1, nrhs)


def solution(mesh):
    plane = Mesh(mesh.devices.reshape(-1, SIDE, SIDE), BOTH)
    return jax.shard_map(
        local,
        mesh=plane,
        in_specs=(
            P(None, ROW, None, None),
            P(None, ROW, COL, None),
            P(None, ROW, None, COL, None, None),
            P(None, ROW, None, COL, None, None),
            P(None, ROW, None, COL),
        ),
        out_specs=(P(None, ROW, None, None), P(None, ROW, None)),
        check_vma=False,
    )
```

time: 206 us -> 185 us (0.90)
  the two profiles are of different devices: /device:TPU:1 before, /device:TPU:224 now
where the time goes in v3:
time: 185 us; the launch traced here: 182 us
  starting transfers between devices  121 us (65%)
  waiting for transfers between devices  41.3 us (22%)
  other arithmetic  8.55 us (5%)
  local copies, waits for them, and re-layouts  4.97 us (3%)
  Pallas kernels  3.24 us (2%)
  between operations  3.18 us (2%)
    ppermute x64, starting transfers between devices, move(): return lax.ppermute(array, BOTH, numbered)  85.4 us
    all_to_all x1, starting transfers between devices, local(): arrived = lax.all_to_all(payload, COL, 0, 0, tiled=True)  35.8 us
    ppermute x64, waiting for transfers between devices, move(): return lax.ppermute(array, BOTH, numbered)  32.5 us
    all_to_all x1, waiting for transfers between devices, local(): arrived = lax.all_to_all(payload, COL, 0, 0, tiled=True)  8.77 us
  transfers between devices with their start and end apart: 65, of which 4 were waited for; matrix products, arithmetic and copies ran while one was open for 5% of the time, Pallas kernels for 1%

profile of v3, /device:TPU:224, one launch (start us, length us, event | category | flops | bytes accessed | tf_op | source)
XLA Modules:
  0.0 182.4 jit_solution(11921755007821227926)
XLA Ops:
  0.6 1.0 fusion.1
  1.6 3.5 %collective-permute-start = (f32[64,1024]{1,0:T(8,128)S(1)}, f32[64,1024]{1,0:T(8,128)S(1)}, u32[]{:S(2)}, u32[]{:S(2)}) collective-permute-start(f32[64,1024]{1,0:T(8,128)S(1)} %get-tuple-element.133), channel_id=1, source_target_pairs={{0,1},{4,5},{8,9},{12,13},{32,33},{36,37},{40,41},{44,45},{48,50},... | collective-permute-start | bytes 786440 | tf_op jit(solution)/shard_map/ppermute | solution.py:179
  5.2 0.7 collective-permute-start.1
  5.8 0.7 collective-permute-start.2
  6.5 0.7 collective-permute-start.3
  8.0 1.0 bitcast_select_fusion.refs_1_.refs_2_
  9.0 0.8 gather_fusion
  9.8 0.7 log_reduce_fusion
  10.5 2.1 %maximum_convert_fusion = f32[256,1024]{1,0:T(8,128)} fusion(bf16[128,1024]{1,0:T(8,128)(2,1)S(1)} %bitcast_select_fusion.refs_1_.refs_2_, bf16[128,1024]{1,0:T(8,128)(2,1)} %bitcast.27), kind=kLoop, calls=%fused_computation.3 | loop fusion | flops 1048576 | bytes 1572864 | tf_op jit(solution)/shard_map/convert_element_type | solution.py:195
  12.8 0.7 collective-permute-start.4
  13.5 1.6 collective-permute-start.12
  15.2 1.0 slice.21
  16.1 0.7 collective-permute-start.5
  16.8 0.9 slice.22
  17.7 1.4 collective-permute-start.6
  19.1 0.7 slice.23
  19.9 0.7 collective-permute-start.7
  20.7 1.4 assemble.1.refs_2_.refs_4_
  22.2 0.7 collective-permute-start.8
  22.8 0.7 collective-permute-start.9
  23.5 1.7 add_convert_fusion
  25.3 0.7 collective-permute-start.10
  26.0 0.7 collective-permute-start.11
  26.8 0.7 collective-permute-start.13
  27.5 0.7 collective-permute-start.15
  28.1 0.7 collective-permute-start.14
  28.9 0.7 collective-permute-start.16
  29.6 0.7 collective-permute-start.18
  30.2 0.7 collective-permute-start.19
  30.9 1.3 collective-permute-start.17
  32.2 25.5 %collective-permute-done.17.heard_ref = f32[4,1024]{1,0:T(4,128)S(1)} collective-permute-done((f32[4,1024]{1,0:T(4,128)S(1)}, f32[4,1024]{1,0:T(4,128)S(1)}, u32[]{:S(2)}, u32[]{:S(2)}) %collective-permute-start.17) | collective-permute-done | bytes 16416 | tf_op jit(solution)/shard_map/ppermute | solution.py:179
  58.1 0.7 collective-permute-start.20
  58.8 0.7 collective-permute-start.22
  59.5 0.7 collective-permute-start.23
  60.1 0.7 collective-permute-start.21
  60.9 0.7 collective-permute-start.24
  61.6 0.7 collective-permute-start.26
  62.2 0.7 collective-permute-start.27
  62.9 0.7 collective-permute-start.25
  63.7 0.7 collective-permute-start.28
  64.4 0.7 collective-permute-start.30
  65.0 0.7 collective-permute-start.31
  65.7 0.7 collective-permute-start.29
  66.5 0.7 collective-permute-start.32
  67.1 0.7 collective-permute-start.34
  69.3 0.7 collective-permute-start.36
  70.6 37.6 %collective-permute-start.39 = (f32[4,1024]{1,0:T(4,128)S(1)}, f32[4,1024]{1,0:T(4,128)S(1)}, u32[]{:S(2)}, u32[]{:S(2)}) collective-permute-start(f32[4,1024]{1,0:T(4,128)S(1)} %get-tuple-element.98.own_ref), channel_id=1, source_target_pairs={{149,152},{164,169},{179,186},{194,203},{209,220},{224,237}} | collective-permute-start | bytes 49160 | tf_op jit(solution)/shard_map/ppermute | solution.py:179
  108.9 0.7 collective-permute-done.39.evens_ref
  109.7 0.7 collective-permute-start.40
  112.5 0.7 collective-permute-start.44
  113.1 0.7 collective-permute-start.46
  113.8 0.7 collective-permute-start.47
  114.5 1.3 collective-permute-start.45
  115.8 6.1 %collective-permute-done.45.heard_ref = f32[4,1024]{1,0:T(4,128)S(1)} collective-permute-done((f32[4,1024]{1,0:T(4,128)S(1)}, f32[4,1024]{1,0:T(4,128)S(1)}, u32[]{:S(2)}, u32[]{:S(2)}) %collective-permute-start.45) | collective-permute-done | bytes 16416 | tf_op jit(solution)/shard_map/ppermute | solution.py:179
  121.9 0.7 collective-permute-start.48
  124.9 0.7 collective-permute-start.52
  127.7 0.7 collective-permute-start.56
  130.5 0.7 collective-permute-start.60
  133.2 0.7 step.31
  133.9 0.7 concatenate.16
  134.5 0.8 broadcast_in_dim.46
  135.3 35.8 %all-to-all-start = ((f32[16,4,1152]{2,1,0:T(4,128)}), f32[16,4,1152]{2,1,0:T(4,128)S(1)}, u32[]{:S(2)}, u32[]{:S(2)}) async-start(f32[16,4,1152]{2,1,0:T(4,128)} %broadcast_in_dim.46), calls=%async_computation | async-start | bytes 589824 | tf_op jit(solution)/shard_map/all_to_all | solution.py:235
  171.2 8.8 %all-to-all-done = f32[16,4,1152]{2,1,0:T(4,128)S(1)} async-done(((f32[16,4,1152]{2,1,0:T(4,128)}), f32[16,4,1152]{2,1,0:T(4,128)S(1)}, u32[]{:S(2)}, u32[]{:S(2)}) %all-to-all-start) | async-done | bytes 294944 | tf_op jit(solution)/shard_map/all_to_all | solution.py:235
  179.9 0.7 multiply_reduce_fusion
  (112 shorter events, 15.4 us)
Async XLA Ops:
  1.6 10.9 %collective-permute-start = (f32[64,1024]{1,0:T(8,128)S(1)}, f32[64,1024]{1,0:T(8,128)S(1)}, u32[]{:S(2)}, u32[]{:S(2)}) collective-permute-start(f32[64,1024]{1,0:T(8,128)S(1)} %get-tuple-element.133), channel_id=1, source_target_pairs={{0,1},{4,5},{8,9},{12,13},{32,33},{36,37},{40,41},{44,45},{48,50},... | collective-permute-start | bytes 786440 | tf_op jit(solution)/shard_map/ppermute | solution.py:179
  5.2 7.4 %collective-permute-start.1 = (f32[64,1024]{1,0:T(8,128)S(1)}, f32[64,1024]{1,0:T(8,128)S(1)}, u32[]{:S(2)}, u32[]{:S(2)}) collective-permute-start(f32[64,1024]{1,0:T(8,128)S(1)} %get-tuple-element.133), channel_id=1, source_target_pairs={{17,16},{21,20},{25,24},{29,28},{49,50},{53,54},{57,58},{61,62},{6... | collective-permute-start | bytes 786440 | tf_op jit(solution)/shard_map/ppermute | solution.py:179
  5.8 6.7 %collective-permute-start.2 = (f32[64,1024]{1,0:T(8,128)S(1)}, f32[64,1024]{1,0:T(8,128)S(1)}, u32[]{:S(2)}, u32[]{:S(2)}) collective-permute-start(f32[64,1024]{1,0:T(8,128)S(1)} %get-tuple-element.133), channel_id=1, source_target_pairs={{2,1},{6,5},{10,9},{14,13},{18,16},{22,20},{26,24},{30,28},{34,33}... | collective-permute-start | bytes 786440 | tf_op jit(solution)/shard_map/ppermute | solution.py:179
  6.5 6.1 %collective-permute-start.3 = (f32[64,1024]{1,0:T(8,128)S(1)}, f32[64,1024]{1,0:T(8,128)S(1)}, u32[]{:S(2)}, u32[]{:S(2)}) collective-permute-start(f32[64,1024]{1,0:T(8,128)S(1)} %get-tuple-element.133), channel_id=1, source_target_pairs={{3,1},{7,5},{11,9},{15,13},{19,16},{23,20},{27,24},{31,28},{35,33}... | collective-permute-start | bytes 786440 | tf_op jit(solution)/shard_map/ppermute | solution.py:179
  12.8 7.8 %collective-permute-start.4 = (f32[256,1024]{1,0:T(8,128)S(1)}, f32[256,1024]{1,0:T(8,128)S(1)}, u32[]{:S(2)}, u32[]{:S(2)}) collective-permute-start(f32[256,1024]{1,0:T(8,128)S(1)} %pad_maximum_fusion.block_ref), channel_id=1, source_target_pairs={{80,84},{97,101},{114,118},{131,135},{144,152},{161,169},{178,186}... | collective-permute-start | bytes 3145736 | tf_op jit(solution)/shard_map/ppermute | solution.py:179
  13.5 10.0 %collective-permute-start.12 = (f32[256,1024]{1,0:T(8,128)}, f32[256,1024]{1,0:T(8,128)}, u32[]{:S(2)}, u32[]{:S(2)}) collective-permute-start(f32[256,1024]{1,0:T(8,128)} %maximum_convert_fusion), channel_id=1, source_target_pairs={{32,33},{49,50},{66,67},{83,84},{100,101},{117,118},{134,135},{151... | collective-permute-start | bytes 3145736 | tf_op jit(solution)/shard_map/ppermute | solution.py:179
  16.1 4.5 %collective-permute-start.5 = (f32[256,768]{1,0:T(8,128)}, f32[256,768]{1,0:T(8,128)S(1)}, u32[]{:S(2)}, u32[]{:S(2)}) collective-permute-start(f32[256,768]{1,0:T(8,128)} %slice.21), channel_id=1, source_target_pairs={{5,1},{20,16},{37,33},{54,50},{71,67},{148,152},{165,169},{182,186... | collective-permute-start | bytes 2359304 | tf_op jit(solution)/shard_map/ppermute | solution.py:179
  17.7 2.9 %collective-permute-start.6 = (f32[256,512]{1,0:T(8,128)}, f32[256,512]{1,0:T(8,128)}, u32[]{:S(2)}, u32[]{:S(2)}) collective-permute-start(f32[256,512]{1,0:T(8,128)} %slice.22), channel_id=1, source_target_pairs={{9,1},{24,16},{41,33},{58,50},{75,67},{88,84},{105,101},{122,118},... | collective-permute-start | bytes 1572872 | tf_op jit(solution)/shard_map/ppermute | solution.py:179
  19.9 0.7 collective-permute-start.7
  22.2 3.1 %collective-permute-start.8 = (f32[2,4,1024]{2,1,0:T(4,128)S(1)}, f32[2,4,1024]{2,1,0:T(4,128)S(1)}, u32[]{:S(2)}, u32[]{:S(2)}) collective-permute-start(f32[2,4,1024]{2,1,0:T(4,128)S(1)} %get-tuple-element.67), channel_id=1, source_target_pairs={{1,16},{84,101},{169,186}} | collective-permute-start | bytes 98312 | tf_op jit(solution)/shard_map/ppermute | solution.py:179
  22.8 2.4 %collective-permute-start.9 = (f32[4,1024]{1,0:T(4,128)S(1)}, f32[4,1024]{1,0:T(4,128)S(1)}, u32[]{:S(2)}, u32[]{:S(2)}) collective-permute-start(f32[4,1024]{1,0:T(4,128)S(1)} %get-tuple-element.68.value_ref), channel_id=1, source_target_pairs={{1,48},{101,166},{116,212},{118,167},{132,228},{133,181},{148,244}... | collective-permute-start | bytes 49160 | tf_op jit(solution)/shard_map/ppermute | solution.py:179
  25.3 1.4 collective-permute-start.10
  26.0 0.7 collective-permute-start.11
  26.8 2.0 %collective-permute-start.13 = (f32[2,4,1024]{2,1,0:T(4,128)S(1)}, f32[2,4,1024]{2,1,0:T(4,128)S(1)}, u32[]{:S(2)}, u32[]{:S(2)}) collective-permute-start(f32[2,4,1024]{2,1,0:T(4,128)S(1)} %get-tuple-element.76), channel_id=1, source_target_pairs={{33,50},{118,135},{203,220}} | collective-permute-start | bytes 98312 | tf_op jit(solution)/shard_map/ppermute | solution.py:179
  27.5 1.3 collective-permute-start.15
  28.9 28.9 %collective-permute-start.16 = (f32[2,4,1024]{2,1,0:T(4,128)S(1)}, f32[2,4,1024]{2,1,0:T(4,128)S(1)}, u32[]{:S(2)}, u32[]{:S(2)}) collective-permute-start(f32[2,4,1024]{2,1,0:T(4,128)S(1)} %get-tuple-element.80), channel_id=1, source_target_pairs={{50,67},{135,152},{220,237}} | collective-permute-start | bytes 98312 | tf_op jit(solution)/shard_map/ppermute | solution.py:179
  29.6 2.6 %collective-permute-start.18 = (f32[4,1024]{1,0:T(4,128)S(1)}, f32[4,1024]{1,0:T(4,128)S(1)}, u32[]{:S(2)}, u32[]{:S(2)}) collective-permute-start(f32[4,1024]{1,0:T(4,128)S(1)} %get-tuple-element.78.own_ref), channel_id=1, source_target_pairs={{65,67},{80,84},{184,186},{199,203},{214,220},{229,237},{244,254}} | collective-permute-start | bytes 49160 | tf_op jit(solution)/shard_map/ppermute | solution.py:179
  30.2 2.0 %collective-permute-start.19 = (f32[4,1024]{1,0:T(4,128)S(1)}, f32[4,1024]{1,0:T(4,128)S(1)}, u32[]{:S(2)}, u32[]{:S(2)}) collective-permute-start(f32[4,1024]{1,0:T(4,128)S(1)} %get-tuple-element.78.own_ref), channel_id=1, source_target_pairs={{64,67},{183,186},{198,203},{213,220},{228,237},{243,254}} | collective-permute-start | bytes 49160 | tf_op jit(solution)/shard_map/ppermute | solution.py:179
  30.9 26.8 %collective-permute-start.17 = (f32[4,1024]{1,0:T(4,128)S(1)}, f32[4,1024]{1,0:T(4,128)S(1)}, u32[]{:S(2)}, u32[]{:S(2)}) collective-permute-start(f32[4,1024]{1,0:T(4,128)S(1)} %get-tuple-element.81.value_ref), channel_id=1, source_target_pairs={{33,98},{48,144},{50,99},{64,160},{65,113},{80,176},{81,129},{82,1... | collective-permute-start | bytes 49160 | tf_op jit(solution)/shard_map/ppermute | solution.py:179
  58.1 2.7 %collective-permute-start.20 = (f32[2,4,1024]{2,1,0:T(4,128)S(1)}, f32[2,4,1024]{2,1,0:T(4,128)S(1)}, u32[]{:S(2)}, u32[]{:S(2)}) collective-permute-start(f32[2,4,1024]{2,1,0:T(4,128)S(1)} %get-tuple-element.84), channel_id=1, source_target_pairs={{67,84},{152,169},{237,254}} | collective-permute-start | bytes 98312 | tf_op jit(solution)/shard_map/ppermute | solution.py:179
  58.8 2.0 %collective-permute-start.22 = (f32[4,1024]{1,0:T(4,128)S(1)}, f32[4,1024]{1,0:T(4,128)S(1)}, u32[]{:S(2)}, u32[]{:S(2)}) collective-permute-start(f32[4,1024]{1,0:T(4,128)S(1)} %get-tuple-element.82.own_ref), channel_id=1, source_target_pairs={{82,84},{97,101},{112,118},{201,203},{216,220},{231,237},{246,254}} | collective-permute-start | bytes 49160 | tf_op jit(solution)/shard_map/ppermute | solution.py:179
  59.5 1.4 collective-permute-start.23
  60.1 0.7 collective-permute-start.21
  60.9 2.7 %collective-permute-start.24 = (f32[2,4,1024]{2,1,0:T(4,128)S(1)}, f32[2,4,1024]{2,1,0:T(4,128)S(1)}, u32[]{:S(2)}, u32[]{:S(2)}) collective-permute-start(f32[2,4,1024]{2,1,0:T(4,128)S(1)} %get-tuple-element.88), channel_id=1, source_target_pairs={{1,16},{84,101},{169,186}} | collective-permute-start | bytes 98312 | tf_op jit(solution)/shard_map/ppermute | solution.py:179
  61.6 2.0 %collective-permute-start.26 = (f32[4,1024]{1,0:T(4,128)S(1)}, f32[4,1024]{1,0:T(4,128)S(1)}, u32[]{:S(2)}, u32[]{:S(2)}) collective-permute-start(f32[4,1024]{1,0:T(4,128)S(1)} %get-tuple-element.86.own_ref), channel_id=1, source_target_pairs={{99,101},{114,118},{129,135},{144,152},{218,220},{233,237},{248,254}} | collective-permute-start | bytes 49160 | tf_op jit(solution)/shard_map/ppermute | solution.py:179
  62.2 1.4 collective-permute-start.27
  62.9 0.7 collective-permute-start.25
  63.7 2.7 %collective-permute-start.28 = (f32[2,4,1024]{2,1,0:T(4,128)S(1)}, f32[2,4,1024]{2,1,0:T(4,128)S(1)}, u32[]{:S(2)}, u32[]{:S(2)}) collective-permute-start(f32[2,4,1024]{2,1,0:T(4,128)S(1)} %get-tuple-element.92), channel_id=1, source_target_pairs={{16,33},{101,118},{186,203}} | collective-permute-start | bytes 98312 | tf_op jit(solution)/shard_map/ppermute | solution.py:179
  64.4 2.0 %collective-permute-start.30 = (f32[4,1024]{1,0:T(4,128)S(1)}, f32[4,1024]{1,0:T(4,128)S(1)}, u32[]{:S(2)}, u32[]{:S(2)}) collective-permute-start(f32[4,1024]{1,0:T(4,128)S(1)} %get-tuple-element.90.own_ref), channel_id=1, source_target_pairs={{116,118},{131,135},{146,152},{161,169},{176,186},{235,237},{250,2... | collective-permute-start | bytes 49160 | tf_op jit(solution)/shard_map/ppermute | solution.py:179
  65.0 1.4 collective-permute-start.31
  65.7 0.7 collective-permute-start.29
  66.5 2.7 %collective-permute-start.32 = (f32[2,4,1024]{2,1,0:T(4,128)S(1)}, f32[2,4,1024]{2,1,0:T(4,128)S(1)}, u32[]{:S(2)}, u32[]{:S(2)}) collective-permute-start(f32[2,4,1024]{2,1,0:T(4,128)S(1)} %get-tuple-element.96), channel_id=1, source_target_pairs={{33,50},{118,135},{203,220}} | collective-permute-start | bytes 98312 | tf_op jit(solution)/shard_map/ppermute | solution.py:179
  67.1 2.0 %collective-permute-start.34 = (f32[4,1024]{1,0:T(4,128)S(1)}, f32[4,1024]{1,0:T(4,128)S(1)}, u32[]{:S(2)}, u32[]{:S(2)}) collective-permute-start(f32[4,1024]{1,0:T(4,128)S(1)} %get-tuple-element.94.own_ref), channel_id=1, source_target_pairs={{133,135},{148,152},{163,169},{178,186},{193,203},{208,220},{252,2... | collective-permute-start | bytes 49160 | tf_op jit(solution)/shard_map/ppermute | solution.py:179
  67.8 1.4 collective-permute-start.35
  68.5 0.7 collective-permute-start.33
  69.3 40.4 %collective-permute-start.36 = (f32[2,4,1024]{2,1,0:T(4,128)S(1)}, f32[2,4,1024]{2,1,0:T(4,128)S(1)}, u32[]{:S(2)}, u32[]{:S(2)}) collective-permute-start(f32[2,4,1024]{2,1,0:T(4,128)S(1)} %get-tuple-element.100), channel_id=1, source_target_pairs={{50,67},{135,152},{220,237}} | collective-permute-start | bytes 98312 | tf_op jit(solution)/shard_map/ppermute | solution.py:179
  69.9 39.0 %collective-permute-start.38 = (f32[4,1024]{1,0:T(4,128)S(1)}, f32[4,1024]{1,0:T(4,128)S(1)}, u32[]{:S(2)}, u32[]{:S(2)}) collective-permute-start(f32[4,1024]{1,0:T(4,128)S(1)} %get-tuple-element.98.own_ref), channel_id=1, source_target_pairs={{150,152},{165,169},{180,186},{195,203},{210,220},{225,237},{240,2... | collective-permute-start | bytes 49160 | tf_op jit(solution)/shard_map/ppermute | solution.py:179
  70.6 39.1 %collective-permute-start.39 = (f32[4,1024]{1,0:T(4,128)S(1)}, f32[4,1024]{1,0:T(4,128)S(1)}, u32[]{:S(2)}, u32[]{:S(2)}) collective-permute-start(f32[4,1024]{1,0:T(4,128)S(1)} %get-tuple-element.98.own_ref), channel_id=1, source_target_pairs={{149,152},{164,169},{179,186},{194,203},{209,220},{224,237}} | collective-permute-start | bytes 49160 | tf_op jit(solution)/shard_map/ppermute | solution.py:179
  108.2 1.4 collective-permute-start.37
  109.7 2.7 %collective-permute-start.40 = (f32[2,4,1024]{2,1,0:T(4,128)S(1)}, f32[2,4,1024]{2,1,0:T(4,128)S(1)}, u32[]{:S(2)}, u32[]{:S(2)}) collective-permute-start(f32[2,4,1024]{2,1,0:T(4,128)S(1)} %get-tuple-element.104), channel_id=1, source_target_pairs={{67,84},{152,169},{237,254}} | collective-permute-start | bytes 98312 | tf_op jit(solution)/shard_map/ppermute | solution.py:179
  110.4 2.0 %collective-permute-start.42 = (f32[4,1024]{1,0:T(4,128)S(1)}, f32[4,1024]{1,0:T(4,128)S(1)}, u32[]{:S(2)}, u32[]{:S(2)}) collective-permute-start(f32[4,1024]{1,0:T(4,128)S(1)} %get-tuple-element.102.own_ref), channel_id=1, source_target_pairs={{48,50},{167,169},{182,186},{197,203},{212,220},{227,237},{242,254}} | collective-permute-start | bytes 49160 | tf_op jit(solution)/shard_map/ppermute | solution.py:179
  111.0 1.4 collective-permute-start.43
  111.7 0.7 collective-permute-start.41
  112.5 9.4 %collective-permute-start.44 = (f32[2,4,1024]{2,1,0:T(4,128)S(1)}, f32[2,4,1024]{2,1,0:T(4,128)S(1)}, u32[]{:S(2)}, u32[]{:S(2)}) collective-permute-start(f32[2,4,1024]{2,1,0:T(4,128)S(1)} %get-tuple-element.108), channel_id=1, source_target_pairs={{1,16},{84,101},{169,186}} | collective-permute-start | bytes 98312 | tf_op jit(solution)/shard_map/ppermute | solution.py:179
  113.1 2.6 %collective-permute-start.46 = (f32[4,1024]{1,0:T(4,128)S(1)}, f32[4,1024]{1,0:T(4,128)S(1)}, u32[]{:S(2)}, u32[]{:S(2)}) collective-permute-start(f32[4,1024]{1,0:T(4,128)S(1)} %get-tuple-element.106.own_ref), channel_id=1, source_target_pairs={{65,67},{80,84},{184,186},{199,203},{214,220},{229,237},{244,254}} | collective-permute-start | bytes 49160 | tf_op jit(solution)/shard_map/ppermute | solution.py:179
  113.8 2.0 %collective-permute-start.47 = (f32[4,1024]{1,0:T(4,128)S(1)}, f32[4,1024]{1,0:T(4,128)S(1)}, u32[]{:S(2)}, u32[]{:S(2)}) collective-permute-start(f32[4,1024]{1,0:T(4,128)S(1)} %get-tuple-element.106.own_ref), channel_id=1, source_target_pairs={{64,67},{183,186},{198,203},{213,220},{228,237},{243,254}} | collective-permute-start | bytes 49160 | tf_op jit(solution)/shard_map/ppermute | solution.py:179
  114.5 7.4 %collective-permute-start.45 = (f32[4,1024]{1,0:T(4,128)S(1)}, f32[4,1024]{1,0:T(4,128)S(1)}, u32[]{:S(2)}, u32[]{:S(2)}) collective-permute-start(f32[4,1024]{1,0:T(4,128)S(1)} %get-tuple-element.109.value_ref), channel_id=1, source_target_pairs={{33,98},{48,144},{50,99},{64,160},{65,113},{80,176},{81,129},{82,1... | collective-permute-start | bytes 49160 | tf_op jit(solution)/shard_map/ppermute | solution.py:179
  121.9 2.7 %collective-permute-start.48 = (f32[2,4,1024]{2,1,0:T(4,128)S(1)}, f32[2,4,1024]{2,1,0:T(4,128)S(1)}, u32[]{:S(2)}, u32[]{:S(2)}) collective-permute-start(f32[2,4,1024]{2,1,0:T(4,128)S(1)} %get-tuple-element.112), channel_id=1, source_target_pairs={{16,33},{101,118},{186,203}} | collective-permute-start | bytes 98312 | tf_op jit(solution)/shard_map/ppermute | solution.py:179
  122.6 2.0 %collective-permute-start.50 = (f32[4,1024]{1,0:T(4,128)S(1)}, f32[4,1024]{1,0:T(4,128)S(1)}, u32[]{:S(2)}, u32[]{:S(2)}) collective-permute-start(f32[4,1024]{1,0:T(4,128)S(1)} %get-tuple-element.110.own_ref), channel_id=1, source_target_pairs={{82,84},{97,101},{112,118},{201,203},{216,220},{231,237},{246,254}} | collective-permute-start | bytes 49160 | tf_op jit(solution)/shard_map/ppermute | solution.py:179
  123.3 1.4 collective-permute-start.51
  124.0 0.7 collective-permute-start.49
  124.9 2.7 %collective-permute-start.52 = (f32[2,4,1024]{2,1,0:T(4,128)S(1)}, f32[2,4,1024]{2,1,0:T(4,128)S(1)}, u32[]{:S(2)}, u32[]{:S(2)}) collective-permute-start(f32[2,4,1024]{2,1,0:T(4,128)S(1)} %get-tuple-element.116), channel_id=1, source_target_pairs={{33,50},{118,135},{203,220}} | collective-permute-start | bytes 98312 | tf_op jit(solution)/shard_map/ppermute | solution.py:179
  125.6 2.0 %collective-permute-start.54 = (f32[4,1024]{1,0:T(4,128)S(1)}, f32[4,1024]{1,0:T(4,128)S(1)}, u32[]{:S(2)}, u32[]{:S(2)}) collective-permute-start(f32[4,1024]{1,0:T(4,128)S(1)} %get-tuple-element.114.own_ref), channel_id=1, source_target_pairs={{99,101},{114,118},{129,135},{144,152},{218,220},{233,237},{248,254}} | collective-permute-start | bytes 49160 | tf_op jit(solution)/shard_map/ppermute | solution.py:179
  126.2 1.4 collective-permute-start.55
  126.9 0.7 collective-permute-start.53
  127.7 2.7 %collective-permute-start.56 = (f32[2,4,1024]{2,1,0:T(4,128)S(1)}, f32[2,4,1024]{2,1,0:T(4,128)S(1)}, u32[]{:S(2)}, u32[]{:S(2)}) collective-permute-start(f32[2,4,1024]{2,1,0:T(4,128)S(1)} %get-tuple-element.120), channel_id=1, source_target_pairs={{50,67},{135,152},{220,237}} | collective-permute-start | bytes 98312 | tf_op jit(solution)/shard_map/ppermute | solution.py:179
  128.4 2.0 %collective-permute-start.58 = (f32[4,1024]{1,0:T(4,128)S(1)}, f32[4,1024]{1,0:T(4,128)S(1)}, u32[]{:S(2)}, u32[]{:S(2)}) collective-permute-start(f32[4,1024]{1,0:T(4,128)S(1)} %get-tuple-element.118.own_ref), channel_id=1, source_target_pairs={{116,118},{131,135},{146,152},{161,169},{176,186},{235,237},{250,2... | collective-permute-start | bytes 49160 | tf_op jit(solution)/shard_map/ppermute | solution.py:179
  129.0 1.4 collective-permute-start.59
  129.7 0.7 collective-permute-start.57
  130.5 2.7 %collective-permute-start.60 = (f32[2,4,1024]{2,1,0:T(4,128)S(1)}, f32[2,4,1024]{2,1,0:T(4,128)S(1)}, u32[]{:S(2)}, u32[]{:S(2)}) collective-permute-start(f32[2,4,1024]{2,1,0:T(4,128)S(1)} %get-tuple-element.124), channel_id=1, source_target_pairs={{67,84},{152,169},{237,254}} | collective-permute-start | bytes 98312 | tf_op jit(solution)/shard_map/ppermute | solution.py:179
  131.1 2.0 %collective-permute-start.62 = (f32[4,1024]{1,0:T(4,128)S(1)}, f32[4,1024]{1,0:T(4,128)S(1)}, u32[]{:S(2)}, u32[]{:S(2)}) collective-permute-start(f32[4,1024]{1,0:T(4,128)S(1)} %get-tuple-element.122.own_ref), channel_id=1, source_target_pairs={{133,135},{148,152},{163,169},{178,186},{193,203},{208,220},{252,2... | collective-permute-start | bytes 49160 | tf_op jit(solution)/shard_map/ppermute | solution.py:179
  131.8 1.4 collective-permute-start.63
  132.5 0.7 collective-permute-start.61
  135.3 44.6 %all-to-all-start = ((f32[16,4,1152]{2,1,0:T(4,128)}), f32[16,4,1152]{2,1,0:T(4,128)S(1)}, u32[]{:S(2)}, u32[]{:S(2)}) async-start(f32[16,4,1152]{2,1,0:T(4,128)} %broadcast_in_dim.46), calls=%async_computation | async-start | bytes 589824 | tf_op jit(solution)/shard_map/all_to_all | solution.py:235
  (4 other events, 15.6 us)

commit v4 on v3

--- a/solution.py
+++ b/solution.py
@@ -13,12 +13,11 @@
 COL = ("col_x", "col_y")
 BOTH = (ROW, *COL)
 SIDE = 4
-BAND = 2
-CHAIN_PERIOD = 5
-SPREAD_PERIOD = 7
-FAR_PERIOD = 7
-ARRIVAL = {3: 0, 4: 1, 5: 1, 6: 2, 7: 2, 8: 2, 9: 3, 10: 3, 11: 3, 12: 3, 13: 3, 14: 3, 15: 4}
-SENDER = {3: 1, 4: 1, 5: 3, 6: 3, 7: 4, 8: 5, 9: 3, 10: 4, 11: 5, 12: 6, 13: 7, 14: 8, 15: 3}
+BAND = 3
+CHAIN_PERIOD = 13
+FAR_PERIOD = 6
+ARRIVAL = {4: 1, 5: 2, 6: 2, 7: 3, 8: 3, 9: 3, 10: 4, 11: 4, 12: 4, 13: 4, 14: 4, 15: 4}
+SENDER = {4: 1, 5: 1, 6: 4, 7: 4, 8: 5, 9: 6, 10: 4, 11: 5, 12: 6, 13: 7, 14: 8, 15: 9}
 
 
 def solver(i):
@@ -35,25 +34,19 @@
 
 
 def plan(n):
-    chain, spread, odd, even = [], [], [], []
+    chain, odd, even = [], [], []
     for r in range(n - 1):
         chain.append([(solver(r), solver(r + 1))])
-        spread.append([])
         odd.append([])
         even.append([])
         for i in range(n):
             for j in range(i - BAND):
                 d = i - j
                 if j + ARRIVAL[d] == r:
-                    spread[r].append((solver(j) if SENDER[d] == 1 else (j + SENDER[d], j), (i, j)))
-                if i - 2 - (d - 3) // 2 == r:
+                    chain[r].append((solver(j) if SENDER[d] == 1 else (j + SENDER[d], j), (i, j)))
+                if i - 2 - (d - 4) // 2 == r:
                     (odd if d % 2 else even)[r].append(((i, j), solver(i)))
-    return (
-        union(chain, CHAIN_PERIOD),
-        union(spread, SPREAD_PERIOD),
-        union(odd, FAR_PERIOD),
-        union(even, FAR_PERIOD),
-    )
+    return union(chain, CHAIN_PERIOD), union(odd, FAR_PERIOD), union(even, FAR_PERIOD)
 
 
 def assemble(place, block, parts):
@@ -79,14 +72,14 @@
     )(place, block, *parts)
 
 
-def step(now, came, heard, odds, evens, value, own, pending, source, v_band, u_band, inverse):
-    held = 1 if now < 1 else BAND
+def step(now, came, odds, evens, send, own, pending, source, v_band, u_band, inverse):
+    held = max(1, min(BAND, now + 1))
     nrhs, width = source.shape
     block = 256
 
-    def body(came_ref, heard_ref, odds_ref, evens_ref, value_ref, own_ref, pending_ref, source_ref, *refs):
+    def body(came_ref, odds_ref, evens_ref, send_ref, own_ref, pending_ref, source_ref, *refs):
         v_refs, u_refs = refs[:held], refs[held : 2 * held]
-        inverse_ref, bundle_out, value_out, own_out, pending_out = refs[2 * held :]
+        inverse_ref, send_out, own_out, pending_out = refs[2 * held :]
         row = lax.axis_index(ROW)
         col = lax.axis_index(COL[0]) * SIDE + lax.axis_index(COL[1])
         gap = row - col
@@ -101,10 +94,10 @@
         behind = row - 1 - now
         adds = (gap == 1) & (behind >= 0)
         left = pending_ref[...]
-        if now >= 2:
-            left = left + jnp.where(adds & (3 + 2 * behind <= row), odds_ref[...], 0.0)
         if now >= 3:
             left = left + jnp.where(adds & (4 + 2 * behind <= row), evens_ref[...], 0.0)
+        if now >= 4:
+            left = left + jnp.where(adds & (5 + 2 * behind <= row), odds_ref[...], 0.0)
         pending_out[...] = left
 
         def share(known, d):
@@ -113,15 +106,20 @@
             )
             return jnp.dot(inner.astype(jnp.bfloat16), u_refs[d][...], preferred_element_type=jnp.float32)
 
+        @pl.when(jnp.logical_not(turn))
+        def _():
+            send_out[1] = jnp.zeros((nrhs, width), jnp.float32)
+            send_out[2] = jnp.zeros((nrhs, width), jnp.float32)
+
         @pl.when(jnp.logical_not(turn | hears))
         def _():
-            value_out[...] = value_ref[...]
+            send_out[0] = send_ref[0]
             own_out[...] = own_ref[...]
 
         @pl.when(hears)
         def _():
-            value_out[...] = heard_ref[...]
-            own_out[...] = share(heard_ref[...], 0)
+            send_out[0] = came_ref[0]
+            own_out[...] = share(came_ref[0], 0)
 
         @pl.when(turn)
         def _():
@@ -129,9 +127,6 @@
             if now >= 0:
                 for d in range(held):
                     total = total - share(came_ref[d], d)
-                bundle_out[1] = came_ref[0]
-            else:
-                bundle_out[1] = jnp.zeros((nrhs, width), jnp.float32)
             reduced = total.astype(jnp.bfloat16)
             columns = []
             for n in range(0, width, block):
@@ -142,21 +137,21 @@
                         preferred_element_type=jnp.float32,
                     )
                 )
-            result = jnp.concatenate(columns, axis=1)
-            bundle_out[0] = result
-            value_out[...] = result
+            send_out[0] = jnp.concatenate(columns, axis=1)
+            for d in range(1, BAND):
+                send_out[d] = came_ref[d - 1] if now >= 0 else jnp.zeros((nrhs, width), jnp.float32)
             own_out[...] = own_ref[...]
 
     vmem = pl.BlockSpec(memory_space=pltpu.VMEM)
     small = jax.ShapeDtypeStruct((nrhs, width), jnp.float32)
     return pl.pallas_call(
         body,
-        in_specs=[vmem] * (8 + 2 * held + 1),
-        out_specs=[vmem] * 4,
-        out_shape=[jax.ShapeDtypeStruct((BAND, nrhs, width), jnp.float32), small, small, small],
+        in_specs=[vmem] * (7 + 2 * held + 1),
+        out_specs=[vmem] * 3,
+        out_shape=[jax.ShapeDtypeStruct((BAND, nrhs, width), jnp.float32), small, small],
         compiler_params=pltpu.CompilerParams(vmem_limit_bytes=8 * 2**20),
         name="step",
-    )(came, heard, odds, evens, value, own, pending, source, *v_band[:held], *u_band[:held], inverse)
+    )(came, odds, evens, send, own, pending, source, *v_band[:held], *u_band[:held], inverse)
 
 
 def local(right_side, inverse_t, u_factor, v_factor, ranks):
@@ -202,33 +197,33 @@
         parts.append(move(block[:, k * quarter :], pairs))
     place = jnp.stack([col // SIDE]).astype(jnp.int32)
 
-    second = move(both, [((i, i - 2), solver(i)) for i in range(2, n)])
+    v_band, u_band = [v_tile], [u_tile]
+    moved = []
+    for d in range(2, BAND + 1):
+        moved.append(move(both, [((i, i - d), solver(i)) for i in range(d, n)]))
     inverse = assemble(place, block, parts)
-    second = (second + jnp.where(gap == 1, 0.0, both)).astype(jnp.bfloat16)
-    v_band = [v_tile, second[:rank_max]]
-    u_band = [u_tile, second[rank_max:]]
-
-    chain, spread, odd, even = plan(n)
+    for tile in moved:
+        tile = (tile + jnp.where(gap == 1, 0.0, both)).astype(jnp.bfloat16)
+        v_band.append(tile[:rank_max])
+        u_band.append(tile[rank_max:])
+
+    chain, odd, even = plan(n)
     nothing = jnp.zeros((nrhs, width), jnp.float32)
-    no_bundle = jnp.zeros((BAND, nrhs, width), jnp.float32)
-    bundle, value, own, pending = step(
-        -1, no_bundle, nothing, nothing, nothing, nothing, nothing, nothing, source, v_band, u_band, inverse
-    )
+    came = jnp.zeros((BAND, nrhs, width), jnp.float32)
+    send, own, pending = step(-1, came, nothing, nothing, came, nothing, nothing, source, v_band, u_band, inverse)
     odds = evens = nothing
     for r in range(n - 1):
-        came = move(bundle, chain[r])
-        heard = more_odds = more_evens = nothing
-        if spread[r]:
-            heard = move(value, spread[r])
-        if 1 <= r < n - 2:
+        came = move(send, chain[r])
+        more_odds = more_evens = nothing
+        if odd[r] and 3 <= r < n - 2:
             more_odds = move(own, odd[r])
-        if 2 <= r < n - 2:
+        if even[r] and 2 <= r < n - 2:
             more_evens = move(own, even[r])
-        bundle, value, own, pending = step(
-            r, came, heard, odds, evens, value, own, pending, source, v_band, u_band, inverse
+        send, own, pending = step(
+            r, came, odds, evens, send, own, pending, source, v_band, u_band, inverse
         )
         odds, evens = more_odds, more_evens
-    result = value
+    result = send[0]
 
     payload = jnp.concatenate([result, jnp.broadcast_to(log_sum, (nrhs, 128))], axis=1)
     payload = jnp.broadcast_to(payload[None], (n_col, *payload.shape))

time: 185 us -> 190 us (1.027)
  starting transfers between devices: 121 us -> 126 us
  waiting for transfers between devices: 41.3 us -> 44 us
    ppermute x64 -> x48, starting transfers between devices: 85.4 us -> 120 us  [move(): return lax.ppermute(array, BOTH, numbered)]
    all_to_all x1, starting transfers between devices: 35.8 us -> 5.79 us  [local(): arrived = lax.all_to_all(payload, COL, 0, 0, tiled=True)]
    ppermute x64 -> x48, waiting for transfers between devices: 32.5 us -> 35.3 us  [move(): return lax.ppermute(array, BOTH, numbered)]
  transfers between devices with their start and end apart: 65 -> 49, of which waited for: 4 -> 4; matrix products, arithmetic and copies ran while one was open for 5% -> 5% of each run, Pallas kernels for 1% -> 1%
where the time goes in v4:
time: 190 us; the launch traced here: 189 us
  starting transfers between devices  126 us (66%)
  waiting for transfers between devices  44 us (23%)
  other arithmetic  9.1 us (5%)
  local copies, waits for them, and re-layouts  4.28 us (2%)
  Pallas kernels  3.25 us (2%)
  between operations  2.89 us (2%)
    ppermute x48, starting transfers between devices, move(): return lax.ppermute(array, BOTH, numbered)  120 us
    ppermute x48, waiting for transfers between devices, move(): return lax.ppermute(array, BOTH, numbered)  35.3 us
    all_to_all x1, waiting for transfers between devices, local(): arrived = lax.all_to_all(payload, COL, 0, 0, tiled=True)  8.66 us
    all_to_all x1, starting transfers between devices, local(): arrived = lax.all_to_all(payload, COL, 0, 0, tiled=True)  5.79 us
  transfers between devices with their start and end apart: 49, of which 4 were waited for; matrix products, arithmetic and copies ran while one was open for 5% of the time, Pallas kernels for 1%

profile of v4, /device:TPU:224, one launch (start us, length us, event | category | flops | bytes accessed | tf_op | source)
XLA Modules:
  0.0 189.3 jit_solution(11827883339833824331)
XLA Ops:
  0.6 1.0 fusion.2
  1.6 3.5 %collective-permute-start = (f32[64,1024]{1,0:T(8,128)S(1)}, f32[64,1024]{1,0:T(8,128)S(1)}, u32[]{:S(2)}, u32[]{:S(2)}) collective-permute-start(f32[64,1024]{1,0:T(8,128)S(1)} %get-tuple-element.107), channel_id=1, source_target_pairs={{0,1},{4,5},{8,9},{12,13},{32,33},{36,37},{40,41},{44,45},{48,50},... | collective-permute-start | bytes 786440 | tf_op jit(solution)/shard_map/ppermute | solution.py:174
  5.2 0.7 collective-permute-start.1
  5.8 0.7 collective-permute-start.2
  6.5 0.7 collective-permute-start.3
  8.0 1.0 bitcast_select_fusion.refs_1_.refs_2_.refs_3_
  9.0 0.8 gather_fusion
  9.8 0.7 log_reduce_fusion
  10.5 2.1 %maximum_convert_fusion = f32[256,1024]{1,0:T(8,128)} fusion(bf16[128,1024]{1,0:T(8,128)(2,1)S(1)} %bitcast_select_fusion.refs_1_.refs_2_.refs_3_, bf16[128,1024]{1,0:T(8,128)(2,1)} %bitcast.29), kind=kLoop, calls=%fused_computation.4 | loop fusion | flops 1048576 | bytes 1572864 | tf_op jit(solution)/shard_map/convert_element_type | solution.py:190
  12.8 0.7 collective-permute-start.4
  13.6 1.6 collective-permute-start.10
  15.2 1.7 collective-permute-start.12
  16.9 0.7 collective-permute-start.7
  17.6 0.9 slice.30
  18.5 0.7 collective-permute-start.5
  19.2 0.9 slice.31
  20.1 1.5 collective-permute-start.6
  21.6 1.4 assemble.1.refs_2_.refs_4_.refs_6_
  23.1 0.7 collective-permute-start.8
  23.8 2.2 %add_convert_fusion = (bf16[256,1024]{1,0:T(8,128)(2,1)S(1)}, bf16[256,1024]{1,0:T(8,128)(2,1)S(1)}) fusion(f32[256,1024]{1,0:T(8,128)} %collective-permute-done.12, f32[256,1024]{1,0:T(8,128)} %maximum_convert_fusion, pred[]{:T(512)S(6)} %eq.28, f32[256,1024]{1,0:T(8,128)} %collective-permute-done.10), kind=kLoop, calls=%fused_computation.2 | loop fusion | flops 1310720 | bytes 4194305 | tf_op jit(solution)/shard_map/convert_element_type | solution.py:206
  26.1 0.7 collective-permute-start.9
  26.9 0.7 collective-permute-start.11
  27.7 0.7 collective-permute-start.13
  28.4 0.7 collective-permute-start.14
  29.1 1.3 collective-permute-start.15
  30.4 0.7 collective-permute-start.16
  31.1 0.7 collective-permute-start.17
  31.8 32.4 %collective-permute-done.15.came_ref = f32[3,4,1024]{2,1,0:T(4,128)S(1)} collective-permute-done((f32[3,4,1024]{2,1,0:T(4,128)S(1)}, f32[3,4,1024]{2,1,0:T(4,128)S(1)}, u32[]{:S(2)}, u32[]{:S(2)}) %collective-permute-start.15) | collective-permute-done | bytes 49184 | tf_op jit(solution)/shard_map/ppermute | solution.py:174
  64.5 0.7 collective-permute-start.18
  65.2 0.7 collective-permute-start.19
  65.9 0.7 collective-permute-start.20
  66.7 0.7 collective-permute-start.21
  67.3 0.7 collective-permute-start.22
  68.0 0.7 collective-permute-start.23
  68.8 0.7 collective-permute-start.24
  69.4 0.7 collective-permute-start.25
  70.1 0.7 collective-permute-start.26
  70.9 0.7 collective-permute-start.27
  71.5 0.7 collective-permute-start.28
  72.2 36.2 %collective-permute-start.29 = (f32[4,1024]{1,0:T(4,128)S(1)}, f32[4,1024]{1,0:T(4,128)S(1)}, u32[]{:S(2)}, u32[]{:S(2)}) collective-permute-start(f32[4,1024]{1,0:T(4,128)S(1)} %get-tuple-element.75.own_ref), channel_id=1, source_target_pairs={{149,152},{164,169},{179,186},{194,203},{209,220},{224,237},{251,2... | collective-permute-start | bytes 49160 | tf_op jit(solution)/shard_map/ppermute | solution.py:174
  108.4 1.4 collective-permute-done.29.evens_ref
  109.8 0.7 collective-permute-start.30
  110.5 0.7 collective-permute-start.31
  111.2 0.7 collective-permute-start.32
  112.0 0.7 collective-permute-start.33
  112.6 0.7 collective-permute-start.34
  113.3 0.7 collective-permute-start.35
  114.2 0.7 collective-permute-start.36
  114.9 0.7 collective-permute-start.37
  115.6 0.7 collective-permute-start.38
  116.3 0.7 collective-permute-start.39
  117.0 0.7 collective-permute-start.40
  118.4 0.7 collective-permute-start.42
  119.1 0.7 collective-permute-start.43
  119.8 0.7 collective-permute-start.44
  120.5 0.7 collective-permute-start.45
  121.2 0.7 collective-permute-start.46
  121.9 46.9 %collective-permute-start.47 = (f32[4,1024]{1,0:T(4,128)S(1)}, f32[4,1024]{1,0:T(4,128)S(1)}, u32[]{:S(2)}, u32[]{:S(2)}) collective-permute-start(f32[4,1024]{1,0:T(4,128)S(1)} %get-tuple-element.93.own_ref), channel_id=1, source_target_pairs={{149,152},{164,169},{179,186},{194,203},{209,220},{224,237},{251,2... | collective-permute-start | bytes 49160 | tf_op jit(solution)/shard_map/ppermute | solution.py:174
  168.8 1.4 collective-permute-done.47.evens_ref
  170.9 0.7 concatenate.16
  171.6 0.7 broadcast_in_dim.47
  172.3 5.8 %all-to-all-start = ((f32[16,4,1152]{2,1,0:T(4,128)}), f32[16,4,1152]{2,1,0:T(4,128)S(1)}, u32[]{:S(2)}, u32[]{:S(2)}) async-start(f32[16,4,1152]{2,1,0:T(4,128)} %broadcast_in_dim.47), calls=%async_computation | async-start | bytes 589824 | tf_op jit(solution)/shard_map/all_to_all | solution.py:230
  178.1 8.7 %all-to-all-done = f32[16,4,1152]{2,1,0:T(4,128)S(1)} async-done(((f32[16,4,1152]{2,1,0:T(4,128)}), f32[16,4,1152]{2,1,0:T(4,128)S(1)}, u32[]{:S(2)}, u32[]{:S(2)}) %all-to-all-start) | async-done | bytes 294944 | tf_op jit(solution)/shard_map/all_to_all | solution.py:230
  186.8 0.7 multiply_reduce_fusion
  (82 shorter events, 4.2 us)
Async XLA Ops:
  0.6 12.0 %copy-start.2 = (bf16[1,1,64,1024]{3,2,1,0:T(8,128)(2,1)S(1)}, bf16[1,1,64,1024]{3,2,1,0:T(8,128)(2,1)}, u32[]{:S(2)}) copy-start(bf16[1,1,64,1024]{3,2,1,0:T(8,128)(2,1)} %param.6) | copy-start | bytes 393220
  1.6 11.0 %collective-permute-start = (f32[64,1024]{1,0:T(8,128)S(1)}, f32[64,1024]{1,0:T(8,128)S(1)}, u32[]{:S(2)}, u32[]{:S(2)}) collective-permute-start(f32[64,1024]{1,0:T(8,128)S(1)} %get-tuple-element.107), channel_id=1, source_target_pairs={{0,1},{4,5},{8,9},{12,13},{32,33},{36,37},{40,41},{44,45},{48,50},... | collective-permute-start | bytes 786440 | tf_op jit(solution)/shard_map/ppermute | solution.py:174
  5.2 7.5 %collective-permute-start.1 = (f32[64,1024]{1,0:T(8,128)S(1)}, f32[64,1024]{1,0:T(8,128)S(1)}, u32[]{:S(2)}, u32[]{:S(2)}) collective-permute-start(f32[64,1024]{1,0:T(8,128)S(1)} %get-tuple-element.107), channel_id=1, source_target_pairs={{17,16},{21,20},{25,24},{29,28},{49,50},{53,54},{57,58},{61,62},{6... | collective-permute-start | bytes 786440 | tf_op jit(solution)/shard_map/ppermute | solution.py:174
  5.8 6.8 %collective-permute-start.2 = (f32[64,1024]{1,0:T(8,128)S(1)}, f32[64,1024]{1,0:T(8,128)S(1)}, u32[]{:S(2)}, u32[]{:S(2)}) collective-permute-start(f32[64,1024]{1,0:T(8,128)S(1)} %get-tuple-element.107), channel_id=1, source_target_pairs={{2,1},{6,5},{10,9},{14,13},{18,16},{22,20},{26,24},{30,28},{34,33}... | collective-permute-start | bytes 786440 | tf_op jit(solution)/shard_map/ppermute | solution.py:174
  6.5 6.1 %collective-permute-start.3 = (f32[64,1024]{1,0:T(8,128)S(1)}, f32[64,1024]{1,0:T(8,128)S(1)}, u32[]{:S(2)}, u32[]{:S(2)}) collective-permute-start(f32[64,1024]{1,0:T(8,128)S(1)} %get-tuple-element.107), channel_id=1, source_target_pairs={{3,1},{7,5},{11,9},{15,13},{19,16},{23,20},{27,24},{31,28},{35,33}... | collective-permute-start | bytes 786440 | tf_op jit(solution)/shard_map/ppermute | solution.py:174
  12.8 8.8 %collective-permute-start.4 = (f32[256,1024]{1,0:T(8,128)S(1)}, f32[256,1024]{1,0:T(8,128)S(1)}, u32[]{:S(2)}, u32[]{:S(2)}) collective-permute-start(f32[256,1024]{1,0:T(8,128)S(1)} %pad_maximum_fusion.block_ref), channel_id=1, source_target_pairs={{80,84},{97,101},{114,118},{131,135},{144,152},{161,169},{178,186}... | collective-permute-start | bytes 3145736 | tf_op jit(solution)/shard_map/ppermute | solution.py:174
  13.6 10.2 %collective-permute-start.10 = (f32[256,1024]{1,0:T(8,128)}, f32[256,1024]{1,0:T(8,128)}, u32[]{:S(2)}, u32[]{:S(2)}) collective-permute-start(f32[256,1024]{1,0:T(8,128)} %maximum_convert_fusion), channel_id=1, source_target_pairs={{32,33},{49,50},{66,67},{83,84},{100,101},{117,118},{134,135},{151... | collective-permute-start | bytes 3145736 | tf_op jit(solution)/shard_map/ppermute | solution.py:174
  15.2 8.6 %collective-permute-start.12 = (f32[256,1024]{1,0:T(8,128)}, f32[256,1024]{1,0:T(8,128)}, u32[]{:S(2)}, u32[]{:S(2)}) collective-permute-start(f32[256,1024]{1,0:T(8,128)} %maximum_convert_fusion), channel_id=1, source_target_pairs={{48,50},{65,67},{82,84},{99,101},{116,118},{133,135},{150,152},{16... | collective-permute-start | bytes 3145736 | tf_op jit(solution)/shard_map/ppermute | solution.py:174
  16.9 3.2 %collective-permute-start.7 = (f32[256,256]{1,0:T(8,128)S(1)}, f32[256,256]{1,0:T(8,128)S(1)}, u32[]{:S(2)}, u32[]{:S(2)}) collective-permute-start(f32[256,256]{1,0:T(8,128)S(1)} %slice.32), channel_id=1, source_target_pairs={{13,1},{28,16},{45,33},{62,50},{79,67},{92,84},{109,101},{126,118}... | collective-permute-start | bytes 786440 | tf_op jit(solution)/shard_map/ppermute | solution.py:174
  18.5 3.1 %collective-permute-start.5 = (f32[256,768]{1,0:T(8,128)}, f32[256,768]{1,0:T(8,128)S(1)}, u32[]{:S(2)}, u32[]{:S(2)}) collective-permute-start(f32[256,768]{1,0:T(8,128)} %slice.30), channel_id=1, source_target_pairs={{5,1},{20,16},{37,33},{54,50},{71,67},{148,152},{165,169},{182,186... | collective-permute-start | bytes 2359304 | tf_op jit(solution)/shard_map/ppermute | solution.py:174
  20.1 1.5 collective-permute-start.6
  21.6 1.5 copy-start
  21.6 1.5 copy-start.1
  23.1 2.9 %collective-permute-start.8 = (f32[3,4,1024]{2,1,0:T(4,128)S(1)}, f32[3,4,1024]{2,1,0:T(4,128)S(1)}, u32[]{:S(2)}, u32[]{:S(2)}) collective-permute-start(f32[3,4,1024]{2,1,0:T(4,128)S(1)} %get-tuple-element.52.send_ref), channel_id=1, source_target_pairs={{1,16},{220,237}} | collective-permute-start | bytes 147464 | tf_op jit(solution)/shard_map/ppermute | solution.py:174
  26.1 0.7 collective-permute-start.9
  26.9 0.7 collective-permute-start.11
  27.7 1.4 collective-permute-start.13
  28.4 0.7 collective-permute-start.14
  29.1 35.0 %collective-permute-start.15 = (f32[3,4,1024]{2,1,0:T(4,128)S(1)}, f32[3,4,1024]{2,1,0:T(4,128)S(1)}, u32[]{:S(2)}, u32[]{:S(2)}) collective-permute-start(f32[3,4,1024]{2,1,0:T(4,128)S(1)} %get-tuple-element.65.send_ref), channel_id=1, source_target_pairs={{33,114},{50,115},{64,160},{67,84},{80,176},{81,129},{96,192},{97,... | collective-permute-start | bytes 147464 | tf_op jit(solution)/shard_map/ppermute | solution.py:174
  30.4 1.3 collective-permute-start.16
  31.1 0.7 collective-permute-start.17
  64.5 2.0 %collective-permute-start.18 = (f32[3,4,1024]{2,1,0:T(4,128)S(1)}, f32[3,4,1024]{2,1,0:T(4,128)S(1)}, u32[]{:S(2)}, u32[]{:S(2)}) collective-permute-start(f32[3,4,1024]{2,1,0:T(4,128)S(1)} %get-tuple-element.68.send_ref), channel_id=1, source_target_pairs={{50,131},{67,132},{81,177},{84,101},{97,193},{98,146},{113,209},{1... | collective-permute-start | bytes 147464 | tf_op jit(solution)/shard_map/ppermute | solution.py:174
  65.2 1.3 collective-permute-start.19
  65.9 0.7 collective-permute-start.20
  66.7 2.0 %collective-permute-start.21 = (f32[3,4,1024]{2,1,0:T(4,128)S(1)}, f32[3,4,1024]{2,1,0:T(4,128)S(1)}, u32[]{:S(2)}, u32[]{:S(2)}) collective-permute-start(f32[3,4,1024]{2,1,0:T(4,128)S(1)} %get-tuple-element.71.send_ref), channel_id=1, source_target_pairs={{67,148},{84,149},{98,194},{101,118},{114,210},{115,163},{130,226}... | collective-permute-start | bytes 147464 | tf_op jit(solution)/shard_map/ppermute | solution.py:174
  67.3 1.3 collective-permute-start.22
  68.0 0.7 collective-permute-start.23
  68.8 2.0 %collective-permute-start.24 = (f32[3,4,1024]{2,1,0:T(4,128)S(1)}, f32[3,4,1024]{2,1,0:T(4,128)S(1)}, u32[]{:S(2)}, u32[]{:S(2)}) collective-permute-start(f32[3,4,1024]{2,1,0:T(4,128)S(1)} %get-tuple-element.74.send_ref), channel_id=1, source_target_pairs={{84,165},{101,166},{115,211},{118,135},{131,227},{132,180},{147,24... | collective-permute-start | bytes 147464 | tf_op jit(solution)/shard_map/ppermute | solution.py:174
  69.4 1.3 collective-permute-start.25
  70.1 0.7 collective-permute-start.26
  70.9 39.0 %collective-permute-start.27 = (f32[3,4,1024]{2,1,0:T(4,128)S(1)}, f32[3,4,1024]{2,1,0:T(4,128)S(1)}, u32[]{:S(2)}, u32[]{:S(2)}) collective-permute-start(f32[3,4,1024]{2,1,0:T(4,128)S(1)} %get-tuple-element.77.send_ref), channel_id=1, source_target_pairs={{101,182},{118,183},{132,228},{135,152},{148,244},{149,197},{165,2... | collective-permute-start | bytes 147464 | tf_op jit(solution)/shard_map/ppermute | solution.py:174
  71.5 36.9 %collective-permute-start.28 = (f32[4,1024]{1,0:T(4,128)S(1)}, f32[4,1024]{1,0:T(4,128)S(1)}, u32[]{:S(2)}, u32[]{:S(2)}) collective-permute-start(f32[4,1024]{1,0:T(4,128)S(1)} %get-tuple-element.75.own_ref), channel_id=1, source_target_pairs={{148,152},{163,169},{178,186},{193,203},{208,220},{250,254}} | collective-permute-start | bytes 49160 | tf_op jit(solution)/shard_map/ppermute | solution.py:174
  72.2 37.6 %collective-permute-start.29 = (f32[4,1024]{1,0:T(4,128)S(1)}, f32[4,1024]{1,0:T(4,128)S(1)}, u32[]{:S(2)}, u32[]{:S(2)}) collective-permute-start(f32[4,1024]{1,0:T(4,128)S(1)} %get-tuple-element.75.own_ref), channel_id=1, source_target_pairs={{149,152},{164,169},{179,186},{194,203},{209,220},{224,237},{251,2... | collective-permute-start | bytes 49160 | tf_op jit(solution)/shard_map/ppermute | solution.py:174
  109.8 2.0 %collective-permute-start.30 = (f32[3,4,1024]{2,1,0:T(4,128)S(1)}, f32[3,4,1024]{2,1,0:T(4,128)S(1)}, u32[]{:S(2)}, u32[]{:S(2)}) collective-permute-start(f32[3,4,1024]{2,1,0:T(4,128)S(1)} %get-tuple-element.80.send_ref), channel_id=1, source_target_pairs={{118,199},{135,200},{149,245},{152,169},{166,214},{182,230},{183,2... | collective-permute-start | bytes 147464 | tf_op jit(solution)/shard_map/ppermute | solution.py:174
  110.5 1.3 collective-permute-start.31
  111.2 0.7 collective-permute-start.32
  112.0 2.0 %collective-permute-start.33 = (f32[3,4,1024]{2,1,0:T(4,128)S(1)}, f32[3,4,1024]{2,1,0:T(4,128)S(1)}, u32[]{:S(2)}, u32[]{:S(2)}) collective-permute-start(f32[3,4,1024]{2,1,0:T(4,128)S(1)} %get-tuple-element.83.send_ref), channel_id=1, source_target_pairs={{135,216},{152,217},{169,186},{183,231},{199,247},{200,232}} | collective-permute-start | bytes 147464 | tf_op jit(solution)/shard_map/ppermute | solution.py:174
  112.6 1.3 collective-permute-start.34
  113.3 0.7 collective-permute-start.35
  114.2 2.0 %collective-permute-start.36 = (f32[3,4,1024]{2,1,0:T(4,128)S(1)}, f32[3,4,1024]{2,1,0:T(4,128)S(1)}, u32[]{:S(2)}, u32[]{:S(2)}) collective-permute-start(f32[3,4,1024]{2,1,0:T(4,128)S(1)} %get-tuple-element.86.send_ref), channel_id=1, source_target_pairs={{152,233},{169,234},{186,203},{200,248},{217,249}} | collective-permute-start | bytes 147464 | tf_op jit(solution)/shard_map/ppermute | solution.py:174
  114.9 1.3 collective-permute-start.37
  115.6 0.7 collective-permute-start.38
  116.3 2.0 %collective-permute-start.39 = (f32[3,4,1024]{2,1,0:T(4,128)S(1)}, f32[3,4,1024]{2,1,0:T(4,128)S(1)}, u32[]{:S(2)}, u32[]{:S(2)}) collective-permute-start(f32[3,4,1024]{2,1,0:T(4,128)S(1)} %get-tuple-element.89.send_ref), channel_id=1, source_target_pairs={{169,250},{186,251},{203,220}} | collective-permute-start | bytes 147464 | tf_op jit(solution)/shard_map/ppermute | solution.py:174
  117.0 1.3 collective-permute-start.40
  117.7 0.7 collective-permute-start.41
  118.4 2.0 %collective-permute-start.42 = (f32[3,4,1024]{2,1,0:T(4,128)S(1)}, f32[3,4,1024]{2,1,0:T(4,128)S(1)}, u32[]{:S(2)}, u32[]{:S(2)}) collective-permute-start(f32[3,4,1024]{2,1,0:T(4,128)S(1)} %get-tuple-element.92.send_ref), channel_id=1, source_target_pairs={{1,16},{220,237}} | collective-permute-start | bytes 147464 | tf_op jit(solution)/shard_map/ppermute | solution.py:174
  119.1 1.3 collective-permute-start.43
  119.8 0.7 collective-permute-start.44
  120.5 49.7 %collective-permute-start.45 = (f32[3,4,1024]{2,1,0:T(4,128)S(1)}, f32[3,4,1024]{2,1,0:T(4,128)S(1)}, u32[]{:S(2)}, u32[]{:S(2)}) collective-permute-start(f32[3,4,1024]{2,1,0:T(4,128)S(1)} %get-tuple-element.95.send_ref), channel_id=1, source_target_pairs={{1,64},{16,33},{237,254}} | collective-permute-start | bytes 147464 | tf_op jit(solution)/shard_map/ppermute | solution.py:174
  121.2 47.6 %collective-permute-start.46 = (f32[4,1024]{1,0:T(4,128)S(1)}, f32[4,1024]{1,0:T(4,128)S(1)}, u32[]{:S(2)}, u32[]{:S(2)}) collective-permute-start(f32[4,1024]{1,0:T(4,128)S(1)} %get-tuple-element.93.own_ref), channel_id=1, source_target_pairs={{148,152},{163,169},{178,186},{193,203},{208,220},{250,254}} | collective-permute-start | bytes 49160 | tf_op jit(solution)/shard_map/ppermute | solution.py:174
  121.9 48.3 %collective-permute-start.47 = (f32[4,1024]{1,0:T(4,128)S(1)}, f32[4,1024]{1,0:T(4,128)S(1)}, u32[]{:S(2)}, u32[]{:S(2)}) collective-permute-start(f32[4,1024]{1,0:T(4,128)S(1)} %get-tuple-element.93.own_ref), channel_id=1, source_target_pairs={{149,152},{164,169},{179,186},{194,203},{209,220},{224,237},{251,2... | collective-permute-start | bytes 49160 | tf_op jit(solution)/shard_map/ppermute | solution.py:174
  172.3 14.5 %all-to-all-start = ((f32[16,4,1152]{2,1,0:T(4,128)}), f32[16,4,1152]{2,1,0:T(4,128)S(1)}, u32[]{:S(2)}, u32[]{:S(2)}) async-start(f32[16,4,1152]{2,1,0:T(4,128)} %broadcast_in_dim.47), calls=%async_computation | async-start | bytes 589824 | tf_op jit(solution)/shard_map/all_to_all | solution.py:230

commit v5 on v4

v5 whole, which is shorter than its diff:
```python
import math

import jax
import jax.numpy as jnp
from jax import lax
from jax.experimental import pallas as pl
from jax.experimental.pallas import tpu as pltpu
from jax.sharding import Mesh
from jax.sharding import PartitionSpec as P


ROW = "row"
COL = ("col_x", "col_y")
BOTH = (ROW, *COL)
SIDE = 4
BAND = 3
CHAIN_PERIOD = 13
FAR_PERIOD = 6
ARRIVAL = {4: 1, 5: 2, 6: 2, 7: 3, 8: 3, 9: 3, 10: 4, 11: 4, 12: 4, 13: 4, 14: 4, 15: 4}
SENDER = {4: 1, 5: 1, 6: 4, 7: 4, 8: 5, 9: 6, 10: 4, 11: 5, 12: 6, 13: 7, 14: 8, 15: 9}


def solver(i):
    return (i, i - 1 if i else 1)


def union(rounds, period):
    patterns = []
    for first in range(min(period, len(rounds))):
        pairs = sorted({pair for moves in rounds[first::period] for pair in moves})
        assert len({s for s, _ in pairs}) == len(pairs) == len({d for _, d in pairs})
        patterns.append(pairs)
    return [patterns[r % period] for r in range(len(rounds))]


def plan(n):
    chain, odd, even = [], [], []
    for r in range(n - 1):
        chain.append([(solver(r), solver(r + 1))])
        odd.append([])
        even.append([])
        for i in range(n):
            for j in range(i - BAND):
                d = i - j
                if j + ARRIVAL[d] == r:
                    chain[r].append((solver(j) if SENDER[d] == 1 else (j + SENDER[d], j), (i, j)))
                if i - 2 - (d - 4) // 2 == r:
                    (odd if d % 2 else even)[r].append(((i, j), solver(i)))
    return union(chain, CHAIN_PERIOD), union(odd, FAR_PERIOD), union(even, FAR_PERIOD)


def assemble(place, block, parts):
    quarter, width = block.shape

    def body(place_ref, block_ref, *refs):
        out = refs[-1]
        for k in range(SIDE):
            start = k * quarter
            got = refs[k][...] + jnp.where(place_ref[0] == k, block_ref[:, start:], 0.0)
            if start:
                out[start : start + quarter, :start] = jnp.zeros((quarter, start), jnp.bfloat16)
            out[start : start + quarter, start:] = got.astype(jnp.bfloat16)

    vmem = pl.BlockSpec(memory_space=pltpu.VMEM)
    return pl.pallas_call(
        body,
        in_specs=[pl.BlockSpec(memory_space=pltpu.SMEM)] + [vmem] * (1 + SIDE),
        out_specs=vmem,
        out_shape=jax.ShapeDtypeStruct((width, width), jnp.bfloat16),
        compiler_params=pltpu.CompilerParams(vmem_limit_bytes=16 * 2**20),
        name="assemble",
    )(place, block, *parts)


VMEM = pl.BlockSpec(memory_space=pltpu.VMEM)
TO_ROWS = (((1,), (1,)), ((), ()))


def call(body, inputs, shapes, limit=8):
    return pl.pallas_call(
        body,
        in_specs=[VMEM] * len(inputs),
        out_specs=[VMEM] * len(shapes),
        out_shape=[jax.ShapeDtypeStruct(shape, dtype) for shape, dtype in shapes],
        compiler_params=pltpu.CompilerParams(vmem_limit_bytes=limit * 2**20),
    )(*inputs)


def here():
    row = lax.axis_index(ROW)
    col = lax.axis_index(COL[0]) * SIDE + lax.axis_index(COL[1])
    return row, col


def in_turn(now):
    row, col = here()
    if now < 0:
        return (row == 0) & (col == 1)
    return (row == now + 1) & (row - col == 1)


def through(lhs, inverse_ref, block=256):
    width = inverse_ref.shape[1]
    columns = [
        jnp.dot(lhs[:, : n + block], inverse_ref[: n + block, n : n + block], preferred_element_type=jnp.float32)
        for n in range(0, width, block)
    ]
    return jnp.concatenate(columns, axis=1)


def settle(factors, inverse):
    rank_max, width = factors.shape[0] // 2, factors.shape[1]

    def body(factors_ref, inverse_ref, v_out, u_out):
        v_out[...] = factors_ref[:rank_max].astype(jnp.bfloat16)
        u_out[...] = through(factors_ref[rank_max:].astype(jnp.bfloat16), inverse_ref).astype(jnp.bfloat16)

    shape = ((rank_max, width), jnp.bfloat16)
    return call(body, (factors, inverse), (shape, shape))


def prepare(now, odds, evens, pending, source, inverse):
    nrhs, width = source.shape

    def body(odds_ref, evens_ref, pending_ref, source_ref, inverse_ref, pending_out, base_out):
        row, col = here()
        behind = row - 1 - now
        adds = (row - col == 1) & (behind >= 0)
        left = pending_ref[...]
        if now >= 3:
            left = left + jnp.where(adds & (4 + 2 * behind <= row), evens_ref[...], 0.0)
        if now >= 4:
            left = left + jnp.where(adds & (5 + 2 * behind <= row), odds_ref[...], 0.0)
        pending_out[...] = left

        @pl.when(in_turn(now))
        def _():
            total = source_ref[...] - left
            high = total.astype(jnp.bfloat16)
            low = (total - high.astype(jnp.float32)).astype(jnp.bfloat16)
            base_out[...] = through(high, inverse_ref) + through(low, inverse_ref)

    small = ((nrhs, width), jnp.float32)
    return call(body, (odds, evens, pending, source, inverse), (small, small))


def step(now, came, send, own, base, v_tile, u_tile, v_band, u_band):
    held = max(0, min(BAND, now + 1))
    nrhs, width = base.shape

    def body(came_ref, send_ref, own_ref, base_ref, v_ref, u_ref, *refs):
        v_refs, u_refs = refs[:held], refs[held : 2 * held]
        send_out, own_out = refs[2 * held :]
        row, col = here()
        gap = row - col
        turn = in_turn(now)
        hears = row < 0
        for when in sorted(set(ARRIVAL.values())):
            gaps = [d for d in ARRIVAL if ARRIVAL[d] == when]
            hears = hears | ((gap >= min(gaps)) & (gap <= max(gaps)) & (col == now - when))

        def share(known, v, u):
            inner = lax.dot_general(known.astype(jnp.bfloat16), v[...], TO_ROWS, preferred_element_type=jnp.float32)
            return jnp.dot(inner.astype(jnp.bfloat16), u[...], preferred_element_type=jnp.float32)

        @pl.when(jnp.logical_not(turn))
        def _():
            for d in range(1, BAND):
                send_out[d] = jnp.zeros((nrhs, width), jnp.float32)

        @pl.when(jnp.logical_not(turn | hears))
        def _():
            send_out[0] = send_ref[0]
            own_out[...] = own_ref[...]

        @pl.when(hears)
        def _():
            send_out[0] = came_ref[0]
            own_out[...] = share(came_ref[0], v_ref, u_ref)

        @pl.when(turn)
        def _():
            total = base_ref[...]
            for d in range(held):
                total = total - share(came_ref[d], v_refs[d], u_refs[d])
            send_out[0] = total
            for d in range(1, BAND):
                send_out[d] = came_ref[d - 1]
            own_out[...] = own_ref[...]

    inputs = (came, send, own, base, v_tile, u_tile, *v_band[:held], *u_band[:held])
    return call(body, inputs, (((BAND, nrhs, width), jnp.float32), ((nrhs, width), jnp.float32)))


def spread_out(send, log_sum, n_col):
    nrhs, width = send.shape[1:]

    def body(send_ref, log_ref, out):
        for c in range(n_col):
            out[c, :, :width] = send_ref[0]
            out[c, :, width:] = log_ref[...]

    return call(body, (send, log_sum), (((n_col, nrhs, width + 128), jnp.float32),))[0]


def finish(arrived, width):
    n_col, nrhs = arrived.shape[:2]

    def body(arrived_ref, solved_out, loglik_out):
        row, _ = here()
        solved = arrived_ref[jnp.where(row == 0, 1, row - 1), :, :width]
        solved_out[...] = solved
        logs = arrived_ref[0, :, width:]
        for c in range(1, n_col):
            logs = logs + arrived_ref[c, :, width:]
        logdiag = logs[0:1, :nrhs] / width
        ones = jnp.ones((1, width), jnp.float32)
        squares = lax.dot_general(
            ones, solved * solved, TO_ROWS, precision=lax.Precision.HIGHEST, preferred_element_type=jnp.float32
        )
        loglik_out[...] = -0.5 * (squares / width) + logdiag - 0.5 * math.log(2.0 * math.pi)

    return call(body, (arrived,), (((nrhs, width), jnp.float32), ((1, nrhs), jnp.float32)))


def local(right_side, inverse_t, u_factor, v_factor, ranks):
    n = lax.axis_size(ROW)
    n_col = lax.axis_size(COL)
    nrhs, width = right_side.shape[2:]
    piece = width // n_col
    rank_max = u_factor.shape[4]
    col = lax.axis_index(COL)
    source = right_side.reshape(nrhs, width)
    u_tile = u_factor.reshape(rank_max, width)
    v_tile = v_factor.reshape(rank_max, width)
    keep = jnp.arange(rank_max, dtype=jnp.int32)[:, None] < ranks.reshape(1, 1)
    u_tile = jnp.where(keep, u_tile, jnp.zeros_like(u_tile))

    def move(array, pairs):
        numbered = [(s[0] * n_col + s[1], d[0] * n_col + d[1]) for s, d in pairs]
        return lax.ppermute(array, BOTH, numbered)

    rows = inverse_t.reshape(piece, width).astype(jnp.float32)
    quarter = width // SIDE
    slabs = []
    for k in range(SIDE):
        pairs = [
            ((r, x * SIDE + k), (r, x * SIDE + solver(r)[1] % SIDE))
            for r in range(n)
            for x in range(SIDE)
            if solver(r)[1] % SIDE != k
        ]
        slabs.append(move(rows, pairs) + jnp.where(col % SIDE == k, rows, 0.0))
    block = jnp.concatenate(slabs, axis=0)
    square = lax.dynamic_slice_in_dim(rows, col * piece, piece, 1)
    log_sum = jnp.broadcast_to(jnp.sum(jnp.log(jnp.diagonal(square))), (nrhs, 128))
    both = jnp.concatenate([v_tile, u_tile], axis=0).astype(jnp.float32)
    block, both, log_sum = lax.optimization_barrier((block, both, log_sum))
    parts = []
    for k in range(SIDE):
        pairs = [
            ((r, k * SIDE + solver(r)[1] % SIDE), solver(r)) for r in range(n) if solver(r)[1] // SIDE != k
        ]
        parts.append(move(block[:, k * quarter :], pairs))
    place = jnp.stack([col // SIDE]).astype(jnp.int32)

    moved = [both]
    for d in range(2, BAND + 1):
        moved.append(move(both, [((i, i - d), solver(i)) for i in range(d, n)]))
    inverse = assemble(place, block, parts)

    chain, odd, even = plan(n)
    nothing = jnp.zeros((nrhs, width), jnp.float32)
    came = jnp.zeros((BAND, nrhs, width), jnp.float32)
    v_band, u_band = [], []
    pending, base = prepare(-1, nothing, nothing, nothing, source, inverse)
    send, own = step(-1, came, came, nothing, base, v_tile, u_tile, v_band, u_band)
    odds = evens = nothing
    for r in range(n - 1):
        came = move(send, chain[r])
        more_odds = more_evens = nothing
        if 3 <= r < n - 2:
            more_odds = move(own, odd[r])
        if 2 <= r < n - 2:
            more_evens = move(own, even[r])
        if r < BAND:
            v_held, u_held = settle(moved[r], inverse)
            v_band.append(v_held)
            u_band.append(u_held)
        pending, base = prepare(r, odds, evens, pending, source, inverse)
        send, own = step(r, came, send, own, base, v_tile, u_tile, v_band, u_band)
        odds, evens = more_odds, more_evens

    payload = spread_out(send, log_sum, n_col)
    arrived = lax.all_to_all(payload, COL, 0, 0, tiled=True)
    solved, loglik = finish(arrived, width)
    return solved.reshape(1, 1, nrhs, width), loglik.reshape(1, 1, nrhs)


def solution(mesh):
    plane = Mesh(mesh.devices.reshape(-1, SIDE, SIDE), BOTH)
    return jax.shard_map(
        local,
        mesh=plane,
        in_specs=(
            P(None, ROW, None, None),
            P(None, ROW, COL, None),
            P(None, ROW, None, COL, None, None),
            P(None, ROW, None, COL, None, None),
            P(None, ROW, None, COL),
        ),
        out_specs=(P(None, ROW, None, None), P(None, ROW, None)),
        check_vma=False,
    )
```

time: 190 us -> 191 us (level)
  blocking collectives: 0 us -> 14.3 us
  waiting for transfers between devices: 44 us -> 34.5 us
  other arithmetic: 9.1 us -> 3.91 us
  Pallas kernels: 3.25 us -> 7.64 us
  starting transfers between devices: 126 us -> 122 us
    all_to_all x0 -> x1, blocking collectives: none -> 14.3 us  [local(): arrived = lax.all_to_all(payload, COL, 0, 0, tiled=True)]
    all_to_all x1 -> x0, waiting for transfers between devices: 8.66 us -> none  [local(): arrived = lax.all_to_all(payload, COL, 0, 0, tiled=True)]
    all_to_all x1 -> x0, starting transfers between devices: 5.79 us -> none  [local(): arrived = lax.all_to_all(payload, COL, 0, 0, tiled=True)]
    pallas_call x16 -> x37, Pallas kernels: 1.84 us -> 5.73 us  [call(): pl.pallas_call(body, in_specs=[VMEM] * len(inputs), out_specs=[VMEM] * le...]
    unnamed x6 -> x10, local copies, waits for them, and re-layouts: 0.02 us -> 2.53 us
    convert_element_type x1 -> x0, other arithmetic: 2.24 us -> none  [local(): tile = (tile + jnp.where(gap == 1, 0.0, both)).astype(jnp.bfloat16)]
  transfers between devices with their start and end apart: 49 -> 48, of which waited for: 4 -> 3; matrix products, arithmetic and copies ran while one was open for 5% -> 3% of each run, Pallas kernels for 1% -> 3%
where the time goes in v5:
time: 191 us; the launch traced here: 190 us
  starting transfers between devices  122 us (64%)
  waiting for transfers between devices  34.5 us (18%)
  blocking collectives  14.3 us (7%)
  Pallas kernels  7.64 us (4%)
  local copies, waits for them, and re-layouts  5.89 us (3%)
  other arithmetic  3.91 us (2%)
  between operations  2.35 us (1%)
    ppermute x48, starting transfers between devices, move(): return lax.ppermute(array, BOTH, numbered)  122 us
    ppermute x48, waiting for transfers between devices, move(): return lax.ppermute(array, BOTH, numbered)  34.5 us
    all_to_all x1, blocking collectives, local(): arrived = lax.all_to_all(payload, COL, 0, 0, tiled=True)  14.3 us
    pallas_call x37, Pallas kernels, call(): pl.pallas_call(body, in_specs=[VMEM] * len(inputs), out_specs=[VMEM] * le...  5.73 us
  transfers between devices with their start and end apart: 48, of which 3 were waited for; matrix products, arithmetic and copies ran while one was open for 3% of the time, Pallas kernels for 3%

profile of v5, /device:TPU:224, one launch (start us, length us, event | category | flops | bytes accessed | tf_op | source)
XLA Modules:
  0.0 190.2 jit_solution(13380521417373365767)
XLA Ops:
  0.6 1.0 fusion
  1.6 3.5 %collective-permute-start = (f32[64,1024]{1,0:T(8,128)S(1)}, f32[64,1024]{1,0:T(8,128)S(1)}, u32[]{:S(2)}, u32[]{:S(2)}) collective-permute-start(f32[64,1024]{1,0:T(8,128)S(1)} %get-tuple-element.149), channel_id=1, source_target_pairs={{0,1},{4,5},{8,9},{12,13},{32,33},{36,37},{40,41},{44,45},{48,50},... | collective-permute-start | bytes 786440 | tf_op jit(solution)/shard_map/ppermute | solution.py:241
  5.2 0.7 collective-permute-start.1
  5.8 0.7 collective-permute-start.2
  6.5 0.7 collective-permute-start.3
  7.9 1.0 bitcast_select_fusion.u_ref
  9.0 0.8 gather_fusion
  10.5 1.1 maximum_convert_fusion.factors_ref
  12.4 1.7 collective-permute-start.4
  14.1 1.6 collective-permute-start.10
  15.7 0.7 collective-permute-start.12
  16.5 0.7 collective-permute-start.7
  17.2 0.9 slice.9
  18.1 1.5 collective-permute-start.5
  19.6 0.8 slice.10
  20.5 0.7 copy-done.2
  21.2 1.5 collective-permute-start.6
  22.7 0.9 copy-done.3
  23.6 1.9 %assemble.1.inverse_ref = bf16[1024,1024]{1,0:T(8,128)(2,1)S(1)} custom-call(s32[1]{0:T(128)} %bitcast.1.place_ref, f32[256,1024]{1,0:T(8,128)S(1)} %pad_maximum_fusion.block_ref, f32[256,1024]{1,0:T(8,128)} %collective-permute-done.4.refs_0_, f32[256,768]{1,0:T(8,128)} %collective-permute-done.5.refs_1_, f32[256,512]{1,0:T(8,128)} %collective-permute-done.6.refs_2_, ...), custom_call_target="tpu_custom_call" | custom-call | tf_op jit(solution)/shard_map/assemble/pallas_call | solution.py:65
  25.6 0.9 copy-done
  26.5 0.7 collective-permute-start.8
  27.6 0.7 collective-permute-start.9
  28.3 1.6 shard_map.74
  30.0 0.7 collective-permute-start.11
  31.2 0.7 collective-permute-start.13
  31.8 0.7 collective-permute-start.14
  32.6 1.3 collective-permute-start.15
  33.9 0.7 collective-permute-start.16
  34.6 0.7 collective-permute-start.17
  35.3 31.5 %collective-permute-done.15.came_ref = f32[3,4,1024]{2,1,0:T(4,128)S(1)} collective-permute-done((f32[3,4,1024]{2,1,0:T(4,128)S(1)}, f32[3,4,1024]{2,1,0:T(4,128)S(1)}, u32[]{:S(2)}, u32[]{:S(2)}) %collective-permute-start.15) | collective-permute-done | bytes 49184 | tf_op jit(solution)/shard_map/ppermute | solution.py:241
  67.2 0.7 collective-permute-start.18
  67.9 0.7 collective-permute-start.19
  68.5 0.7 collective-permute-start.20
  69.3 0.7 collective-permute-start.21
  70.0 0.7 collective-permute-start.22
  70.7 0.7 collective-permute-start.23
  71.5 0.7 collective-permute-start.24
  72.1 0.7 collective-permute-start.25
  72.8 0.7 collective-permute-start.26
  73.6 0.7 collective-permute-start.27
  74.3 0.7 collective-permute-start.28
  74.9 37.0 %collective-permute-start.29 = (f32[4,1024]{1,0:T(4,128)S(1)}, f32[4,1024]{1,0:T(4,128)S(1)}, u32[]{:S(2)}, u32[]{:S(2)}) collective-permute-start(f32[4,1024]{1,0:T(4,128)S(1)} %get-tuple-element.113.own_ref), channel_id=1, source_target_pairs={{149,152},{164,169},{179,186},{194,203},{209,220},{224,237},{251,2... | collective-permute-start | bytes 49160 | tf_op jit(solution)/shard_map/ppermute | solution.py:241
  112.0 1.4 collective-permute-done.29.evens_ref
  113.5 0.7 collective-permute-start.30
  114.1 0.7 collective-permute-start.31
  114.8 0.7 collective-permute-start.32
  115.8 0.7 collective-permute-start.33
  116.4 0.7 collective-permute-start.34
  117.1 0.7 collective-permute-start.35
  117.9 0.7 collective-permute-start.36
  118.6 0.7 collective-permute-start.37
  119.2 0.7 collective-permute-start.38
  120.0 0.7 collective-permute-start.39
  120.7 0.7 collective-permute-start.40
  121.4 0.7 collective-permute-start.41
  122.1 0.7 collective-permute-start.42
  122.8 0.7 collective-permute-start.43
  123.5 0.7 collective-permute-start.44
  124.3 0.7 collective-permute-start.45
  124.9 0.7 collective-permute-start.46
  125.6 47.0 %collective-permute-start.47 = (f32[4,1024]{1,0:T(4,128)S(1)}, f32[4,1024]{1,0:T(4,128)S(1)}, u32[]{:S(2)}, u32[]{:S(2)}) collective-permute-start(f32[4,1024]{1,0:T(4,128)S(1)} %get-tuple-element.137.own_ref), channel_id=1, source_target_pairs={{149,152},{164,169},{179,186},{194,203},{209,220},{224,237},{251,2... | collective-permute-start | bytes 49160 | tf_op jit(solution)/shard_map/ppermute | solution.py:241
  172.6 1.4 collective-permute-done.47.evens_ref
  175.3 14.3 %all_to_all.5.arrived_ref = f32[16,4,1152]{2,1,0:T(4,128)S(1)} all-to-all(f32[16,4,1152]{2,1,0:T(4,128)S(1)} %shard_map.103), channel_id=1, replica_groups=mesh['row'=16,'col_x'=4,'col_y'=4] {'col_x','col_y'}, dimensions={0} | all-to-all | bytes 589824 | tf_op jit(solution)/shard_map/all_to_all | solution.py:295
  189.5 0.7 shard_map.104
  (97 shorter events, 5.2 us)
Async XLA Ops:
  0.6 10.9 %copy-start.4 = (bf16[1,1,64,1024]{3,2,1,0:T(8,128)(2,1)S(1)}, bf16[1,1,64,1024]{3,2,1,0:T(8,128)(2,1)}, u32[]{:S(2)}) copy-start(bf16[1,1,64,1024]{3,2,1,0:T(8,128)(2,1)} %param.6) | copy-start | bytes 393220
  1.6 9.9 %collective-permute-start = (f32[64,1024]{1,0:T(8,128)S(1)}, f32[64,1024]{1,0:T(8,128)S(1)}, u32[]{:S(2)}, u32[]{:S(2)}) collective-permute-start(f32[64,1024]{1,0:T(8,128)S(1)} %get-tuple-element.149), channel_id=1, source_target_pairs={{0,1},{4,5},{8,9},{12,13},{32,33},{36,37},{40,41},{44,45},{48,50},... | collective-permute-start | bytes 786440 | tf_op jit(solution)/shard_map/ppermute | solution.py:241
  5.2 6.4 %collective-permute-start.1 = (f32[64,1024]{1,0:T(8,128)S(1)}, f32[64,1024]{1,0:T(8,128)S(1)}, u32[]{:S(2)}, u32[]{:S(2)}) collective-permute-start(f32[64,1024]{1,0:T(8,128)S(1)} %get-tuple-element.149), channel_id=1, source_target_pairs={{17,16},{21,20},{25,24},{29,28},{49,50},{53,54},{57,58},{61,62},{6... | collective-permute-start | bytes 786440 | tf_op jit(solution)/shard_map/ppermute | solution.py:241
  5.8 5.7 %collective-permute-start.2 = (f32[64,1024]{1,0:T(8,128)S(1)}, f32[64,1024]{1,0:T(8,128)S(1)}, u32[]{:S(2)}, u32[]{:S(2)}) collective-permute-start(f32[64,1024]{1,0:T(8,128)S(1)} %get-tuple-element.149), channel_id=1, source_target_pairs={{2,1},{6,5},{10,9},{14,13},{18,16},{22,20},{26,24},{30,28},{34,33}... | collective-permute-start | bytes 786440 | tf_op jit(solution)/shard_map/ppermute | solution.py:241
  6.5 5.0 %collective-permute-start.3 = (f32[64,1024]{1,0:T(8,128)S(1)}, f32[64,1024]{1,0:T(8,128)S(1)}, u32[]{:S(2)}, u32[]{:S(2)}) collective-permute-start(f32[64,1024]{1,0:T(8,128)S(1)} %get-tuple-element.149), channel_id=1, source_target_pairs={{3,1},{7,5},{11,9},{15,13},{19,16},{23,20},{27,24},{31,28},{35,33}... | collective-permute-start | bytes 786440 | tf_op jit(solution)/shard_map/ppermute | solution.py:241
  12.4 10.2 %collective-permute-start.4 = (f32[256,1024]{1,0:T(8,128)S(1)}, f32[256,1024]{1,0:T(8,128)}, u32[]{:S(2)}, u32[]{:S(2)}) collective-permute-start(f32[256,1024]{1,0:T(8,128)S(1)} %pad_maximum_fusion.block_ref), channel_id=1, source_target_pairs={{80,84},{97,101},{114,118},{131,135},{144,152},{161,169},{178,186}... | collective-permute-start | bytes 3145736 | tf_op jit(solution)/shard_map/ppermute | solution.py:241
  14.1 14.2 %collective-permute-start.10 = (f32[256,1024]{1,0:T(8,128)S(1)}, f32[256,1024]{1,0:T(8,128)}, u32[]{:S(2)}, u32[]{:S(2)}) collective-permute-start(f32[256,1024]{1,0:T(8,128)S(1)} %maximum_convert_fusion.factors_ref), channel_id=1, source_target_pairs={{32,33},{49,50},{66,67},{83,84},{100,101},{117,118},{134,135},{151... | collective-permute-start | bytes 3145736 | tf_op jit(solution)/shard_map/ppermute | solution.py:241
  15.7 15.0 %collective-permute-start.12 = (f32[256,1024]{1,0:T(8,128)S(1)}, f32[256,1024]{1,0:T(8,128)S(1)}, u32[]{:S(2)}, u32[]{:S(2)}) collective-permute-start(f32[256,1024]{1,0:T(8,128)S(1)} %maximum_convert_fusion.factors_ref), channel_id=1, source_target_pairs={{48,50},{65,67},{82,84},{99,101},{116,118},{133,135},{150,152},{16... | collective-permute-start | bytes 3145736 | tf_op jit(solution)/shard_map/ppermute | solution.py:241
  16.5 4.0 %collective-permute-start.7 = (f32[256,256]{1,0:T(8,128)S(1)}, f32[256,256]{1,0:T(8,128)S(1)}, u32[]{:S(2)}, u32[]{:S(2)}) collective-permute-start(f32[256,256]{1,0:T(8,128)S(1)} %slice.11), channel_id=1, source_target_pairs={{13,1},{28,16},{45,33},{62,50},{79,67},{92,84},{109,101},{126,118}... | collective-permute-start | bytes 786440 | tf_op jit(solution)/shard_map/ppermute | solution.py:241
  18.1 4.6 %collective-permute-start.5 = (f32[256,768]{1,0:T(8,128)}, f32[256,768]{1,0:T(8,128)}, u32[]{:S(2)}, u32[]{:S(2)}) collective-permute-start(f32[256,768]{1,0:T(8,128)} %slice.9), channel_id=1, source_target_pairs={{5,1},{20,16},{37,33},{54,50},{71,67},{148,152},{165,169},{182,186... | collective-permute-start | bytes 2359304 | tf_op jit(solution)/shard_map/ppermute | solution.py:241
  20.5 0.7 copy-start.2
  21.2 1.5 collective-permute-start.6
  22.7 1.0 copy-start.3
  23.6 1.9 %copy-start.1 = (f32[1,1,4,1024]{3,2,1,0:T(4,128)S(1)}, f32[1,1,4,1024]{3,2,1,0:T(4,128)}, u32[]{:S(2)}) copy-start(f32[1,1,4,1024]{3,2,1,0:T(4,128)} %param.5) | copy-start | bytes 49156
  25.6 1.0 copy-start
  26.5 1.1 collective-permute-start.8
  27.6 2.3 %collective-permute-start.9 = (f32[3,4,1024]{2,1,0:T(4,128)S(1)}, f32[3,4,1024]{2,1,0:T(4,128)S(1)}, u32[]{:S(2)}, u32[]{:S(2)}) collective-permute-start(f32[3,4,1024]{2,1,0:T(4,128)S(1)} %get-tuple-element.84.send_ref), channel_id=1, source_target_pairs={{1,64},{16,33},{237,254}} | collective-permute-start | bytes 147464 | tf_op jit(solution)/shard_map/ppermute | solution.py:241
  30.0 1.1 collective-permute-start.11
  31.2 1.4 collective-permute-start.13
  31.8 0.7 collective-permute-start.14
  32.6 34.2 %collective-permute-start.15 = (f32[3,4,1024]{2,1,0:T(4,128)S(1)}, f32[3,4,1024]{2,1,0:T(4,128)S(1)}, u32[]{:S(2)}, u32[]{:S(2)}) collective-permute-start(f32[3,4,1024]{2,1,0:T(4,128)S(1)} %get-tuple-element.100.send_ref), channel_id=1, source_target_pairs={{33,114},{50,115},{64,160},{67,84},{80,176},{81,129},{96,192},{97,... | collective-permute-start | bytes 147464 | tf_op jit(solution)/shard_map/ppermute | solution.py:241
  33.9 1.3 collective-permute-start.16
  34.6 0.7 collective-permute-start.17
  67.2 2.1 %collective-permute-start.18 = (f32[3,4,1024]{2,1,0:T(4,128)S(1)}, f32[3,4,1024]{2,1,0:T(4,128)S(1)}, u32[]{:S(2)}, u32[]{:S(2)}) collective-permute-start(f32[3,4,1024]{2,1,0:T(4,128)S(1)} %get-tuple-element.104.send_ref), channel_id=1, source_target_pairs={{50,131},{67,132},{81,177},{84,101},{97,193},{98,146},{113,209},{1... | collective-permute-start | bytes 147464 | tf_op jit(solution)/shard_map/ppermute | solution.py:241
  67.9 1.3 collective-permute-start.19
  68.5 0.7 collective-permute-start.20
  69.3 2.1 %collective-permute-start.21 = (f32[3,4,1024]{2,1,0:T(4,128)S(1)}, f32[3,4,1024]{2,1,0:T(4,128)S(1)}, u32[]{:S(2)}, u32[]{:S(2)}) collective-permute-start(f32[3,4,1024]{2,1,0:T(4,128)S(1)} %get-tuple-element.108.send_ref), channel_id=1, source_target_pairs={{67,148},{84,149},{98,194},{101,118},{114,210},{115,163},{130,226}... | collective-permute-start | bytes 147464 | tf_op jit(solution)/shard_map/ppermute | solution.py:241
  70.0 1.3 collective-permute-start.22
  70.7 0.7 collective-permute-start.23
  71.5 2.1 %collective-permute-start.24 = (f32[3,4,1024]{2,1,0:T(4,128)S(1)}, f32[3,4,1024]{2,1,0:T(4,128)S(1)}, u32[]{:S(2)}, u32[]{:S(2)}) collective-permute-start(f32[3,4,1024]{2,1,0:T(4,128)S(1)} %get-tuple-element.112.send_ref), channel_id=1, source_target_pairs={{84,165},{101,166},{115,211},{118,135},{131,227},{132,180},{147,24... | collective-permute-start | bytes 147464 | tf_op jit(solution)/shard_map/ppermute | solution.py:241
  72.1 1.3 collective-permute-start.25
  72.8 0.7 collective-permute-start.26
  73.6 39.8 %collective-permute-start.27 = (f32[3,4,1024]{2,1,0:T(4,128)S(1)}, f32[3,4,1024]{2,1,0:T(4,128)S(1)}, u32[]{:S(2)}, u32[]{:S(2)}) collective-permute-start(f32[3,4,1024]{2,1,0:T(4,128)S(1)} %get-tuple-element.116.send_ref), channel_id=1, source_target_pairs={{101,182},{118,183},{132,228},{135,152},{148,244},{149,197},{165,2... | collective-permute-start | bytes 147464 | tf_op jit(solution)/shard_map/ppermute | solution.py:241
  74.3 37.7 %collective-permute-start.28 = (f32[4,1024]{1,0:T(4,128)S(1)}, f32[4,1024]{1,0:T(4,128)S(1)}, u32[]{:S(2)}, u32[]{:S(2)}) collective-permute-start(f32[4,1024]{1,0:T(4,128)S(1)} %get-tuple-element.113.own_ref), channel_id=1, source_target_pairs={{148,152},{163,169},{178,186},{193,203},{208,220},{250,254}} | collective-permute-start | bytes 49160 | tf_op jit(solution)/shard_map/ppermute | solution.py:241
  74.9 38.5 %collective-permute-start.29 = (f32[4,1024]{1,0:T(4,128)S(1)}, f32[4,1024]{1,0:T(4,128)S(1)}, u32[]{:S(2)}, u32[]{:S(2)}) collective-permute-start(f32[4,1024]{1,0:T(4,128)S(1)} %get-tuple-element.113.own_ref), channel_id=1, source_target_pairs={{149,152},{164,169},{179,186},{194,203},{209,220},{224,237},{251,2... | collective-permute-start | bytes 49160 | tf_op jit(solution)/shard_map/ppermute | solution.py:241
  113.5 2.3 %collective-permute-start.30 = (f32[3,4,1024]{2,1,0:T(4,128)S(1)}, f32[3,4,1024]{2,1,0:T(4,128)S(1)}, u32[]{:S(2)}, u32[]{:S(2)}) collective-permute-start(f32[3,4,1024]{2,1,0:T(4,128)S(1)} %get-tuple-element.120.send_ref), channel_id=1, source_target_pairs={{118,199},{135,200},{149,245},{152,169},{166,214},{182,230},{183,2... | collective-permute-start | bytes 147464 | tf_op jit(solution)/shard_map/ppermute | solution.py:241
  114.1 1.3 collective-permute-start.31
  114.8 0.7 collective-permute-start.32
  115.8 2.1 %collective-permute-start.33 = (f32[3,4,1024]{2,1,0:T(4,128)S(1)}, f32[3,4,1024]{2,1,0:T(4,128)S(1)}, u32[]{:S(2)}, u32[]{:S(2)}) collective-permute-start(f32[3,4,1024]{2,1,0:T(4,128)S(1)} %get-tuple-element.124.send_ref), channel_id=1, source_target_pairs={{135,216},{152,217},{169,186},{183,231},{199,247},{200,232}} | collective-permute-start | bytes 147464 | tf_op jit(solution)/shard_map/ppermute | solution.py:241
  116.4 1.3 collective-permute-start.34
  117.1 0.7 collective-permute-start.35
  117.9 2.1 %collective-permute-start.36 = (f32[3,4,1024]{2,1,0:T(4,128)S(1)}, f32[3,4,1024]{2,1,0:T(4,128)S(1)}, u32[]{:S(2)}, u32[]{:S(2)}) collective-permute-start(f32[3,4,1024]{2,1,0:T(4,128)S(1)} %get-tuple-element.128.send_ref), channel_id=1, source_target_pairs={{152,233},{169,234},{186,203},{200,248},{217,249}} | collective-permute-start | bytes 147464 | tf_op jit(solution)/shard_map/ppermute | solution.py:241
  118.6 1.3 collective-permute-start.37
  119.2 0.7 collective-permute-start.38
  120.0 2.1 %collective-permute-start.39 = (f32[3,4,1024]{2,1,0:T(4,128)S(1)}, f32[3,4,1024]{2,1,0:T(4,128)S(1)}, u32[]{:S(2)}, u32[]{:S(2)}) collective-permute-start(f32[3,4,1024]{2,1,0:T(4,128)S(1)} %get-tuple-element.132.send_ref), channel_id=1, source_target_pairs={{169,250},{186,251},{203,220}} | collective-permute-start | bytes 147464 | tf_op jit(solution)/shard_map/ppermute | solution.py:241
  120.7 1.3 collective-permute-start.40
  121.4 0.7 collective-permute-start.41
  122.1 2.1 %collective-permute-start.42 = (f32[3,4,1024]{2,1,0:T(4,128)S(1)}, f32[3,4,1024]{2,1,0:T(4,128)S(1)}, u32[]{:S(2)}, u32[]{:S(2)}) collective-permute-start(f32[3,4,1024]{2,1,0:T(4,128)S(1)} %get-tuple-element.136.send_ref), channel_id=1, source_target_pairs={{1,16},{220,237}} | collective-permute-start | bytes 147464 | tf_op jit(solution)/shard_map/ppermute | solution.py:241
  122.8 1.3 collective-permute-start.43
  123.5 0.7 collective-permute-start.44
  124.3 50.4 %collective-permute-start.45 = (f32[3,4,1024]{2,1,0:T(4,128)S(1)}, f32[3,4,1024]{2,1,0:T(4,128)S(1)}, u32[]{:S(2)}, u32[]{:S(2)}) collective-permute-start(f32[3,4,1024]{2,1,0:T(4,128)S(1)} %get-tuple-element.140.send_ref), channel_id=1, source_target_pairs={{1,64},{16,33},{237,254}} | collective-permute-start | bytes 147464 | tf_op jit(solution)/shard_map/ppermute | solution.py:241
  124.9 47.6 %collective-permute-start.46 = (f32[4,1024]{1,0:T(4,128)S(1)}, f32[4,1024]{1,0:T(4,128)S(1)}, u32[]{:S(2)}, u32[]{:S(2)}) collective-permute-start(f32[4,1024]{1,0:T(4,128)S(1)} %get-tuple-element.137.own_ref), channel_id=1, source_target_pairs={{148,152},{163,169},{178,186},{193,203},{208,220},{250,254}} | collective-permute-start | bytes 49160 | tf_op jit(solution)/shard_map/ppermute | solution.py:241
  125.6 48.4 %collective-permute-start.47 = (f32[4,1024]{1,0:T(4,128)S(1)}, f32[4,1024]{1,0:T(4,128)S(1)}, u32[]{:S(2)}, u32[]{:S(2)}) collective-permute-start(f32[4,1024]{1,0:T(4,128)S(1)} %get-tuple-element.137.own_ref), channel_id=1, source_target_pairs={{149,152},{164,169},{179,186},{194,203},{209,220},{224,237},{251,2... | collective-permute-start | bytes 49160 | tf_op jit(solution)/shard_map/ppermute | solution.py:241
